TPU v7x, 16 devices: a whole 2x2x2 slice. The times are simulated.
16 devices in a mesh: data: 16 (over z, y, x, core).
Axes of the slice: x: 2, y: 2, z: 2, core: 2. Of those that a mesh axis runs over, the one named last changes fastest.
Arguments:
- tokens: bfloat16 [8192, 768], P('data')
- d_logits: bfloat16 [8192, 32000], P('data')
- w_up: bfloat16 [2, 768, 2048], replicated
- w_down: bfloat16 [2, 2048, 768], replicated
- w_out: bfloat16 [768, 32000], replicated
- proj_up: bfloat16 [2, 768, 256], replicated
- proj_down: bfloat16 [2, 768, 256], replicated
- mom_up: float32 [2, 256, 2048], P(None, None, 'data')
- var_up: float32 [2, 256, 2048], P(None, None, 'data')
- mom_down: float32 [2, 2048, 256], P(None, 'data')
- var_down: float32 [2, 2048, 256], P(None, 'data')
- mom_out: float32 [768, 32000], P(None, 'data')
- var_out: float32 [768, 32000], P(None, 'data')
Outputs:
- output 1: bfloat16 [2, 768, 2048], replicated
- output 2: bfloat16 [2, 2048, 768], replicated
- output 3: bfloat16 [768, 32000], replicated
- output 4: float32 [2, 256, 2048], P(None, None, 'data')
- output 5: float32 [2, 256, 2048], P(None, None, 'data')
- output 6: float32 [2, 2048, 256], P(None, 'data')
- output 7: float32 [2, 2048, 256], P(None, 'data')
- output 8: float32 [768, 32000], P(None, 'data')
- output 9: float32 [768, 32000], P(None, 'data')
All inputs are finite; a program needn't handle non-finite values.
Results may differ from a plain program's by a relative error of at most 0.00427494.
Values are sent between devices in bfloat16 or wider.
A program may use at most 1 GiB of HBM per device.

v0:
```python
import jax
import jax.numpy as jnp
from jax import lax
from jax.sharding import PartitionSpec as P

BETA1 = 0.9
BETA2 = 0.999
EPS = 1e-8
STEP = 4
LR = 0.02
ALPHA = 0.5
LR_HEAD = 0.01
DATA_AXIS = 'data'


def gelu_tanh(values):
    return jax.nn.gelu(values, approximate=True)


def adam_update(gradient, moment_one, moment_two):
    moment_one = BETA1 * moment_one + (1.0 - BETA1) * gradient
    moment_two = BETA2 * moment_two + (1.0 - BETA2) * gradient * gradient
    direction = (moment_one / (1.0 - BETA1 ** STEP)) / (jnp.sqrt(moment_two / (1.0 - BETA2 ** STEP)) + EPS)
    return moment_one, moment_two, direction


def forward_backward(tokens, d_logits, w_up, w_down, w_out):
    num_layers = w_up.shape[0]
    hidden = tokens
    saved_acts = []
    for layer_idx in range(num_layers):
        pre_act = jnp.dot(hidden, w_up[layer_idx], preferred_element_type=jnp.float32).astype(jnp.bfloat16)
        post_act = gelu_tanh(pre_act.astype(jnp.float32)).astype(jnp.bfloat16)
        saved_acts.append((hidden, pre_act, post_act))
        hidden = (hidden.astype(jnp.float32) + jnp.dot(post_act, w_down[layer_idx], preferred_element_type=jnp.float32)).astype(jnp.bfloat16)
    grad_head = jnp.einsum('td,tv->dv', hidden, d_logits, preferred_element_type=jnp.float32)
    grad_hidden = jnp.einsum('tv,dv->td', d_logits, w_out, preferred_element_type=jnp.float32).astype(jnp.bfloat16)
    grads_up = [None] * num_layers
    grads_down = [None] * num_layers
    for layer_idx in reversed(range(num_layers)):
        hidden_in, pre_act, post_act = saved_acts[layer_idx]
        grads_down[layer_idx] = jnp.einsum('tf,td->fd', post_act, grad_hidden, preferred_element_type=jnp.float32)
        d_post = jnp.einsum('td,fd->tf', grad_hidden, w_down[layer_idx], preferred_element_type=jnp.float32)
        gelu_pull = jax.vjp(gelu_tanh, pre_act.astype(jnp.float32))[1]
        d_pre = gelu_pull(d_post)[0].astype(jnp.bfloat16)
        grads_up[layer_idx] = jnp.einsum('td,tf->df', hidden_in, d_pre, preferred_element_type=jnp.float32)
        if layer_idx > 0:
            grad_hidden = (grad_hidden.astype(jnp.float32) + jnp.einsum('tf,df->td', d_pre, w_up[layer_idx], preferred_element_type=jnp.float32)).astype(jnp.bfloat16)
    return grad_head, grads_up, grads_down


def local_step(tokens, d_logits, w_up, w_down, w_out, proj_up, proj_down, mom_up, var_up, mom_down, var_down, mom_out, var_out):
    grad_head, grads_up, grads_down = forward_backward(tokens, d_logits, w_up, w_down, w_out)
    up_weights = []
    down_weights = []
    up_first = []
    up_second = []
    down_first = []
    down_second = []
    for layer_idx in range(len(grads_up)):
        low_up = jnp.einsum('dr,df->rf', proj_up[layer_idx].astype(jnp.float32), grads_up[layer_idx], preferred_element_type=jnp.float32)
        low_down = jnp.einsum('fd,dr->fr', grads_down[layer_idx], proj_down[layer_idx].astype(jnp.float32), preferred_element_type=jnp.float32)
        low_up = lax.psum_scatter(low_up, DATA_AXIS, scatter_dimension=1, tiled=True)
        low_down = lax.psum_scatter(low_down, DATA_AXIS, scatter_dimension=0, tiled=True)
        m_up, v_up, dir_up = adam_update(low_up, mom_up[layer_idx], var_up[layer_idx])
        m_down, v_down, dir_down = adam_update(low_down, mom_down[layer_idx], var_down[layer_idx])
        dir_up = lax.all_gather(dir_up.astype(jnp.bfloat16), DATA_AXIS, axis=1, tiled=True)
        dir_down = lax.all_gather(dir_down.astype(jnp.bfloat16), DATA_AXIS, axis=0, tiled=True)
        step_up = jnp.dot(proj_up[layer_idx], dir_up, preferred_element_type=jnp.float32)
        step_down = jnp.einsum('fr,dr->fd', dir_down, proj_down[layer_idx], preferred_element_type=jnp.float32)
        up_weights.append((w_up[layer_idx].astype(jnp.float32) - LR * ALPHA * step_up).astype(jnp.bfloat16))
        down_weights.append((w_down[layer_idx].astype(jnp.float32) - LR * ALPHA * step_down).astype(jnp.bfloat16))
        up_first.append(m_up)
        up_second.append(v_up)
        down_first.append(m_down)
        down_second.append(v_down)
    head_part = lax.psum_scatter(grad_head, DATA_AXIS, scatter_dimension=1, tiled=True)
    m_out, v_out, dir_out = adam_update(head_part, mom_out, var_out)
    shard_cols = mom_out.shape[1]
    w_out_part = lax.dynamic_slice_in_dim(w_out, lax.axis_index(DATA_AXIS) * shard_cols, shard_cols, axis=1)
    w_out_part = (w_out_part.astype(jnp.float32) - LR_HEAD * dir_out).astype(jnp.bfloat16)
    w_out_new = lax.all_gather(w_out_part, DATA_AXIS, axis=1, tiled=True)
    return (jnp.stack(up_weights), jnp.stack(down_weights), w_out_new,
            jnp.stack(up_first), jnp.stack(up_second), jnp.stack(down_first), jnp.stack(down_second),
            m_out, v_out)


def solution(mesh):
    row_spec = P(DATA_AXIS, None)
    whole = P()
    up_spec = P(None, None, DATA_AXIS)
    down_spec = P(None, DATA_AXIS, None)
    head_spec = P(None, DATA_AXIS)
    in_specs = (row_spec, row_spec, whole, whole, whole, whole, whole, up_spec, up_spec, down_spec, down_spec, head_spec, head_spec)
    out_specs = (whole, whole, whole, up_spec, up_spec, down_spec, down_spec, head_spec, head_spec)
    return jax.shard_map(local_step, mesh=mesh, in_specs=in_specs, out_specs=out_specs, check_vma=False)
```

profile of v0, /device:TPU:0, one launch (start us, length us, event | category | flops | bytes accessed | tf_op | source)
XLA Modules:
  0.0 1146.4 jit_solution(458249518231635002)
XLA Ops:
  7.2 4.1 fusion.37
  11.4 5.4 add_convert_fusion.2
  16.8 3.1 fusion.40
  19.9 33.1 %convolution_convert_fusion = bf16[512,768]{1,0:T(8,128)(2,1)S(1)} fusion(bf16[512,32000]{1,0:T(8,128)(2,1)} %param.14, bf16[768,32000]{1,0:T(8,128)(2,1)} %param.17), kind=kOutput, calls=%fused_computation.77 | convolution fusion | flops 25166217216 | bytes 82706432 | tf_op jit(solution)/shard_map/tv,dv->td/dot_general | solution.py:37
  53.0 6.8 fusion.7
  59.8 4.5 add_convert_fusion.1
  64.3 5.8 fusion.29
  70.1 9.6 convolution_bitcast_fusion.1
  79.8 5.6 convolution_bitcast_fusion
  85.7 6.9 fusion.55
  92.6 6.7 fusion.58
  99.7 5.2 add_convert_fusion
  104.9 46.8 %fusion.124 = f32[768,32000]{0,1:T(8,128)} fusion(bf16[512,768]{1,0:T(8,128)(2,1)S(1)} %add_convert_fusion, bf16[512,32000]{1,0:T(8,128)(2,1)} %param.14), kind=kOutput, calls=%fused_computation.135 | convolution fusion | flops 25165824000 | bytes 131858432 | tf_op jit(solution)/shard_map/td,tv->dv/dot_general | solution.py:36
  154.9 44.5 %reduce-scatter.10.cloned.1.call-done = f32[256,128]{0,1:T(8,128)} async-done(((f32[256,2048]{0,1:T(8,128)}), f32[256,128]{0,1:T(8,128)}) %reduce-scatter.10.cloned.1.call-update) | async-done | bytes 131088 | tf_op jit(solution)/shard_map/reduce_scatter | solution.py:63
  201.1 56.8 %reduce-scatter.14.cloned.1.call-done = f32[128,256]{1,0:T(8,128)} async-done(((f32[2048,256]{1,0:T(8,128)}), f32[128,256]{1,0:T(8,128)}) %reduce-scatter.14.cloned.1.call-update) | async-done | bytes 131088 | tf_op jit(solution)/shard_map/reduce_scatter | solution.py:64
  257.9 59.0 %reduce-scatter.12.cloned.1.call-done = f32[128,256]{1,0:T(8,128)} async-done(((f32[2048,256]{1,0:T(8,128)}), f32[128,256]{1,0:T(8,128)}) %reduce-scatter.12.cloned.1.call-update) | async-done | bytes 131088 | tf_op jit(solution)/shard_map/reduce_scatter | solution.py:64
  319.8 3.3 constant_dynamic-slice_fusion
  325.9 453.9 %reduce-scatter.16.cloned.1.call-done = f32[768,2000]{0,1:T(8,128)} async-done(((f32[768,32000]{0,1:T(8,128)}), f32[768,2000]{0,1:T(8,128)}) %reduce-scatter.16.cloned.1.call-update) | async-done | bytes 6144016
  779.8 14.5 %subtract_convert_fusion.2 = (bf16[768,2000]{0,1:T(8,128)(2,1)}, f32[768,2000]{0,1:T(8,128)}, f32[768,2000]{0,1:T(8,128)}) fusion(bf16[768,2000]{0,1:T(8,128)(2,1)} %copy.50, f32[768,2000]{0,1:T(8,128)} %reduce-scatter.16.cloned.1.call-done, f32[768,2000]{0,1:T(8,128)} %param.24, f32[768,2000]{0,1:T(8,128)} %param.25), kind=kLoop, calls=%fused_computation.20 | loop fusion | flops 23040000 | bytes 36864000 | tf_op jit(solution)/shard_map/convert_element_type | solution.py:81
  794.3 5.4 fusion.121
  802.4 3.2 copy.46
  811.9 5.0 fusion.45
  817.0 18.1 %all-gather.8.cloned.1.call-done = bf16[256,2048]{0,1:T(8,128)(2,1)} async-done(((bf16[256,128]{0,1:T(8,128)(2,1)}), bf16[256,2048]{0,1:T(8,128)(2,1)}) %all-gather.8.cloned.1.call-update) | async-done | bytes 1048592 | tf_op jit(solution)/shard_map/all_gather | solution.py:67
  837.5 3.2 pad_maximum_fusion
  840.8 8.6 copy.40
  849.4 13.3 %all-gather.12.cloned.1.call-done = bf16[2048,256]{1,0:T(8,128)(2,1)} async-done(((bf16[128,256]{1,0:T(8,128)(2,1)}), bf16[2048,256]{1,0:T(8,128)(2,1)}) %all-gather.12.cloned.1.call-update) | async-done | bytes 1048592 | tf_op jit(solution)/shard_map/all_gather | solution.py:68
  862.7 3.4 fusion.44
  866.1 24.3 %all-gather.10.cloned.1.call-done = bf16[2048,256]{1,0:T(8,128)(2,1)} async-done(((bf16[128,256]{1,0:T(8,128)(2,1)}), bf16[2048,256]{1,0:T(8,128)(2,1)}) %all-gather.10.cloned.1.call-update) | async-done | bytes 1048592 | tf_op jit(solution)/shard_map/all_gather | solution.py:68
  890.4 3.4 fusion.43
  893.8 3.2 pad_maximum_fusion.1
  897.0 178.3 %all-gather.14.cloned.1.call-done = bf16[768,32000]{0,1:T(8,128)(2,1)} async-done(((bf16[768,2000]{0,1:T(8,128)(2,1)}), bf16[768,32000]{0,1:T(8,128)(2,1)}) %all-gather.14.cloned.1.call-update) | async-done | bytes 49152016 | tf_op jit(solution)/shard_map/all_gather | solution.py:82
  1075.4 63.8 %copy.41 = bf16[768,32000]{1,0:T(8,128)(2,1)} copy(bf16[768,32000]{0,1:T(8,128)(2,1)} %all-gather.14.cloned.1.call-done) | data formatting | bytes 98304000
  (65 shorter events, 22.8 us)
Async XLA Ops:
  7.2 4.2 copy-start.6
  7.2 145.7 %reduce-scatter.8.cloned.1.call-start = ((), (), s32[]{:S(2)}) async-start(), calls=%async_computation.5 | async-start | bytes 2228224 | tf_op jit(solution)/shard_map/reduce_scatter | solution.py:63
  7.2 9.5 slice-start
  11.3 5.4 copy-start.8
  11.3 5.4 slice-start.1
  53.0 6.8 copy-start.10
  59.8 4.5 copy-start.9
  64.3 5.8 copy-start.1
  79.7 5.9 copy-start.7
  79.7 119.6 %reduce-scatter.10.cloned.1.call-start = ((), (), s32[]{:S(2)}) async-start(), calls=%async_computation.7 | async-start | bytes 2228224 | tf_op jit(solution)/shard_map/reduce_scatter | solution.py:63
  85.4 172.4 %reduce-scatter.14.cloned.1.call-start = ((), (), s32[]{:S(2)}) async-start(), calls=%async_computation.11 | async-start | bytes 2228224 | tf_op jit(solution)/shard_map/reduce_scatter | solution.py:64
  92.6 224.2 %reduce-scatter.12.cloned.1.call-start = ((), (), s32[]{:S(2)}) async-start(), calls=%async_computation.9 | async-start | bytes 2228224 | tf_op jit(solution)/shard_map/reduce_scatter | solution.py:64
  99.4 680.4 %reduce-scatter.16.cloned.1.call-start = ((), (), s32[]{:S(2)}) async-start(), calls=%async_computation.14 | async-start | bytes 104448000
  151.7 1.0 copy-start.2
  151.7 1.1 copy-start.3
  151.7 165.1 %copy-start.4 = (f32[2,128,256]{2,1,0:T(8,128)S(1)}, f32[2,128,256]{2,1,0:T(8,128)}, u32[]{:S(2)}) copy-start(f32[2,128,256]{2,1,0:T(8,128)} %param.22) | copy-start | bytes 786436
  151.7 165.1 %copy-start.5 = (f32[2,128,256]{2,1,0:T(8,128)S(1)}, f32[2,128,256]{2,1,0:T(8,128)}, u32[]{:S(2)}) copy-start(f32[2,128,256]{2,1,0:T(8,128)} %param.23) | copy-start | bytes 786436
  151.7 660.2 %all-gather.6.cloned.1.call-start = ((), (), s32[]{:S(2)}) async-start(), calls=%async_computation.6 | async-start | bytes 1114112 | tf_op jit(solution)/shard_map/all_gather | solution.py:67
  154.6 680.4 %all-gather.8.cloned.1.call-start = ((), (), s32[]{:S(2)}) async-start(), calls=%async_computation.8 | async-start | bytes 1114112 | tf_op jit(solution)/shard_map/all_gather | solution.py:67
  201.1 661.7 %all-gather.12.cloned.1.call-start = ((), (), s32[]{:S(2)}) async-start(), calls=%async_computation.12 | async-start | bytes 1114112 | tf_op jit(solution)/shard_map/all_gather | solution.py:68
  318.8 571.7 %all-gather.10.cloned.1.call-start = ((), (), s32[]{:S(2)}) async-start(), calls=%async_computation.10 | async-start | bytes 1114112 | tf_op jit(solution)/shard_map/all_gather | solution.py:68
  319.5 755.9 %all-gather.14.cloned.1.call-start = ((), (), s32[]{:S(2)}) async-start(), calls=%async_computation.13 | async-start | bytes 52224000 | tf_op jit(solution)/shard_map/all_gather | solution.py:82
  835.0 2.5 copy-start
Sparse Core Ops, SparseCore 0:
  79.8 60.3 reduce-scatter.7
  143.1 56.1 reduce-scatter.9
  201.6 56.2 reduce-scatter.13
  260.5 56.2 reduce-scatter.11
  322.0 457.7 reduce-scatter.15
  781.9 25.4 all-gather.5
  809.6 25.4 all-gather.7
  837.3 25.4 all-gather.11
  865.0 25.4 all-gather.9
  893.1 182.2 all-gather.13
where the time goes:
time: 1160 us; the launch traced here: 1150 us
  waiting for transfers between devices  849 us (73%)
  matrix products  158 us (14%)
  local copies, waits for them, and re-layouts  93.8 us (8%)
  other arithmetic  29.9 us (3%)
  between operations  14.9 us (1%)
    unnamed x11, waiting for transfers between devices  455 us
    all_gather x1, waiting for transfers between devices, local_step(): w_out_new = lax.all_gather(w_out_part, DATA_AXIS, axis=1, tiled=True)  178 us
    reduce_scatter x2, waiting for transfers between devices, local_step(): lax.psum_scatter(low_down, DATA_AXIS, scatter_dimension=0, tiled=True)  116 us
    unnamed x37, local copies, waits for them, and re-layouts  85.1 us
    dot_general x1, matrix products, forward_backward(): jnp.einsum('td,tv->dv', hidden, d_logits, preferred_element_type=jnp.floa...  46.8 us
    reduce_scatter x2, waiting for transfers between devices, local_step(): lax.psum_scatter(low_up, DATA_AXIS, scatter_dimension=1, tiled=True)  44.5 us
    all_gather x2, waiting for transfers between devices, local_step(): lax.all_gather(dir_down.astype(jnp.bfloat16), DATA_AXIS, axis=0, tiled=True)  37.7 us
    dot_general x1, matrix products, forward_backward(): jnp.einsum('tv,dv->td', d_logits, w_out, preferred_element_type=jnp.float32)  33.1 us
  transfers between devices with their start and end apart: 10, of which 8 were waited for; matrix products, arithmetic and copies ran while one was open for 13% of the time, Pallas kernels for 0%

commit v1 on v0

v1 whole, which is shorter than its diff:
```python
import jax
import jax.numpy as jnp
from jax import lax
from jax.experimental import pallas as pl
from jax.experimental.pallas import tpu as pltpu
from jax.sharding import PartitionSpec as P


BETA1 = 0.9
BETA2 = 0.999
EPS = 1e-8
STEP = 4
LR = 0.02
ALPHA = 0.5
LR_HEAD = 0.01
DATA_AXIS = 'data'
DEVICES = 16
LANES = 128
CORE, X, Y, Z = 1, 2, 4, 8
GROUP_BITS = ((Z, Y, X), (Y, X, Z), (X, Z, Y))
GROUP_TILES = (6, 5, 5)
ROW_CHUNK = 256


def gelu_tanh(values):
    return jax.nn.gelu(values, approximate=True)


def adam_update(gradient, moment_one, moment_two):
    moment_one = BETA1 * moment_one + (1.0 - BETA1) * gradient
    moment_two = BETA2 * moment_two + (1.0 - BETA2) * gradient * gradient
    direction = (moment_one / (1.0 - BETA1 ** STEP)) / (jnp.sqrt(moment_two / (1.0 - BETA2 ** STEP)) + EPS)
    return moment_one, moment_two, direction


def swap(values, mask):
    return lax.ppermute(values, DATA_AXIS, [(i, i ^ mask) for i in range(DEVICES)])


def group_offsets():
    offsets = [0]
    for tiles in GROUP_TILES:
        offsets.append(offsets[-1] + tiles * LANES)
    return offsets


def pack_columns(values, jobs, shard_cols):
    rows, total = values.shape
    count = jobs[0][0].shape[0]
    row_block = 256
    tables, in_specs, out_specs, out_shapes = [], [], [], []
    for j, (owners, offset, width) in enumerate(jobs):
        window = width + LANES
        starts = owners * shard_cols + offset
        tiles = starts // LANES
        bases = jnp.minimum(tiles, (total - window) // LANES)
        tables.append(jnp.stack([bases, tiles - bases, starts % LANES]))
        in_specs.append(pl.BlockSpec((pl.Element(rows), pl.Element(window)), lambda s, t, j=j: (0, pl.multiple_of(t[j, 0, s] * LANES, LANES))))
        out_specs.append(pl.BlockSpec((1, rows, width), lambda s, t: (s, 0, 0)))
        out_shapes.append(jax.ShapeDtypeStruct((count, rows, width), jnp.bfloat16))

    def body(table_ref, *refs):
        entry = pl.program_id(0)

        def selector(depth, cols, by):
            source = lax.broadcasted_iota(jnp.int32, (depth, cols), 0)
            target = lax.broadcasted_iota(jnp.int32, (depth, cols), 1)
            return jnp.where(source == target + by, 1.0, 0.0).astype(jnp.bfloat16)

        for j, (_, _, width) in enumerate(jobs):
            in_ref, out_ref = refs[j], refs[len(jobs) + j]
            first, shift = table_ref[j, 1, entry], table_ref[j, 2, entry]
            tail = width % (2 * LANES) or 2 * LANES
            inner = selector(3 * LANES, 2 * LANES, shift)
            outer = selector(tail + LANES, tail, shift + first * LANES)

            def step(i, carry):
                sl = pl.ds(pl.multiple_of(i * row_block, row_block), row_block)
                for at in range(0, width - tail, 2 * LANES):
                    source = in_ref[sl, pl.ds(pl.multiple_of(first * LANES + at, LANES), 3 * LANES)]
                    out_ref[0, sl, at:at + 2 * LANES] = jnp.dot(source, inner, preferred_element_type=jnp.float32).astype(jnp.bfloat16)
                at = width - tail
                out_ref[0, sl, at:] = jnp.dot(in_ref[sl, at:], outer, preferred_element_type=jnp.float32).astype(jnp.bfloat16)
                return carry

            lax.fori_loop(0, rows // row_block, step, 0)

    moved = sum(count * rows * width for _, _, width in jobs)
    return pl.pallas_call(
        body,
        grid_spec=pltpu.PrefetchScalarGridSpec(num_scalar_prefetch=1, grid=(count,), in_specs=in_specs, out_specs=out_specs),
        out_shape=out_shapes,
        cost_estimate=pl.CostEstimate(flops=moved * 768, bytes_accessed=moved * 4, transcendentals=0),
        name='pack_columns',
    )(jnp.stack(tables), *[values] * len(jobs))


def project_gradients(terms, owners):
    count = len(terms)
    model, rank = terms[0][0].shape
    tokens, hidden = terms[0][2].shape
    cols = hidden // owners
    step_owners = 4
    block = step_owners * cols

    def body(*refs):
        out_ref, turned = refs[-2], refs[-1]
        for m in range(count):
            p_ref, h_ref, e_ref = refs[3 * m:3 * m + 3]

            @pl.when(pl.program_id(0) == m)
            def _():
                @pl.when(pl.program_id(1) == 0)
                def _():
                    turned[...] = h_ref[...].T

                gradient = jnp.dot(turned[...], e_ref[...], preferred_element_type=jnp.float32)
                high = gradient.astype(jnp.bfloat16)
                low = (gradient - high.astype(jnp.float32)).astype(jnp.bfloat16)
                left = p_ref[...]
                total = jnp.dot(left, high, preferred_element_type=jnp.float32) + jnp.dot(left, low, preferred_element_type=jnp.float32)
                for k in range(step_owners):
                    out_ref[k, 0] = total[:, k * cols:(k + 1) * cols]

    in_specs, operands = [], []
    for m, (p, h, e) in enumerate(terms):
        in_specs += [pl.BlockSpec((rank, model), lambda t, c: (0, 0)), pl.BlockSpec((tokens, model), lambda t, c: (0, 0)),
                     pl.BlockSpec((tokens, block), lambda t, c, m=m: (0, jnp.where(t == m, c, jnp.where(t < m, 0, hidden // block - 1))))]
        operands += [p.T, h, e]
    return pl.pallas_call(
        body,
        grid=(count, hidden // block),
        in_specs=in_specs,
        out_specs=pl.BlockSpec((step_owners, 1, rank, cols), lambda t, c: (c, t, 0, 0)),
        out_shape=jax.ShapeDtypeStruct((owners, count, rank, cols), jnp.float32),
        scratch_shapes=[pltpu.VMEM((model, tokens), jnp.bfloat16)],
        cost_estimate=pl.CostEstimate(flops=count * 2 * model * hidden * (tokens + 2 * rank), bytes_accessed=count * hidden * (tokens * 2 + rank * 4), transcendentals=0),
        name='project_gradients',
    )(*operands)


def reduce_head(near, packed, w_own, mom_out, var_out, chunk):
    groups = len(GROUP_BITS)
    offsets = group_offsets()
    shard_cols = mom_out.shape[0]
    owners, tokens, _ = packed[0][0].shape
    widths = [offsets[g + 1] - offsets[g] for g in range(groups)]
    masks = [(0, CORE, bit, bit | CORE) for bit, _, _ in GROUP_BITS]
    near_keys = sorted(near)

    def body(*refs):
        near_refs = dict(zip(near_keys, refs))
        refs = refs[len(near_keys):]
        packed_refs = [refs[4 * g:4 * g + 4] for g in range(groups)]
        refs = refs[4 * groups:]
        w_ref, mom_ref, var_ref, w_out_ref, mom_out_ref, var_out_ref = refs[:6]
        refs = refs[6:]
        blocks, refs = refs[:groups], refs[groups:]
        part, refs = refs[:groups], refs[groups:]
        got, refs = refs[:groups], refs[groups:]
        got_own, refs = refs[:groups], refs[groups:]
        w_buf, mom_buf, var_buf, mom_turned, var_turned, load_sem, first_send, first_recv, second_send, second_recv, state_sem = refs
        me = lax.axis_index(DATA_AXIS)
        barrier = pltpu.get_barrier_semaphore()
        for bit in (X, Y, Z):
            pl.semaphore_signal(barrier, inc=1, device_id=(me ^ bit,), device_id_type=pl.DeviceIdType.MESH)

        def load(g, entry):
            return [pltpu.make_async_copy(packed_refs[g][k].at[entry], blocks[g].at[k], load_sem.at[g, k]) for k in range(4)]

        for g in range(groups):
            for copy in load(g, 3):
                copy.start()
        rows = pl.ds(chunk * ROW_CHUNK, ROW_CHUNK)
        valid = pl.ds(0, shard_cols)
        state = [pltpu.make_async_copy(w_ref.at[rows], w_buf, state_sem.at[0]),
                 pltpu.make_async_copy(mom_ref.at[:, rows], mom_turned.at[valid], state_sem.at[1]),
                 pltpu.make_async_copy(var_ref.at[:, rows], var_turned.at[valid], state_sem.at[2])]
        for copy in state:
            copy.start()
        pl.semaphore_wait(barrier, 3)

        def first_copy(g, entry):
            return pltpu.make_async_remote_copy(
                src_ref=part[g].at[entry], dst_ref=got[g].at[entry - 2], send_sem=first_send.at[g, entry - 2], recv_sem=first_recv.at[g, entry - 2],
                device_id=(me ^ GROUP_BITS[g][1],), device_id_type=pl.DeviceIdType.MESH)

        def second_copy(g):
            return pltpu.make_async_remote_copy(
                src_ref=part[g].at[1], dst_ref=got_own[g], send_sem=second_send.at[g], recv_sem=second_recv.at[g],
                device_id=(me ^ GROUP_BITS[g][2],), device_id_type=pl.DeviceIdType.MESH)

        def step(i, carry):
            entry = 3 - i
            for g in range(groups):
                for copy in load(g, entry):
                    copy.wait()
                acc = None
                for k in range(4):
                    term = jnp.dot(near_refs[masks[g][k]][...], blocks[g][k], preferred_element_type=jnp.float32)
                    acc = term if acc is None else acc + term
                part[g][entry] = acc

                @pl.when(i < 3)
                def _():
                    for copy in load(g, entry - 1):
                        copy.start()

                @pl.when(i == 0)
                def _():
                    first_copy(g, 3).start()

                @pl.when(i == 1)
                def _():
                    first_copy(g, 2).start()

                @pl.when(i == 2)
                def _():
                    first_copy(g, 3).wait_recv()
                    part[g][1] = part[g][1] + got[g][1]
                    second_copy(g).start()
            return carry

        lax.fori_loop(0, 4, step, 0)

        for copy in state:
            copy.wait()
        for at in range(0, offsets[-1], LANES):
            cols = slice(at, at + LANES)
            mom_buf[:, cols] = mom_turned[cols].T
            var_buf[:, cols] = var_turned[cols].T
        block = 32
        for g in range(groups):
            first_copy(g, 2).wait_recv()
            second_copy(g).wait_recv()
            cols = slice(offsets[g], offsets[g + 1])

            def adam(i, carry):
                sl = pl.ds(pl.multiple_of(i * block, block), block)
                gradient = part[g][0, sl] + got[g][0, sl] + got_own[g][sl]
                m_new, v_new, direction = adam_update(gradient, mom_buf[sl, cols], var_buf[sl, cols])
                mom_buf[sl, cols] = m_new
                var_buf[sl, cols] = v_new
                w_buf[sl, cols] = (w_buf[sl, cols].astype(jnp.float32) - LR_HEAD * direction).astype(jnp.bfloat16)
                return carry

            lax.fori_loop(0, ROW_CHUNK // block, adam, 0)
        results = [pltpu.make_async_copy(w_buf, w_out_ref, state_sem.at[0]),
                   pltpu.make_async_copy(mom_turned.at[valid], mom_out_ref, state_sem.at[1]),
                   pltpu.make_async_copy(var_turned.at[valid], var_out_ref, state_sem.at[2])]
        results[0].start()
        for at in range(0, offsets[-1], LANES):
            cols = slice(at, at + LANES)
            mom_turned[cols] = mom_buf[:, cols].T
            var_turned[cols] = var_buf[:, cols].T
        results[1].start()
        results[2].start()
        for g in range(groups):
            first_copy(g, 3).wait_send()
            first_copy(g, 2).wait_send()
            second_copy(g).wait_send()
        for copy in results:
            copy.wait()

    anywhere = pl.BlockSpec(memory_space=pl.ANY)
    near_spec = pl.BlockSpec((ROW_CHUNK, tokens), lambda s: (chunk, 0))
    scratch = [pltpu.VMEM((4, tokens, w), jnp.bfloat16) for w in widths]
    scratch += [pltpu.VMEM((owners, ROW_CHUNK, w), jnp.float32) for w in widths]
    scratch += [pltpu.VMEM((2, ROW_CHUNK, w), jnp.float32) for w in widths]
    scratch += [pltpu.VMEM((ROW_CHUNK, w), jnp.float32) for w in widths]
    scratch += [pltpu.VMEM((ROW_CHUNK, offsets[-1]), jnp.bfloat16)]
    scratch += [pltpu.VMEM((ROW_CHUNK, offsets[-1]), jnp.float32)] * 2 + [pltpu.VMEM((offsets[-1], ROW_CHUNK), jnp.float32)] * 2
    scratch += [pltpu.SemaphoreType.DMA((groups, 4)), pltpu.SemaphoreType.DMA((groups, 2)), pltpu.SemaphoreType.DMA((groups, 2)),
                pltpu.SemaphoreType.DMA((groups,)), pltpu.SemaphoreType.DMA((groups,)), pltpu.SemaphoreType.DMA((3,))]
    return pl.pallas_call(
        body,
        grid=(1,),
        in_specs=[near_spec] * len(near_keys) + [anywhere] * (4 * groups + 3),
        out_specs=[anywhere] * 3,
        out_shape=[jax.ShapeDtypeStruct((ROW_CHUNK, offsets[-1]), jnp.bfloat16)] + [jax.ShapeDtypeStruct((shard_cols, ROW_CHUNK), jnp.float32)] * 2,
        scratch_shapes=scratch,
        cost_estimate=pl.CostEstimate(flops=60_000_000_000, bytes_accessed=100_000_000, transcendentals=0),
        compiler_params=pltpu.CompilerParams(collective_id=chunk, has_side_effects=True, vmem_limit_bytes=60 * 1024 * 1024),
        name='reduce_head',
    )(*[near[k] for k in near_keys], *[packed[g][m] for g in range(groups) for m in masks[g]], w_own, mom_out, var_out)


def place_parts(parts, vocab, total_rows, row_chunk, previous):
    shard_cols = vocab // DEVICES
    rows = 32
    count = -(-shard_cols // LANES)

    def body(*refs):
        part_ref, out_ref = refs[0], refs[-1]
        lane = lax.broadcasted_iota(jnp.int32, (rows, LANES), 1)
        pending = None
        for owner in range(DEVICES):
            base, shift = divmod(owner * shard_cols, LANES)
            rolled = []
            for index in range(count):
                piece = part_ref[owner, :, index * LANES:(index + 1) * LANES]
                rolled.append(pltpu.roll(piece, shift, 1) if shift else piece)
            end = owner * shard_cols + shard_cols
            for tile in range(base, -(-end // LANES)):
                index = tile - base
                if shift == 0:
                    value = rolled[index]
                elif index == 0:
                    value = jnp.where(lane < shift, pending, rolled[0])
                elif index == count:
                    value = rolled[count - 1]
                else:
                    value = jnp.where(lane < shift, rolled[index - 1], rolled[index])
                if (tile + 1) * LANES <= end:
                    out_ref[:, tile * LANES:(tile + 1) * LANES] = value
                else:
                    pending = value

    steps = ROW_CHUNK // rows
    in_specs = [pl.BlockSpec((DEVICES, rows, count * LANES), lambda s: (0, s, 0))]
    operands = [parts]
    aliases = {}
    if previous is not None:
        in_specs.append(pl.BlockSpec(memory_space=pl.ANY))
        operands.append(previous)
        aliases = {1: 0}
    return pl.pallas_call(
        body,
        grid=(steps,),
        in_specs=in_specs,
        out_specs=pl.BlockSpec((rows, vocab), lambda s: (row_chunk * steps + s, 0)),
        out_shape=jax.ShapeDtypeStruct((total_rows, vocab), jnp.bfloat16),
        input_output_aliases=aliases,
        cost_estimate=pl.CostEstimate(flops=ROW_CHUNK * vocab * 16, bytes_accessed=ROW_CHUNK * vocab * 4, transcendentals=0),
        name='place_parts',
    )(*operands)


def back_project(gathered, w_up, w_down, proj_up, proj_down):
    layers, model, hidden = w_up.shape
    _, _, rank, cols = gathered.shape
    step_owners = 4
    block = step_owners * cols

    def body(up_dir_ref, down_dir_ref, w_up_ref, w_down_ref, p_ref, q_ref, up_ref, down_ref):
        up_dir = jnp.concatenate([up_dir_ref[k, 0] for k in range(step_owners)], axis=1)
        down_dir = jnp.concatenate([down_dir_ref[k, 0] for k in range(step_owners)], axis=1)
        step_up = jnp.dot(p_ref[0], up_dir, preferred_element_type=jnp.float32)
        up_ref[0] = (w_up_ref[0].astype(jnp.float32) - LR * ALPHA * step_up).astype(jnp.bfloat16)
        step_down = lax.dot_general(down_dir, q_ref[0], (((0,), (1,)), ((), ())), preferred_element_type=jnp.float32)
        down_ref[0] = (w_down_ref[0].astype(jnp.float32) - LR * ALPHA * step_down).astype(jnp.bfloat16)

    up_spec = pl.BlockSpec((1, model, block), lambda l, c: (l, 0, c))
    down_spec = pl.BlockSpec((1, block, model), lambda l, c: (l, c, 0))
    proj_spec = pl.BlockSpec((1, model, rank), lambda l, c: (l, 0, 0))
    return pl.pallas_call(
        body,
        grid=(layers, hidden // block),
        in_specs=[pl.BlockSpec((step_owners, 1, rank, cols), lambda l, c: (c, l, 0, 0)),
                  pl.BlockSpec((step_owners, 1, rank, cols), lambda l, c: (c, layers + l, 0, 0)),
                  up_spec, down_spec, proj_spec, proj_spec],
        out_specs=[up_spec, down_spec],
        out_shape=[jax.ShapeDtypeStruct(w_up.shape, jnp.bfloat16), jax.ShapeDtypeStruct(w_down.shape, jnp.bfloat16)],
        cost_estimate=pl.CostEstimate(flops=8 * model * hidden * rank, bytes_accessed=30_000_000, transcendentals=0),
        name='back_project',
    )(gathered, gathered, w_up, w_down, proj_up, proj_down)


def forward(tokens, w_up, w_down):
    num_layers = w_up.shape[0]
    hidden = tokens
    saved_acts = []
    for layer_idx in range(num_layers):
        pre_act = jnp.dot(hidden, w_up[layer_idx], preferred_element_type=jnp.float32).astype(jnp.bfloat16)
        post_act = gelu_tanh(pre_act.astype(jnp.float32)).astype(jnp.bfloat16)
        saved_acts.append((hidden, pre_act, post_act))
        hidden = (hidden.astype(jnp.float32) + jnp.dot(post_act, w_down[layer_idx], preferred_element_type=jnp.float32)).astype(jnp.bfloat16)
    return hidden, saved_acts


def backward(saved_acts, d_logits, w_up, w_down, w_out):
    num_layers = w_up.shape[0]
    grad_hidden = jnp.einsum('tv,dv->td', d_logits, w_out, preferred_element_type=jnp.float32).astype(jnp.bfloat16)
    up_terms = [None] * num_layers
    down_terms = [None] * num_layers
    for layer_idx in reversed(range(num_layers)):
        hidden_in, pre_act, post_act = saved_acts[layer_idx]
        down_terms[layer_idx] = (grad_hidden, post_act)
        d_post = jnp.einsum('td,fd->tf', grad_hidden, w_down[layer_idx], preferred_element_type=jnp.float32)
        gelu_pull = jax.vjp(gelu_tanh, pre_act.astype(jnp.float32))[1]
        d_pre = gelu_pull(d_post)[0].astype(jnp.bfloat16)
        up_terms[layer_idx] = (hidden_in, d_pre)
        if layer_idx > 0:
            grad_hidden = (grad_hidden.astype(jnp.float32) + jnp.einsum('tf,df->td', d_pre, w_up[layer_idx], preferred_element_type=jnp.float32)).astype(jnp.bfloat16)
    return up_terms, down_terms


def exchange_hidden(hidden):
    near = {0: hidden.T}
    near[CORE] = swap(near[0], CORE)
    for bit in (Z, Y, X):
        near[bit] = swap(near[0], bit)
    for bit in (Z, Y, X):
        near[bit | CORE] = swap(near[bit], CORE)
    return near


def local_step(tokens, d_logits, w_up, w_down, w_out, proj_up, proj_down, mom_up, var_up, mom_down, var_down, mom_out, var_out):
    me = lax.axis_index(DATA_AXIS)
    layers = w_up.shape[0]
    total_rows, vocab = w_out.shape
    shard_cols = mom_out.shape[1]
    offsets = group_offsets()
    mine = {}
    for partner in (2, 3, 1, 0):
        jobs, masks = [], []
        for g, (bit, first, second) in enumerate(GROUP_BITS):
            masks.append((0, CORE, bit, bit | CORE)[partner])
            rels = jnp.array([0, second, first, first | second], jnp.int32) ^ masks[-1]
            jobs.append((rels ^ me, offsets[g], offsets[g + 1] - offsets[g]))
        for g, value in enumerate(pack_columns(d_logits, jobs, shard_cols)):
            mine[g, masks[g]] = value
    packed = [dict() for _ in GROUP_BITS]
    for (g, mask), value in mine.items():
        packed[g][mask] = swap(value, mask) if mask else value
    tokens, mine = lax.optimization_barrier((tokens, mine))
    hidden, saved_acts = forward(tokens, w_up, w_down)
    near = exchange_hidden(hidden)
    up_terms, down_terms = backward(saved_acts, d_logits, w_up, w_down, w_out)
    terms = [(proj_up[l], *up_terms[l]) for l in range(layers)] + [(proj_down[l], *down_terms[l]) for l in range(layers)]
    low = project_gradients(terms, DEVICES)
    _, _, rank, cols = low.shape
    low_scattered = lax.psum_scatter(low.reshape(-1, cols), DATA_AXIS, scatter_dimension=0, tiled=True).reshape(2 * layers, rank, cols)
    w_own = pack_columns(w_out, [(me[None], 0, offsets[-1])], shard_cols)[0][0]
    w_own, near, low = lax.optimization_barrier((w_own, near, low))
    chunks = total_rows // ROW_CHUNK
    results = []
    gathered = []
    for chunk in range(chunks):
        if results:
            w_own, results[-1][0] = lax.optimization_barrier((w_own, results[-1][0]))
        results.append(list(reduce_head(near, packed, w_own, mom_out.T, var_out.T, chunk)))
        payload = results[-1][0]
        if chunk == 1:
            low_scattered, payload = lax.optimization_barrier((low_scattered, payload))
            m_up, v_up, dir_up = adam_update(low_scattered[:layers], mom_up, var_up)
            m_down, v_down, dir_down = adam_update(low_scattered[layers:].transpose(0, 2, 1), mom_down, var_down)
            dirs = jnp.concatenate([dir_up, dir_down.transpose(0, 2, 1)], axis=0).astype(jnp.bfloat16)
            side = payload.shape[1] // cols
            dirs = dirs.reshape(side, -1, cols).transpose(1, 0, 2).reshape(-1, payload.shape[1])
            payload = jnp.concatenate([payload, dirs], axis=0)
        gathered.append(lax.all_gather(payload, DATA_AXIS, axis=0))
    w_out_new = None
    gathered[0], results[-1][1] = lax.optimization_barrier((gathered[0], results[-1][1]))
    for chunk in range(chunks):
        w_out_new = place_parts(gathered[chunk], vocab, total_rows, chunk, w_out_new)
    dirs = gathered[1][:, ROW_CHUNK:].reshape(DEVICES, -1, side, cols).transpose(0, 2, 1, 3).reshape(DEVICES, 2 * layers, rank, cols)
    w_up_new, w_down_new = back_project(dirs, w_up, w_down, proj_up, proj_down)
    m_out = jnp.concatenate([r[1] for r in results], axis=1).T
    v_out = jnp.concatenate([r[2] for r in results], axis=1).T
    return w_up_new, w_down_new, w_out_new, m_up, v_up, m_down, v_down, m_out, v_out


def solution(mesh):
    row_spec = P(DATA_AXIS, None)
    whole = P()
    up_spec = P(None, None, DATA_AXIS)
    down_spec = P(None, DATA_AXIS, None)
    head_spec = P(None, DATA_AXIS)
    in_specs = (row_spec, row_spec, whole, whole, whole, whole, whole, up_spec, up_spec, down_spec, down_spec, head_spec, head_spec)
    out_specs = (whole, whole, whole, up_spec, up_spec, down_spec, down_spec, head_spec, head_spec)

    return jax.shard_map(local_step, mesh=mesh, in_specs=in_specs, out_specs=out_specs, check_vma=False)
```

time: 1160 us -> 870 us (0.75)
  waiting for transfers between devices: 849 us -> 331 us
  Pallas kernels: 0 us -> 377 us
  matrix products: 158 us -> 70.7 us
  local copies, waits for them, and re-layouts: 93.8 us -> 21.7 us
  starting transfers between devices: 1.05 us -> 25.3 us
    unnamed x11 -> x4, waiting for transfers between devices: 455 us -> 0.07 us
    pallas_call x0 -> x13, Pallas kernels: none -> 377 us  [the longest x3 235 us: reduce_head(): pl.pallas_call(body, grid=(1,), in_specs=[near_spec] * len(near_keys) + [...]
    ppermute x0 -> x16, waiting for transfers between devices: none -> 272 us  [swap(): lax.ppermute(values, DATA_AXIS, [(i, i ^ mask) for i in range(DEVICES)])]
    all_gather x5 -> x3, waiting for transfers between devices: 234 us -> 59.5 us  [local_step(): gathered.append(lax.all_gather(payload, DATA_AXIS, axis=0))]
    reduce_scatter x4 -> x1, waiting for transfers between devices: 160 us -> 0.02 us  [local_step(): lax.psum_scatter(low.reshape(-1, cols), DATA_AXIS, scatter_dimension=0, t...]
    dot_general x17 -> x8, matrix products: 158 us -> 70.7 us  [the longest x1 33.5 us: backward(): jnp.einsum('tv,dv->td', d_logits, w_out, preferred_element_type=jnp.float32)]
    unnamed x37 -> x77, local copies, waits for them, and re-layouts: 85.1 us -> 12.8 us
    convert_element_type x2 -> x0, other arithmetic: 16.4 us -> none  [the longest x1 14.5 us: local_step(): (w_out_part.astype(jnp.float32) - LR_HEAD * dir_out).astype(jnp.bfloat16)]
  transfers between devices with their start and end apart: 10 -> 20, of which waited for: 8 -> 10; matrix products, arithmetic and copies ran while one was open for 13% -> 4% of each run, Pallas kernels for 0% -> 33%
where the time goes in v1:
time: 870 us; the launch traced here: 860 us
  Pallas kernels  377 us (43%)
  waiting for transfers between devices  331 us (38%)
  matrix products  70.7 us (8%)
  starting transfers between devices  25.3 us (3%)
  local copies, waits for them, and re-layouts  21.7 us (2%)
  other arithmetic  19.2 us (2%)
  between operations  14.8 us (2%)
    ppermute x16, waiting for transfers between devices, swap(): lax.ppermute(values, DATA_AXIS, [(i, i ^ mask) for i in range(DEVICES)])  272 us
    pallas_call x3, Pallas kernels, reduce_head(): pl.pallas_call(body, grid=(1,), in_specs=[near_spec] * len(near_keys) + [...  235 us
    all_gather x3, waiting for transfers between devices, local_step(): gathered.append(lax.all_gather(payload, DATA_AXIS, axis=0))  59.5 us
    pallas_call x5, Pallas kernels, pack_columns(): pl.pallas_call(body, grid_spec=pltpu.PrefetchScalarGridSpec(num_scalar_pr...  59.3 us
    pallas_call x3, Pallas kernels, place_parts(): pl.pallas_call(body, grid=(steps,), in_specs=in_specs, out_specs=pl.Block...  46.2 us
    dot_general x1, matrix products, backward(): jnp.einsum('tv,dv->td', d_logits, w_out, preferred_element_type=jnp.float32)  33.5 us
    pallas_call x1, Pallas kernels, project_gradients(): pl.pallas_call(body, grid=(count, hidden // block), in_specs=in_specs, ou...  22.6 us
  transfers between devices with their start and end apart: 20, of which 10 were waited for; matrix products, arithmetic and copies ran while one was open for 4% of the time, Pallas kernels for 33%

profile of v1, /device:TPU:0, one launch (start us, length us, event | category | flops | bytes accessed | tf_op | source)
XLA Modules:
  0.0 859.7 jit_solution(7688304168670186591)
XLA Ops:
  8.9 13.1 %pack_columns.5 = (bf16[4,512,768]{2,1,0:T(8,128)(2,1)}, bf16[4,512,640]{2,1,0:T(8,128)(2,1)}, bf16[4,512,640]{2,1,0:T(8,128)(2,1)}) custom-call(s32[3,3,4]{2,1,0:T(4,128)} %pad_add_fusion.table_ref, bf16[512,32000]{1,0:T(8,128)(2,1)} %refs_2_.7, bf16[512,32000]{1,0:T(8,128)(2,1)} %refs_2_.7, bf16[512,32000]{1,0:T(8,128)(2,1)} %refs_2_.7), custom_call_target="tpu_custom_call" | custom-call | flops 3221225472 | bytes 16777216 | tf_op jit(solution)/shard_map/pack_columns/pallas_call | solution.py:89
  22.6 13.3 %pack_columns.6 = (bf16[4,512,768]{2,1,0:T(8,128)(2,1)}, bf16[4,512,640]{2,1,0:T(8,128)(2,1)}, bf16[4,512,640]{2,1,0:T(8,128)(2,1)}) custom-call(s32[3,3,4]{2,1,0:T(4,128)} %pad_add_fusion.1.table_ref, bf16[512,32000]{1,0:T(8,128)(2,1)} %refs_2_.7, bf16[512,32000]{1,0:T(8,128)(2,1)} %refs_2_.7, bf16[512,32000]{1,0:T(8,128)(2,1)} %refs_2_.7), custom_call_target="tpu_custom_call" | custom-call | flops 3221225472 | bytes 16777216 | tf_op jit(solution)/shard_map/pack_columns/pallas_call | solution.py:89
  36.6 13.1 %pack_columns.7 = (bf16[4,512,768]{2,1,0:T(8,128)(2,1)}, bf16[4,512,640]{2,1,0:T(8,128)(2,1)}, bf16[4,512,640]{2,1,0:T(8,128)(2,1)}) custom-call(s32[3,3,4]{2,1,0:T(4,128)} %pad_add_fusion.2.table_ref, bf16[512,32000]{1,0:T(8,128)(2,1)} %refs_2_.7, bf16[512,32000]{1,0:T(8,128)(2,1)} %refs_2_.7, bf16[512,32000]{1,0:T(8,128)(2,1)} %refs_2_.7), custom_call_target="tpu_custom_call" | custom-call | flops 3221225472 | bytes 16777216 | tf_op jit(solution)/shard_map/pack_columns/pallas_call | solution.py:89
  50.3 13.2 %pack_columns.8 = (bf16[4,512,768]{2,1,0:T(8,128)(2,1)}, bf16[4,512,640]{2,1,0:T(8,128)(2,1)}, bf16[4,512,640]{2,1,0:T(8,128)(2,1)}) custom-call(s32[3,3,4]{2,1,0:T(4,128)} %pad_add_fusion.3.table_ref, bf16[512,32000]{1,0:T(8,128)(2,1)} %refs_2_.7, bf16[512,32000]{1,0:T(8,128)(2,1)} %refs_2_.7, bf16[512,32000]{1,0:T(8,128)(2,1)} %refs_2_.7), custom_call_target="tpu_custom_call" | custom-call | flops 3221225472 | bytes 16777216 | tf_op jit(solution)/shard_map/pack_columns/pallas_call | solution.py:89
  63.9 6.0 fusion.11
  69.9 5.0 add_convert_fusion.2
  74.9 4.2 fusion.19
  80.3 33.5 %convolution_convert_fusion.refs_10_ = bf16[512,768]{1,0:T(8,128)(2,1)S(1)} fusion(bf16[512,32000]{1,0:T(8,128)(2,1)} %refs_2_.7, bf16[768,32000]{1,0:T(8,128)(2,1)} %refs_0_.9), kind=kOutput, calls=%fused_computation.59 | convolution fusion | flops 25166217216 | bytes 82706432 | tf_op jit(solution)/shard_map/tv,dv->td/dot_general | solution.py:383
  113.8 6.3 fusion.4.refs_5_
  121.5 3.9 add_convert_fusion.1.refs_7_
  126.3 6.9 fusion.7.refs_2_
  137.0 22.6 %project_gradients.1 = f32[16,4,256,128]{3,2,1,0:T(8,128)} custom-call(bf16[256,768]{1,0:T(8,128)(2,1)} %bitcast.216, bf16[512,768]{1,0:T(8,128)(2,1)} %refs_1_.8, bf16[512,2048]{1,0:T(8,128)(2,1)} %fusion.7.refs_2_, bf16[256,768]{1,0:T(8,128)(2,1)} %bitcast.217, bf16[512,768]{1,0:T(8,128)(2,1)} %copy.56.refs_4_, bf16[512,2048]{1,0:T(8,128)(2,1)} %copy-done.27, ...), custom_call_target="tpu_custom_call" | custom-call | flops 12884901888 | bytes 16777216 | tf_op jit(solution)/shard_map/project_gradients/pallas_call | solution.py:130
  159.6 10.3 %all-gather.11.cloned.1.call-start = ((), (), s32[]{:S(2)}) async-start(), calls=%async_computation.4 | async-start | bytes 17825792 | tf_op jit(solution)/shard_map/all_gather | solution.py:452
  169.9 5.0 fusion.57.refs_0_
  181.8 31.4 %collective-permute-done.1.refs_2_ = bf16[768,512]{1,0:T(8,128)(2,1)S(1)} collective-permute-done((bf16[768,512]{1,0:T(8,128)(2,1)S(1)}, bf16[768,512]{1,0:T(8,128)(2,1)S(1)}, u32[]{:S(2)}, u32[]{:S(2)}) %collective-permute-start.1) | collective-permute-done | bytes 786464 | tf_op jit(solution)/shard_map/ppermute | solution.py:37
  217.7 5.1 collective-permute-done.4.refs_5_
  226.8 72.9 %collective-permute-done.11.refs_14_ = bf16[4,512,640]{2,1,0:T(8,128)(2,1)S(1)} collective-permute-done((bf16[4,512,640]{2,1,0:T(8,128)(2,1)S(1)}, bf16[4,512,640]{2,1,0:T(8,128)(2,1)S(1)}, u32[]{:S(2)}, u32[]{:S(2)}) %collective-permute-start.11) | collective-permute-done | bytes 2621472 | tf_op jit(solution)/shard_map/ppermute | solution.py:37
  299.7 54.7 %collective-permute-done.12.refs_15_ = bf16[4,512,640]{2,1,0:T(8,128)(2,1)S(1)} collective-permute-done((bf16[4,512,640]{2,1,0:T(8,128)(2,1)S(1)}, bf16[4,512,640]{2,1,0:T(8,128)(2,1)S(1)}, u32[]{:S(2)}, u32[]{:S(2)}) %collective-permute-start.12) | collective-permute-done | bytes 2621472 | tf_op jit(solution)/shard_map/ppermute | solution.py:37
  360.2 6.6 pack_columns.9
  366.8 47.6 %collective-permute-done.14.refs_18_ = bf16[4,512,640]{2,1,0:T(8,128)(2,1)} collective-permute-done((bf16[4,512,640]{2,1,0:T(8,128)(2,1)}, bf16[4,512,640]{2,1,0:T(8,128)(2,1)}, u32[]{:S(2)}, u32[]{:S(2)}) %collective-permute-start.14) | collective-permute-done | bytes 2621472 | tf_op jit(solution)/shard_map/ppermute | solution.py:37
  414.5 56.2 %collective-permute-done.15.refs_19_ = bf16[4,512,640]{2,1,0:T(8,128)(2,1)} collective-permute-done((bf16[4,512,640]{2,1,0:T(8,128)(2,1)}, bf16[4,512,640]{2,1,0:T(8,128)(2,1)}, u32[]{:S(2)}, u32[]{:S(2)}) %collective-permute-start.15) | collective-permute-done | bytes 2621472 | tf_op jit(solution)/shard_map/ppermute | solution.py:37
  472.3 58.6 %reduce_head.3 = (bf16[256,2048]{1,0:T(8,128)(2,1)}, f32[2000,256]{1,0:T(8,128)}, f32[2000,256]{1,0:T(8,128)}) custom-call(bf16[768,512]{1,0:T(8,128)(2,1)} %copy-done.20, bf16[768,512]{1,0:T(8,128)(2,1)} %collective-permute-done.refs_1_, bf16[768,512]{1,0:T(8,128)(2,1)} %copy-done.21, bf16[768,512]{1,0:T(8,128)(2,1)} %copy-done.24, ...), custom_call_target="tpu_custom_call" | custom-call | flops 60000002048 | bytes 100000000 | tf_op jit(solution)/shard_map/reduce_head/pallas_call | solution.py:275
  531.3 91.6 %reduce_head.4 = (bf16[256,2048]{1,0:T(8,128)(2,1)}, f32[2000,256]{1,0:T(8,128)}, f32[2000,256]{1,0:T(8,128)}) custom-call(bf16[768,512]{1,0:T(8,128)(2,1)} %copy-done.20, bf16[768,512]{1,0:T(8,128)(2,1)} %collective-permute-done.refs_1_, bf16[768,512]{1,0:T(8,128)(2,1)} %copy-done.21, bf16[768,512]{1,0:T(8,128)(2,1)} %copy-done.24, ...), custom_call_target="tpu_custom_call" | custom-call | flops 60000002048 | bytes 100000000 | tf_op jit(solution)/shard_map/reduce_head/pallas_call | solution.py:275
  627.6 84.7 %reduce_head.5 = (bf16[256,2048]{1,0:T(8,128)(2,1)}, f32[2000,256]{1,0:T(8,128)}, f32[2000,256]{1,0:T(8,128)}) custom-call(bf16[768,512]{1,0:T(8,128)(2,1)} %copy-done.20, bf16[768,512]{1,0:T(8,128)(2,1)} %collective-permute-done.refs_1_, bf16[768,512]{1,0:T(8,128)(2,1)} %copy-done.21, bf16[768,512]{1,0:T(8,128)(2,1)} %copy-done.24, ...), custom_call_target="tpu_custom_call" | custom-call | flops 60000002048 | bytes 100000000 | tf_op jit(solution)/shard_map/reduce_head/pallas_call | solution.py:275
  712.4 6.0 maximum_bitcast_fusion.1
  720.0 15.9 %place_parts.3.refs_1_ = bf16[768,32000]{1,0:T(8,128)(2,1)} custom-call(bf16[16,256,2048]{2,1,0:T(8,128)(2,1)} %bitcast.205), custom_call_target="tpu_custom_call" | custom-call | flops 131072000 | bytes 32768000 | tf_op jit(solution)/shard_map/place_parts/pallas_call | solution.py:327
  735.9 5.3 maximum_bitcast_fusion
  741.2 17.9 %all-gather.7.cloned.1.call-done = bf16[5120,2048]{1,0:T(8,128)(2,1)} async-done(((bf16[320,2048]{1,0:T(8,128)(2,1)}), bf16[5120,2048]{1,0:T(8,128)(2,1)}) %all-gather.7.cloned.1.call-update) | async-done | bytes 20971536 | tf_op jit(solution)/shard_map/all_gather | solution.py:452
  767.2 15.3 %place_parts.4.refs_1_ = bf16[768,32000]{1,0:T(8,128)(2,1)} custom-call(bf16[16,320,2048]{2,1,0:T(8,128)(2,1)} %bitcast.201, bf16[768,32000]{1,0:T(8,128)(2,1)} %place_parts.3.refs_1_), custom_call_target="tpu_custom_call", output_to_operand_aliasing={{}: (1, {})} | custom-call | flops 131072000 | bytes 32768000 | tf_op jit(solution)/shard_map/place_parts/pallas_call | solution.py:327
  782.5 13.7 %back_project.1 = (bf16[2,768,2048]{2,1,0:T(8,128)(2,1)}, bf16[2,2048,768]{2,1,0:T(8,128)(2,1)}) custom-call(bf16[16,4,256,128]{3,2,1,0:T(8,128)(2,1)} %bitcast.198, bf16[16,4,256,128]{3,2,1,0:T(8,128)(2,1)} %bitcast.199, bf16[2,768,2048]{2,1,0:T(8,128)(2,1)} %w_up_ref.1, bf16[2,2048,768]{2,1,0:T(8,128)(2,1)} %w_down_ref.1, bf16[2,768,256]{2,1,0:T(8,128)(2,1)} %p_ref.1, ...), custom_call_target="tpu_custom_call" | custom-call | flops 3221225472 | bytes 30000000 | tf_op jit(solution)/shard_map/back_project/pallas_call | solution.py:356
  796.2 41.5 %all-gather.9.cloned.1.call-done = bf16[4096,2048]{1,0:T(8,128)(2,1)} async-done(((bf16[256,2048]{1,0:T(8,128)(2,1)}), bf16[4096,2048]{1,0:T(8,128)(2,1)}) %all-gather.9.cloned.1.call-update) | async-done | bytes 16777232 | tf_op jit(solution)/shard_map/all_gather | solution.py:452
  837.7 15.0 %place_parts.5 = bf16[768,32000]{1,0:T(8,128)(2,1)} custom-call(bf16[16,256,2048]{2,1,0:T(8,128)(2,1)} %bitcast.202, bf16[768,32000]{1,0:T(8,128)(2,1)} %place_parts.4.refs_1_), custom_call_target="tpu_custom_call", output_to_operand_aliasing={{}: (1, {})} | custom-call | flops 131072000 | bytes 32768000 | tf_op jit(solution)/shard_map/place_parts/pallas_call | solution.py:327
  (165 shorter events, 48.6 us)
Async XLA Ops:
  7.2 615.7 %reduce-scatter.2.cloned.1.call-start = ((), (), s32[]{:S(2)}) async-start(), calls=%async_computation.1 | async-start | bytes 8912896 | tf_op jit(solution)/shard_map/reduce_scatter | solution.py:433
  159.6 560.4 %all-gather.11.cloned.1.call-start = ((), (), s32[]{:S(2)}) async-start(), calls=%async_computation.4 | async-start | bytes 17825792 | tf_op jit(solution)/shard_map/all_gather | solution.py:452
  174.9 180.8 %copy-start.20 = (bf16[768,512]{1,0:T(8,128)(2,1)}, bf16[768,512]{1,0:T(8,128)(2,1)S(1)}, u32[]{:S(2)}) copy-start(bf16[768,512]{1,0:T(8,128)(2,1)S(1)} %fusion.57.refs_0_) | copy-start | bytes 2359300
  174.9 38.3 %collective-permute-start.1 = (bf16[768,512]{1,0:T(8,128)(2,1)S(1)}, bf16[768,512]{1,0:T(8,128)(2,1)S(1)}, u32[]{:S(2)}, u32[]{:S(2)}) collective-permute-start(bf16[768,512]{1,0:T(8,128)(2,1)S(1)} %fusion.57.refs_0_), channel_id=1, source_target_pairs={{0,2},{1,3},{2,0},{3,1},{4,6},{5,7},{6,4},{7,5},{8,10},{9,11},{10,... | collective-permute-start | bytes 2359304 | tf_op jit(solution)/shard_map/ppermute | solution.py:37
  178.2 37.1 %collective-permute-start.3 = (bf16[768,512]{1,0:T(8,128)(2,1)S(1)}, bf16[768,512]{1,0:T(8,128)(2,1)S(1)}, u32[]{:S(2)}, u32[]{:S(2)}) collective-permute-start(bf16[768,512]{1,0:T(8,128)(2,1)S(1)} %fusion.57.refs_0_), channel_id=1, source_target_pairs={{0,4},{1,5},{2,6},{3,7},{4,0},{5,1},{6,2},{7,3},{8,12},{9,13},{10,... | collective-permute-start | bytes 2359304 | tf_op jit(solution)/shard_map/ppermute | solution.py:37
  179.7 35.6 %collective-permute-start.5 = (bf16[768,512]{1,0:T(8,128)(2,1)S(1)}, bf16[768,512]{1,0:T(8,128)(2,1)S(1)}, u32[]{:S(2)}, u32[]{:S(2)}) collective-permute-start(bf16[768,512]{1,0:T(8,128)(2,1)S(1)} %fusion.57.refs_0_), channel_id=1, source_target_pairs={{0,8},{1,9},{2,10},{3,11},{4,12},{5,13},{6,14},{7,15},{8,0},{9,1},... | collective-permute-start | bytes 2359304 | tf_op jit(solution)/shard_map/ppermute | solution.py:37
  181.3 34.2 %collective-permute-start = (bf16[768,512]{1,0:T(8,128)(2,1)S(1)}, bf16[768,512]{1,0:T(8,128)(2,1)}, u32[]{:S(2)}, u32[]{:S(2)}) collective-permute-start(bf16[768,512]{1,0:T(8,128)(2,1)S(1)} %fusion.57.refs_0_), channel_id=1, source_target_pairs={{0,1},{1,0},{2,3},{3,2},{4,5},{5,4},{6,7},{7,6},{8,9},{9,8},{10,11... | collective-permute-start | bytes 2359304 | tf_op jit(solution)/shard_map/ppermute | solution.py:37
  181.3 44.1 %collective-permute-start.10 = (bf16[4,512,640]{2,1,0:T(8,128)(2,1)S(1)}, bf16[4,512,640]{2,1,0:T(8,128)(2,1)}, u32[]{:S(2)}, u32[]{:S(2)}) collective-permute-start(bf16[4,512,640]{2,1,0:T(8,128)(2,1)S(1)} %copy-done.16), channel_id=1, source_target_pairs={{0,1},{1,0},{2,3},{3,2},{4,5},{5,4},{6,7},{7,6},{8,9},{9,8},{10,11... | collective-permute-start | bytes 7864328 | tf_op jit(solution)/shard_map/ppermute | solution.py:37
  213.2 142.5 %copy-start.21 = (bf16[768,512]{1,0:T(8,128)(2,1)}, bf16[768,512]{1,0:T(8,128)(2,1)S(1)}, u32[]{:S(2)}) copy-start(bf16[768,512]{1,0:T(8,128)(2,1)S(1)} %collective-permute-done.1.refs_2_) | copy-start | bytes 2359300
  213.2 86.5 %collective-permute-start.11 = (bf16[4,512,640]{2,1,0:T(8,128)(2,1)S(1)}, bf16[4,512,640]{2,1,0:T(8,128)(2,1)S(1)}, u32[]{:S(2)}, u32[]{:S(2)}) collective-permute-start(bf16[4,512,640]{2,1,0:T(8,128)(2,1)S(1)} %copy-done.18), channel_id=1, source_target_pairs={{0,4},{1,5},{2,6},{3,7},{4,0},{5,1},{6,2},{7,3},{8,12},{9,13},{10,... | collective-permute-start | bytes 7864328 | tf_op jit(solution)/shard_map/ppermute | solution.py:37
  215.2 140.5 %copy-start.22 = (bf16[768,512]{1,0:T(8,128)(2,1)}, bf16[768,512]{1,0:T(8,128)(2,1)S(1)}, u32[]{:S(2)}) copy-start(bf16[768,512]{1,0:T(8,128)(2,1)S(1)} %collective-permute-done.3.refs_4_) | copy-start | bytes 2359300
  215.2 2.3 collective-permute-start.2
  215.3 140.4 %copy-start.23 = (bf16[768,512]{1,0:T(8,128)(2,1)}, bf16[768,512]{1,0:T(8,128)(2,1)S(1)}, u32[]{:S(2)}) copy-start(bf16[768,512]{1,0:T(8,128)(2,1)S(1)} %collective-permute-done.5.refs_6_) | copy-start | bytes 2359300
  215.3 139.1 %collective-permute-start.12 = (bf16[4,512,640]{2,1,0:T(8,128)(2,1)S(1)}, bf16[4,512,640]{2,1,0:T(8,128)(2,1)S(1)}, u32[]{:S(2)}, u32[]{:S(2)}) collective-permute-start(bf16[4,512,640]{2,1,0:T(8,128)(2,1)S(1)} %copy-done.19), channel_id=1, source_target_pairs={{0,5},{1,4},{2,7},{3,6},{4,1},{5,0},{6,3},{7,2},{8,13},{9,12},{10,... | collective-permute-start | bytes 7864328 | tf_op jit(solution)/shard_map/ppermute | solution.py:37
  215.5 140.2 %collective-permute-start.13 = (bf16[4,512,640]{2,1,0:T(8,128)(2,1)S(1)}, bf16[4,512,640]{2,1,0:T(8,128)(2,1)S(1)}, u32[]{:S(2)}, u32[]{:S(2)}) collective-permute-start(bf16[4,512,640]{2,1,0:T(8,128)(2,1)S(1)} %copy-done.13), channel_id=1, source_target_pairs={{0,1},{1,0},{2,3},{3,2},{4,5},{5,4},{6,7},{7,6},{8,9},{9,8},{10,11... | collective-permute-start | bytes 7864328 | tf_op jit(solution)/shard_map/ppermute | solution.py:37
  217.6 138.1 %copy-start.24 = (bf16[768,512]{1,0:T(8,128)(2,1)}, bf16[768,512]{1,0:T(8,128)(2,1)S(1)}, u32[]{:S(2)}) copy-start(bf16[768,512]{1,0:T(8,128)(2,1)S(1)} %collective-permute-done.2.refs_3_) | copy-start | bytes 2359300
  217.6 5.2 collective-permute-start.4
  222.8 132.9 %copy-start.25 = (bf16[768,512]{1,0:T(8,128)(2,1)}, bf16[768,512]{1,0:T(8,128)(2,1)S(1)}, u32[]{:S(2)}) copy-start(bf16[768,512]{1,0:T(8,128)(2,1)S(1)} %collective-permute-done.4.refs_5_) | copy-start | bytes 2359300
  222.8 2.4 collective-permute-start.6
  225.2 130.5 %copy-start.26 = (bf16[768,512]{1,0:T(8,128)(2,1)}, bf16[768,512]{1,0:T(8,128)(2,1)S(1)}, u32[]{:S(2)}) copy-start(bf16[768,512]{1,0:T(8,128)(2,1)S(1)} %collective-permute-done.6.refs_7_) | copy-start | bytes 2359300
  225.2 245.4 %collective-permute-start.7 = (bf16[4,512,768]{2,1,0:T(8,128)(2,1)}, bf16[4,512,768]{2,1,0:T(8,128)(2,1)S(1)}, u32[]{:S(2)}, u32[]{:S(2)}) collective-permute-start(bf16[4,512,768]{2,1,0:T(8,128)(2,1)} %get-tuple-element.49), channel_id=1, source_target_pairs={{0,1},{1,0},{2,3},{3,2},{4,5},{5,4},{6,7},{7,6},{8,9},{9,8},{10,11... | collective-permute-start | bytes 9437192 | tf_op jit(solution)/shard_map/ppermute | solution.py:37
  225.3 245.3 %collective-permute-start.8 = (bf16[4,512,768]{2,1,0:T(8,128)(2,1)}, bf16[4,512,768]{2,1,0:T(8,128)(2,1)}, u32[]{:S(2)}, u32[]{:S(2)}) collective-permute-start(bf16[4,512,768]{2,1,0:T(8,128)(2,1)} %get-tuple-element.50), channel_id=1, source_target_pairs={{0,8},{1,9},{2,10},{3,11},{4,12},{5,13},{6,14},{7,15},{8,0},{9,1},... | collective-permute-start | bytes 9437192 | tf_op jit(solution)/shard_map/ppermute | solution.py:37
  299.7 170.9 %collective-permute-start.9 = (bf16[4,512,768]{2,1,0:T(8,128)(2,1)}, bf16[4,512,768]{2,1,0:T(8,128)(2,1)}, u32[]{:S(2)}, u32[]{:S(2)}) collective-permute-start(bf16[4,512,768]{2,1,0:T(8,128)(2,1)} %get-tuple-element.51), channel_id=1, source_target_pairs={{0,9},{1,8},{2,11},{3,10},{4,13},{5,12},{6,15},{7,14},{8,1},{9,0},... | collective-permute-start | bytes 9437192 | tf_op jit(solution)/shard_map/ppermute | solution.py:37
  354.4 60.1 %collective-permute-start.14 = (bf16[4,512,640]{2,1,0:T(8,128)(2,1)}, bf16[4,512,640]{2,1,0:T(8,128)(2,1)}, u32[]{:S(2)}, u32[]{:S(2)}) collective-permute-start(bf16[4,512,640]{2,1,0:T(8,128)(2,1)} %get-tuple-element.58), channel_id=1, source_target_pairs={{0,2},{1,3},{2,0},{3,1},{4,6},{5,7},{6,4},{7,5},{8,10},{9,11},{10,... | collective-permute-start | bytes 7864328 | tf_op jit(solution)/shard_map/ppermute | solution.py:37
  357.5 113.1 %collective-permute-start.15 = (bf16[4,512,640]{2,1,0:T(8,128)(2,1)}, bf16[4,512,640]{2,1,0:T(8,128)(2,1)}, u32[]{:S(2)}, u32[]{:S(2)}) collective-permute-start(bf16[4,512,640]{2,1,0:T(8,128)(2,1)} %get-tuple-element.59), channel_id=1, source_target_pairs={{0,3},{1,2},{2,1},{3,0},{4,7},{5,6},{6,5},{7,4},{8,11},{9,10},{10,... | collective-permute-start | bytes 7864328 | tf_op jit(solution)/shard_map/ppermute | solution.py:37
  472.3 58.7 %copy-start.6 = (f32[2,128,256]{2,1,0:T(8,128)S(1)}, f32[2,128,256]{2,1,0:T(8,128)}, u32[]{:S(2)}) copy-start(f32[2,128,256]{2,1,0:T(8,128)} %param.34) | copy-start | bytes 786436
  472.3 58.8 %copy-start.7 = (f32[2,128,256]{2,1,0:T(8,128)S(1)}, f32[2,128,256]{2,1,0:T(8,128)}, u32[]{:S(2)}) copy-start(f32[2,128,256]{2,1,0:T(8,128)} %param.35) | copy-start | bytes 786436
  530.9 228.2 %all-gather.7.cloned.1.call-start = ((), (), s32[]{:S(2)}) async-start(), calls=%async_computation.2 | async-start | bytes 22282240 | tf_op jit(solution)/shard_map/all_gather | solution.py:452
  531.3 92.9 %copy-start.8 = (f32[2,256,128]{2,1,0:T(8,128)S(1)}, f32[2,256,128]{2,1,0:T(8,128)}, u32[]{:S(2)}) copy-start(f32[2,256,128]{2,1,0:T(8,128)} %param.32) | copy-start | bytes 786436
  531.3 92.9 %copy-start.9 = (f32[2,256,128]{2,1,0:T(8,128)S(1)}, f32[2,256,128]{2,1,0:T(8,128)}, u32[]{:S(2)}) copy-start(f32[2,256,128]{2,1,0:T(8,128)} %param.33) | copy-start | bytes 786436
  627.3 85.0 %copy-start.3 = (f32[2000,256]{1,0:T(8,128)S(1)}, f32[2000,256]{1,0:T(8,128)}, u32[]{:S(2)}) copy-start(f32[2000,256]{1,0:T(8,128)} %get-tuple-element.84) | copy-start | bytes 6144004
  627.3 210.4 %all-gather.9.cloned.1.call-start = ((), (), s32[]{:S(2)}) async-start(), calls=%async_computation.3 | async-start | bytes 17825792 | tf_op jit(solution)/shard_map/all_gather | solution.py:452
  (22 other events, 315.6 us)
Sparse Core Ops, SparseCore 0:
  159.7 112.5 reduce-scatter.1
  531.0 113.0 all-gather.10
  646.9 112.1 all-gather.6
  761.3 76.4 all-gather.8

commit v2 on v1

--- a/solution.py
+++ b/solution.py
@@ -19,7 +19,10 @@
 CORE, X, Y, Z = 1, 2, 4, 8
 GROUP_BITS = ((Z, Y, X), (Y, X, Z), (X, Z, Y))
 GROUP_TILES = (6, 5, 5)
-ROW_CHUNK = 256
+TERM_BITS = ((X, Y, Z), (Y, Z, X), (Z, X, Y), (Z, Y, X))
+LOW_STEPS = 2
+PACKS = (((0, 2),), ((1, 2), (2, 2)), ((0, 3), (1, 3), (2, 3)), ((0, 1), (1, 1), (2, 1)), ((0, 0), (1, 0), (2, 0)))
+ROW_CHUNKS = (256, 256, 256)
 
 
 def gelu_tanh(values):
@@ -37,11 +40,32 @@
     return lax.ppermute(values, DATA_AXIS, [(i, i ^ mask) for i in range(DEVICES)])
 
 
+def partner_mask(group, partner):
+    bit = GROUP_BITS[group][0]
+    return (0, CORE, bit, bit | CORE)[partner]
+
+
 def group_offsets():
     offsets = [0]
     for tiles in GROUP_TILES:
         offsets.append(offsets[-1] + tiles * LANES)
     return offsets
+
+
+def shift_left(ref, rows, first, tiles, shift, lane):
+    last = ref.shape[1] // LANES - 1
+
+    def rolled(index):
+        at = pl.multiple_of(jnp.minimum(first + index, last) * LANES, LANES)
+        return pltpu.roll(ref[rows, pl.ds(at, LANES)], (LANES - shift) % LANES, 1)
+
+    pieces = []
+    left = rolled(0)
+    for index in range(tiles):
+        right = rolled(index + 1)
+        pieces.append(jnp.where(lane < LANES - shift, left, right))
+        left = right
+    return pieces
 
 
 def pack_columns(values, jobs, shard_cols):
@@ -67,23 +91,31 @@
             target = lax.broadcasted_iota(jnp.int32, (depth, cols), 1)
             return jnp.where(source == target + by, 1.0, 0.0).astype(jnp.bfloat16)
 
+        plans = []
         for j, (_, _, width) in enumerate(jobs):
-            in_ref, out_ref = refs[j], refs[len(jobs) + j]
             first, shift = table_ref[j, 1, entry], table_ref[j, 2, entry]
             tail = width % (2 * LANES) or 2 * LANES
-            inner = selector(3 * LANES, 2 * LANES, shift)
-            outer = selector(tail + LANES, tail, shift + first * LANES)
-
-            def step(i, carry):
-                sl = pl.ds(pl.multiple_of(i * row_block, row_block), row_block)
+            by_roll = len(jobs) > 2 and j == len(jobs) - 1
+            selectors = None if by_roll else (selector(3 * LANES, 2 * LANES, shift), selector(tail + LANES, tail, shift + first * LANES))
+            plans.append((refs[j], refs[len(jobs) + j], width, tail, first, shift, selectors))
+        lane = lax.broadcasted_iota(jnp.int32, (row_block, LANES), 1)
+
+        def step(i, carry):
+            sl = pl.ds(pl.multiple_of(i * row_block, row_block), row_block)
+            for in_ref, out_ref, width, tail, first, shift, selectors in plans:
+                if selectors is None:
+                    for t, piece in enumerate(shift_left(in_ref, sl, first, width // LANES, shift, lane)):
+                        out_ref[0, sl, t * LANES:(t + 1) * LANES] = piece
+                    continue
+                inner, outer = selectors
                 for at in range(0, width - tail, 2 * LANES):
                     source = in_ref[sl, pl.ds(pl.multiple_of(first * LANES + at, LANES), 3 * LANES)]
                     out_ref[0, sl, at:at + 2 * LANES] = jnp.dot(source, inner, preferred_element_type=jnp.float32).astype(jnp.bfloat16)
                 at = width - tail
                 out_ref[0, sl, at:] = jnp.dot(in_ref[sl, at:], outer, preferred_element_type=jnp.float32).astype(jnp.bfloat16)
-                return carry
-
-            lax.fori_loop(0, rows // row_block, step, 0)
+            return carry
+
+        lax.fori_loop(0, rows // row_block, step, 0)
 
     moved = sum(count * rows * width for _, _, width in jobs)
     return pl.pallas_call(
@@ -95,15 +127,18 @@
     )(jnp.stack(tables), *[values] * len(jobs))
 
 
-def project_gradients(terms, owners):
+def project_gradients(terms, owners, me):
     count = len(terms)
     model, rank = terms[0][0].shape
     tokens, hidden = terms[0][2].shape
     cols = hidden // owners
-    step_owners = 4
+    step_owners = 8
     block = step_owners * cols
 
-    def body(*refs):
+    rel = jnp.arange(owners, dtype=jnp.int32) ^ me
+    table = jnp.stack([sum(jnp.where(rel & bit, owners >> (k + 1), 0) for k, bit in enumerate((CORE, *bits))) for bits in TERM_BITS])
+
+    def body(table_ref, *refs):
         out_ref, turned = refs[-2], refs[-1]
         for m in range(count):
             p_ref, h_ref, e_ref = refs[3 * m:3 * m + 3]
@@ -120,28 +155,34 @@
                 left = p_ref[...]
                 total = jnp.dot(left, high, preferred_element_type=jnp.float32) + jnp.dot(left, low, preferred_element_type=jnp.float32)
                 for k in range(step_owners):
-                    out_ref[k, 0] = total[:, k * cols:(k + 1) * cols]
+                    out_ref[0, table_ref[m, pl.program_id(1) * step_owners + k]] = total[:, k * cols:(k + 1) * cols]
 
     in_specs, operands = [], []
     for m, (p, h, e) in enumerate(terms):
-        in_specs += [pl.BlockSpec((rank, model), lambda t, c: (0, 0)), pl.BlockSpec((tokens, model), lambda t, c: (0, 0)),
-                     pl.BlockSpec((tokens, block), lambda t, c, m=m: (0, jnp.where(t == m, c, jnp.where(t < m, 0, hidden // block - 1))))]
+        in_specs += [pl.BlockSpec((rank, model), lambda t, c, _: (0, 0)), pl.BlockSpec((tokens, model), lambda t, c, _: (0, 0)),
+                     pl.BlockSpec((tokens, block), lambda t, c, _, m=m: (0, jnp.where(t == m, c, jnp.where(t < m, 0, hidden // block - 1))))]
         operands += [p.T, h, e]
     return pl.pallas_call(
         body,
-        grid=(count, hidden // block),
-        in_specs=in_specs,
-        out_specs=pl.BlockSpec((step_owners, 1, rank, cols), lambda t, c: (c, t, 0, 0)),
-        out_shape=jax.ShapeDtypeStruct((owners, count, rank, cols), jnp.float32),
-        scratch_shapes=[pltpu.VMEM((model, tokens), jnp.bfloat16)],
+        grid_spec=pltpu.PrefetchScalarGridSpec(
+            num_scalar_prefetch=1,
+            grid=(count, hidden // block),
+            in_specs=in_specs,
+            out_specs=pl.BlockSpec((1, owners, rank, cols), lambda t, c, _: (t, 0, 0, 0)),
+            scratch_shapes=[pltpu.VMEM((model, tokens), jnp.bfloat16)],
+        ),
+        out_shape=jax.ShapeDtypeStruct((count, owners, rank, cols), jnp.float32),
         cost_estimate=pl.CostEstimate(flops=count * 2 * model * hidden * (tokens + 2 * rank), bytes_accessed=count * hidden * (tokens * 2 + rank * 4), transcendentals=0),
         name='project_gradients',
-    )(*operands)
-
-
-def reduce_head(near, packed, w_own, mom_out, var_out, chunk):
+    )(table, *operands)
+
+
+def reduce_head(near, packed, w_out, mom_out, var_out, chunk, low=None):
     groups = len(GROUP_BITS)
     offsets = group_offsets()
+    row_chunk = ROW_CHUNKS[chunk]
+    places = 0 if low is None else low.shape[1]
+    last_tile = (w_out.shape[1] - offsets[-1] - LANES) // LANES
     shard_cols = mom_out.shape[0]
     owners, tokens, _ = packed[0][0].shape
     widths = [offsets[g + 1] - offsets[g] for g in range(groups)]
@@ -151,10 +192,16 @@
     def body(*refs):
         near_refs = dict(zip(near_keys, refs))
         refs = refs[len(near_keys):]
+        if low is not None:
+            low_ref, refs = refs[0], refs[1:]
         packed_refs = [refs[4 * g:4 * g + 4] for g in range(groups)]
         refs = refs[4 * groups:]
         w_ref, mom_ref, var_ref, w_out_ref, mom_out_ref, var_out_ref = refs[:6]
         refs = refs[6:]
+        if low is not None:
+            low_out_ref, low_buf, *low_got, low_load, low_send, low_recv = refs[:5 + LOW_STEPS]
+            refs = refs[5 + LOW_STEPS:]
+        near_buf, near_sem, w_window, *refs = refs
         blocks, refs = refs[:groups], refs[groups:]
         part, refs = refs[:groups], refs[groups:]
         got, refs = refs[:groups], refs[groups:]
@@ -162,7 +209,8 @@
         w_buf, mom_buf, var_buf, mom_turned, var_turned, load_sem, first_send, first_recv, second_send, second_recv, state_sem = refs
         me = lax.axis_index(DATA_AXIS)
         barrier = pltpu.get_barrier_semaphore()
-        for bit in (X, Y, Z):
+        greeted = (X, Y, Z, CORE) if low is not None and chunk == 0 else (X, Y, Z)
+        for bit in greeted:
             pl.semaphore_signal(barrier, inc=1, device_id=(me ^ bit,), device_id_type=pl.DeviceIdType.MESH)
 
         def load(g, entry):
@@ -171,14 +219,49 @@
         for g in range(groups):
             for copy in load(g, 3):
                 copy.start()
-        rows = pl.ds(chunk * ROW_CHUNK, ROW_CHUNK)
+        rows = pl.ds(sum(ROW_CHUNKS[:chunk]), row_chunk)
         valid = pl.ds(0, shard_cols)
-        state = [pltpu.make_async_copy(w_ref.at[rows], w_buf, state_sem.at[0]),
+        own_tile = (me * shard_cols) // LANES
+        base_tile = jnp.minimum(own_tile, last_tile)
+        window = pl.ds(pl.multiple_of(base_tile * LANES, LANES), offsets[-1] + LANES)
+        state = [pltpu.make_async_copy(w_ref.at[rows, window], w_window, state_sem.at[0]),
                  pltpu.make_async_copy(mom_ref.at[:, rows], mom_turned.at[valid], state_sem.at[1]),
                  pltpu.make_async_copy(var_ref.at[:, rows], var_turned.at[valid], state_sem.at[2])]
+        near_loads = [pltpu.make_async_copy(near_refs[masks[g][k]].at[rows], near_buf.at[g, k], near_sem.at[g, k]) for g in range(groups) for k in range(4)]
+        for copy in near_loads:
+            copy.start()
         for copy in state:
             copy.start()
-        pl.semaphore_wait(barrier, 3)
+        pl.semaphore_wait(barrier, len(greeted))
+
+        def low_copy(at, term):
+            half = places >> (at + 1)
+            source = low_ref if at == 0 else low_buf
+            return pltpu.make_async_remote_copy(
+                src_ref=source.at[term, pl.ds(half, half)], dst_ref=low_got[at].at[term], send_sem=low_send.at[at, term], recv_sem=low_recv.at[at, term],
+                device_id=(me ^ (CORE, *TERM_BITS[term])[chunk * LOW_STEPS + at],), device_id_type=pl.DeviceIdType.MESH)
+
+        def low_step(at):
+            half = places >> (at + 1)
+            for term in range(len(TERM_BITS)):
+                low_copy(at, term).wait_recv()
+
+                def add(e, carry):
+                    low_buf[term, e] = low_buf[term, e] + low_got[at][term, e]
+                    return carry
+
+                lax.fori_loop(0, half, add, 0)
+                if at + 1 < LOW_STEPS:
+                    low_copy(at + 1, term).start()
+
+        if low is not None:
+            keep = pl.ds(0, places // 2)
+            low_loads = [pltpu.make_async_copy(low_ref.at[term, keep], low_buf.at[term], low_load.at[term]) for term in range(len(TERM_BITS))]
+            for term, copy in enumerate(low_loads):
+                low_copy(0, term).start()
+                copy.start()
+        for copy in near_loads:
+            copy.wait()
 
         def first_copy(g, entry):
             return pltpu.make_async_remote_copy(
@@ -192,14 +275,30 @@
 
         def step(i, carry):
             entry = 3 - i
+            if low is not None:
+                @pl.when(i == 1)
+                def _():
+                    for copy in low_loads:
+                        copy.wait()
+                    low_step(0)
             for g in range(groups):
                 for copy in load(g, entry):
                     copy.wait()
-                acc = None
-                for k in range(4):
-                    term = jnp.dot(near_refs[masks[g][k]][...], blocks[g][k], preferred_element_type=jnp.float32)
-                    acc = term if acc is None else acc + term
-                part[g][entry] = acc
+
+                def accumulate(k, carry):
+                    term = jnp.dot(near_buf[g, k], blocks[g][k], preferred_element_type=jnp.float32)
+
+                    @pl.when(k == 0)
+                    def _():
+                        part[g][entry] = term
+
+                    @pl.when(k > 0)
+                    def _():
+                        part[g][entry] = part[g][entry] + term
+
+                    return carry
+
+                lax.fori_loop(0, 4, accumulate, 0)
 
                 @pl.when(i < 3)
                 def _():
@@ -225,6 +324,15 @@
 
         for copy in state:
             copy.wait()
+        lane = lax.broadcasted_iota(jnp.int32, (64, LANES), 1)
+
+        def align(i, carry):
+            sl = pl.ds(pl.multiple_of(i * 64, 64), 64)
+            for t, piece in enumerate(shift_left(w_window, sl, own_tile - base_tile, offsets[-1] // LANES, (me * shard_cols) % LANES, lane)):
+                w_buf[sl, t * LANES:(t + 1) * LANES] = piece
+            return carry
+
+        lax.fori_loop(0, row_chunk // 64, align, 0)
         for at in range(0, offsets[-1], LANES):
             cols = slice(at, at + LANES)
             mom_buf[:, cols] = mom_turned[cols].T
@@ -232,6 +340,7 @@
         block = 32
         for g in range(groups):
             first_copy(g, 2).wait_recv()
+        for g in range(groups):
             second_copy(g).wait_recv()
             cols = slice(offsets[g], offsets[g + 1])
 
@@ -244,7 +353,7 @@
                 w_buf[sl, cols] = (w_buf[sl, cols].astype(jnp.float32) - LR_HEAD * direction).astype(jnp.bfloat16)
                 return carry
 
-            lax.fori_loop(0, ROW_CHUNK // block, adam, 0)
+            lax.fori_loop(0, row_chunk // block, adam, 0)
         results = [pltpu.make_async_copy(w_buf, w_out_ref, state_sem.at[0]),
                    pltpu.make_async_copy(mom_turned.at[valid], mom_out_ref, state_sem.at[1]),
                    pltpu.make_async_copy(var_turned.at[valid], var_out_ref, state_sem.at[2])]
@@ -255,6 +364,14 @@
             var_turned[cols] = var_buf[:, cols].T
         results[1].start()
         results[2].start()
+        if low is not None:
+            low_step(1)
+            results += [pltpu.make_async_copy(low_buf.at[term, pl.ds(0, places >> LOW_STEPS)], low_out_ref.at[term], low_load.at[term]) for term in range(len(TERM_BITS))]
+            for copy in results[3:]:
+                copy.start()
+            for at in range(LOW_STEPS):
+                for term in range(len(TERM_BITS)):
+                    low_copy(at, term).wait_send()
         for g in range(groups):
             first_copy(g, 3).wait_send()
             first_copy(g, 2).wait_send()
@@ -263,29 +380,36 @@
             copy.wait()
 
     anywhere = pl.BlockSpec(memory_space=pl.ANY)
-    near_spec = pl.BlockSpec((ROW_CHUNK, tokens), lambda s: (chunk, 0))
-    scratch = [pltpu.VMEM((4, tokens, w), jnp.bfloat16) for w in widths]
-    scratch += [pltpu.VMEM((owners, ROW_CHUNK, w), jnp.float32) for w in widths]
-    scratch += [pltpu.VMEM((2, ROW_CHUNK, w), jnp.float32) for w in widths]
-    scratch += [pltpu.VMEM((ROW_CHUNK, w), jnp.float32) for w in widths]
-    scratch += [pltpu.VMEM((ROW_CHUNK, offsets[-1]), jnp.bfloat16)]
-    scratch += [pltpu.VMEM((ROW_CHUNK, offsets[-1]), jnp.float32)] * 2 + [pltpu.VMEM((offsets[-1], ROW_CHUNK), jnp.float32)] * 2
+    out_shapes = [jax.ShapeDtypeStruct((row_chunk, offsets[-1]), jnp.bfloat16)] + [jax.ShapeDtypeStruct((shard_cols, row_chunk), jnp.float32)] * 2
+    scratch = []
+    if low is not None:
+        terms, _, rank, cols = low.shape
+        out_shapes.append(jax.ShapeDtypeStruct((terms, places >> LOW_STEPS, rank, cols), jnp.float32))
+        scratch.append(pltpu.VMEM((terms, places // 2, rank, cols), jnp.float32))
+        scratch += [pltpu.VMEM((terms, places >> (at + 1), rank, cols), jnp.float32) for at in range(LOW_STEPS)]
+        scratch += [pltpu.SemaphoreType.DMA((terms,)), pltpu.SemaphoreType.DMA((LOW_STEPS, terms)), pltpu.SemaphoreType.DMA((LOW_STEPS, terms))]
+    scratch += [pltpu.VMEM((groups, 4, row_chunk, tokens), jnp.bfloat16), pltpu.SemaphoreType.DMA((groups, 4)), pltpu.VMEM((row_chunk, offsets[-1] + LANES), jnp.bfloat16)]
+    scratch += [pltpu.VMEM((4, tokens, w), jnp.bfloat16) for w in widths]
+    scratch += [pltpu.VMEM((owners, row_chunk, w), jnp.float32) for w in widths]
+    scratch += [pltpu.VMEM((2, row_chunk, w), jnp.float32) for w in widths]
+    scratch += [pltpu.VMEM((row_chunk, w), jnp.float32) for w in widths]
+    scratch += [pltpu.VMEM((row_chunk, offsets[-1]), jnp.bfloat16)]
+    scratch += [pltpu.VMEM((row_chunk, offsets[-1]), jnp.float32)] * 2 + [pltpu.VMEM((offsets[-1], row_chunk), jnp.float32)] * 2
     scratch += [pltpu.SemaphoreType.DMA((groups, 4)), pltpu.SemaphoreType.DMA((groups, 2)), pltpu.SemaphoreType.DMA((groups, 2)),
                 pltpu.SemaphoreType.DMA((groups,)), pltpu.SemaphoreType.DMA((groups,)), pltpu.SemaphoreType.DMA((3,))]
     return pl.pallas_call(
         body,
-        grid=(1,),
-        in_specs=[near_spec] * len(near_keys) + [anywhere] * (4 * groups + 3),
-        out_specs=[anywhere] * 3,
-        out_shape=[jax.ShapeDtypeStruct((ROW_CHUNK, offsets[-1]), jnp.bfloat16)] + [jax.ShapeDtypeStruct((shard_cols, ROW_CHUNK), jnp.float32)] * 2,
+        in_specs=[anywhere] * (len(near_keys) + 4 * groups + 3 + (low is not None)),
+        out_specs=[anywhere] * len(out_shapes),
+        out_shape=out_shapes,
         scratch_shapes=scratch,
         cost_estimate=pl.CostEstimate(flops=60_000_000_000, bytes_accessed=100_000_000, transcendentals=0),
         compiler_params=pltpu.CompilerParams(collective_id=chunk, has_side_effects=True, vmem_limit_bytes=60 * 1024 * 1024),
         name='reduce_head',
-    )(*[near[k] for k in near_keys], *[packed[g][m] for g in range(groups) for m in masks[g]], w_own, mom_out, var_out)
-
-
-def place_parts(parts, vocab, total_rows, row_chunk, previous):
+    )(*[near[k] for k in near_keys], *([] if low is None else [low]), *[packed[g][m] for g in range(groups) for m in masks[g]], w_out, mom_out, var_out)
+
+
+def place_parts(parts, vocab, total_rows, chunk, previous):
     shard_cols = vocab // DEVICES
     rows = 32
     count = -(-shard_cols // LANES)
@@ -316,7 +440,8 @@
                 else:
                     pending = value
 
-    steps = ROW_CHUNK // rows
+    steps = ROW_CHUNKS[chunk] // rows
+    start = sum(ROW_CHUNKS[:chunk]) // rows
     in_specs = [pl.BlockSpec((DEVICES, rows, count * LANES), lambda s: (0, s, 0))]
     operands = [parts]
     aliases = {}
@@ -328,10 +453,10 @@
         body,
         grid=(steps,),
         in_specs=in_specs,
-        out_specs=pl.BlockSpec((rows, vocab), lambda s: (row_chunk * steps + s, 0)),
+        out_specs=pl.BlockSpec((rows, vocab), lambda s: (start + s, 0)),
         out_shape=jax.ShapeDtypeStruct((total_rows, vocab), jnp.bfloat16),
         input_output_aliases=aliases,
-        cost_estimate=pl.CostEstimate(flops=ROW_CHUNK * vocab * 16, bytes_accessed=ROW_CHUNK * vocab * 4, transcendentals=0),
+        cost_estimate=pl.CostEstimate(flops=ROW_CHUNKS[chunk] * vocab * 16, bytes_accessed=ROW_CHUNKS[chunk] * vocab * 4, transcendentals=0),
         name='place_parts',
     )(*operands)
 
@@ -412,14 +537,16 @@
     shard_cols = mom_out.shape[1]
     offsets = group_offsets()
     mine = {}
-    for partner in (2, 3, 1, 0):
-        jobs, masks = [], []
-        for g, (bit, first, second) in enumerate(GROUP_BITS):
-            masks.append((0, CORE, bit, bit | CORE)[partner])
-            rels = jnp.array([0, second, first, first | second], jnp.int32) ^ masks[-1]
+    for pack in PACKS:
+        jobs, keys = [], []
+        for g, partner in pack:
+            _, first, second = GROUP_BITS[g]
+            mask = partner_mask(g, partner)
+            rels = jnp.array([0, second, first, first | second], jnp.int32) ^ mask
             jobs.append((rels ^ me, offsets[g], offsets[g + 1] - offsets[g]))
-        for g, value in enumerate(pack_columns(d_logits, jobs, shard_cols)):
-            mine[g, masks[g]] = value
+            keys.append((g, mask))
+        for key, value in zip(keys, pack_columns(d_logits, jobs, shard_cols)):
+            mine[key] = value
     packed = [dict() for _ in GROUP_BITS]
     for (g, mask), value in mine.items():
         packed[g][mask] = swap(value, mask) if mask else value
@@ -428,21 +555,20 @@
     near = exchange_hidden(hidden)
     up_terms, down_terms = backward(saved_acts, d_logits, w_up, w_down, w_out)
     terms = [(proj_up[l], *up_terms[l]) for l in range(layers)] + [(proj_down[l], *down_terms[l]) for l in range(layers)]
-    low = project_gradients(terms, DEVICES)
+    low = project_gradients(terms, DEVICES, me)
     _, _, rank, cols = low.shape
-    low_scattered = lax.psum_scatter(low.reshape(-1, cols), DATA_AXIS, scatter_dimension=0, tiled=True).reshape(2 * layers, rank, cols)
-    w_own = pack_columns(w_out, [(me[None], 0, offsets[-1])], shard_cols)[0][0]
-    w_own, near, low = lax.optimization_barrier((w_own, near, low))
-    chunks = total_rows // ROW_CHUNK
+    near, low = lax.optimization_barrier((near, low))
+    chunks = len(ROW_CHUNKS)
     results = []
     gathered = []
     for chunk in range(chunks):
         if results:
-            w_own, results[-1][0] = lax.optimization_barrier((w_own, results[-1][0]))
-        results.append(list(reduce_head(near, packed, w_own, mom_out.T, var_out.T, chunk)))
+            near, results[-1][0] = lax.optimization_barrier((near, results[-1][0]))
+        results.append(list(reduce_head(near, packed, w_out, mom_out.T, var_out.T, chunk, low)))
+        low = results[-1][3] if chunk == 0 else None
         payload = results[-1][0]
         if chunk == 1:
-            low_scattered, payload = lax.optimization_barrier((low_scattered, payload))
+            low_scattered = results[1][3][:, 0]
             m_up, v_up, dir_up = adam_update(low_scattered[:layers], mom_up, var_up)
             m_down, v_down, dir_down = adam_update(low_scattered[layers:].transpose(0, 2, 1), mom_down, var_down)
             dirs = jnp.concatenate([dir_up, dir_down.transpose(0, 2, 1)], axis=0).astype(jnp.bfloat16)
@@ -454,7 +580,7 @@
     gathered[0], results[-1][1] = lax.optimization_barrier((gathered[0], results[-1][1]))
     for chunk in range(chunks):
         w_out_new = place_parts(gathered[chunk], vocab, total_rows, chunk, w_out_new)
-    dirs = gathered[1][:, ROW_CHUNK:].reshape(DEVICES, -1, side, cols).transpose(0, 2, 1, 3).reshape(DEVICES, 2 * layers, rank, cols)
+    dirs = gathered[1][:, ROW_CHUNKS[1]:].reshape(DEVICES, -1, side, cols).transpose(0, 2, 1, 3).reshape(DEVICES, 2 * layers, rank, cols)
     w_up_new, w_down_new = back_project(dirs, w_up, w_down, proj_up, proj_down)
     m_out = jnp.concatenate([r[1] for r in results], axis=1).T
     v_out = jnp.concatenate([r[2] for r in results], axis=1).T

time: 870 us -> 718 us (0.83)
  waiting for transfers between devices: 331 us -> 151 us
  Pallas kernels: 377 us -> 418 us
  starting transfers between devices: 25.3 us -> 14.1 us
    ppermute x16, waiting for transfers between devices: 272 us -> 106 us  [swap(): lax.ppermute(values, DATA_AXIS, [(i, i ^ mask) for i in range(DEVICES)])]
    pallas_call x4, Pallas kernels: 257 us -> 311 us  [the longest x3 289 us: reduce_head(): pl.pallas_call(body, in_specs=[anywhere] * (len(near_keys) + 4 * groups +...]
    all_gather x3, waiting for transfers between devices: 59.5 us -> 44.1 us  [local_step(): gathered.append(lax.all_gather(payload, DATA_AXIS, axis=0))]
    pallas_call x5, Pallas kernels: 59.3 us -> 47.4 us  [pack_columns(): pl.pallas_call(body, grid_spec=pltpu.PrefetchScalarGridSpec(num_scalar_pr...]
    all_gather x3, starting transfers between devices: 10.6 us -> 0.12 us  [local_step(): gathered.append(lax.all_gather(payload, DATA_AXIS, axis=0))]
  transfers between devices with their start and end apart: 20 -> 19, of which waited for: 10 -> 9; matrix products, arithmetic and copies ran while one was open for 4% -> 13% of each run, Pallas kernels for 33% -> 38%
where the time goes in v2:
time: 718 us; the launch traced here: 710 us
  Pallas kernels  418 us (58%)
  waiting for transfers between devices  151 us (21%)
  matrix products  69.9 us (10%)
  local copies, waits for them, and re-layouts  22.5 us (3%)
  other arithmetic  19.7 us (3%)
  between operations  14.7 us (2%)
  starting transfers between devices  14.1 us (2%)
    pallas_call x3, Pallas kernels, reduce_head(): pl.pallas_call(body, in_specs=[anywhere] * (len(near_keys) + 4 * groups +...  289 us
    ppermute x16, waiting for transfers between devices, swap(): lax.ppermute(values, DATA_AXIS, [(i, i ^ mask) for i in range(DEVICES)])  106 us
    pallas_call x5, Pallas kernels, pack_columns(): pl.pallas_call(body, grid_spec=pltpu.PrefetchScalarGridSpec(num_scalar_pr...  47.4 us
    pallas_call x3, Pallas kernels, place_parts(): pl.pallas_call(body, grid=(steps,), in_specs=in_specs, out_specs=pl.Block...  45.8 us
    all_gather x3, waiting for transfers between devices, local_step(): gathered.append(lax.all_gather(payload, DATA_AXIS, axis=0))  44.1 us
    dot_general x1, matrix products, backward(): jnp.einsum('tv,dv->td', d_logits, w_out, preferred_element_type=jnp.float32)  34.6 us
    pallas_call x1, Pallas kernels, project_gradients(): pl.pallas_call(body, grid_spec=pltpu.PrefetchScalarGridSpec(num_scalar_pr...  22.6 us
  transfers between devices with their start and end apart: 19, of which 9 were waited for; matrix products, arithmetic and copies ran while one was open for 13% of the time, Pallas kernels for 38%

profile of v2, /device:TPU:0, one launch (start us, length us, event | category | flops | bytes accessed | tf_op | source)
XLA Modules:
  0.0 709.7 jit_solution(13194485092028085621)
XLA Ops:
  8.9 10.5 %pack_columns.5 = (bf16[4,512,768]{2,1,0:T(8,128)(2,1)}, bf16[4,512,640]{2,1,0:T(8,128)(2,1)}, bf16[4,512,640]{2,1,0:T(8,128)(2,1)}) custom-call(s32[3,3,4]{2,1,0:T(4,128)} %pad_add_fusion.table_ref, bf16[512,32000]{1,0:T(8,128)(2,1)} %refs_1_.7, bf16[512,32000]{1,0:T(8,128)(2,1)} %refs_1_.7, bf16[512,32000]{1,0:T(8,128)(2,1)} %refs_1_.7), custom_call_target="tpu_custom_call" | custom-call | flops 3221225472 | bytes 16777216 | tf_op jit(solution)/shard_map/pack_columns/pallas_call | solution.py:121
  20.0 10.7 %pack_columns.6 = (bf16[4,512,768]{2,1,0:T(8,128)(2,1)}, bf16[4,512,640]{2,1,0:T(8,128)(2,1)}, bf16[4,512,640]{2,1,0:T(8,128)(2,1)}) custom-call(s32[3,3,4]{2,1,0:T(4,128)} %pad_add_fusion.1.table_ref, bf16[512,32000]{1,0:T(8,128)(2,1)} %refs_1_.7, bf16[512,32000]{1,0:T(8,128)(2,1)} %refs_1_.7, bf16[512,32000]{1,0:T(8,128)(2,1)} %refs_1_.7), custom_call_target="tpu_custom_call" | custom-call | flops 3221225472 | bytes 16777216 | tf_op jit(solution)/shard_map/pack_columns/pallas_call | solution.py:121
  31.4 10.5 %pack_columns.8 = (bf16[4,512,768]{2,1,0:T(8,128)(2,1)}, bf16[4,512,640]{2,1,0:T(8,128)(2,1)}, bf16[4,512,640]{2,1,0:T(8,128)(2,1)}) custom-call(s32[3,3,4]{2,1,0:T(4,128)} %pad_add_fusion.2.table_ref, bf16[512,32000]{1,0:T(8,128)(2,1)} %refs_1_.7, bf16[512,32000]{1,0:T(8,128)(2,1)} %refs_1_.7, bf16[512,32000]{1,0:T(8,128)(2,1)} %refs_1_.7), custom_call_target="tpu_custom_call" | custom-call | flops 3221225472 | bytes 16777216 | tf_op jit(solution)/shard_map/pack_columns/pallas_call | solution.py:121
  42.6 8.7 %pack_columns.9 = (bf16[4,512,640]{2,1,0:T(8,128)(2,1)}, bf16[4,512,640]{2,1,0:T(8,128)(2,1)}) custom-call(s32[2,3,4]{2,1,0:T(4,128)} %pad_add_fusion.3.table_ref, bf16[512,32000]{1,0:T(8,128)(2,1)} %refs_1_.7, bf16[512,32000]{1,0:T(8,128)(2,1)} %refs_1_.7), custom_call_target="tpu_custom_call" | custom-call | flops 2013265920 | bytes 10485760 | tf_op jit(solution)/shard_map/pack_columns/pallas_call | solution.py:121
  51.9 7.0 pack_columns.7
  59.2 6.1 fusion.11
  65.3 5.0 add_convert_fusion.2
  70.4 4.1 fusion.17
  74.5 2.3 fusion.57.refs_0_
  76.9 3.2 collective-permute-start.1
  83.2 14.4 %collective-permute-done.1.refs_2_ = bf16[768,512]{1,0:T(8,128)(2,1)S(1)} collective-permute-done((bf16[768,512]{1,0:T(8,128)(2,1)S(1)}, bf16[768,512]{1,0:T(8,128)(2,1)S(1)}, u32[]{:S(2)}, u32[]{:S(2)}) %collective-permute-start.1) | collective-permute-done | bytes 786464 | tf_op jit(solution)/shard_map/ppermute | solution.py:40
  102.9 34.6 %convolution_convert_fusion.refs_10_ = bf16[512,768]{1,0:T(8,128)(2,1)} fusion(bf16[512,32000]{1,0:T(8,128)(2,1)} %refs_1_.7, bf16[768,32000]{1,0:T(8,128)(2,1)} %refs_20_.1), kind=kOutput, calls=%fused_computation.59 | convolution fusion | flops 25166217216 | bytes 82706432 | tf_op jit(solution)/shard_map/tv,dv->td/dot_general | solution.py:508
  138.6 8.1 %fusion.4.refs_5_ = bf16[512,2048]{1,0:T(8,128)(2,1)} fusion(bf16[512,2048]{1,0:T(8,128)(2,1)} %copy-done.23, bf16[512,768]{1,0:T(8,128)(2,1)} %convolution_convert_fusion.refs_10_, bf16[2,2048,768]{2,1,0:T(8,128)(2,1)} %w_down_ref.1), kind=kOutput, calls=%fused_computation.16 | convolution fusion | flops 1632632832 | bytes 8126464 | tf_op jit(solution)/shard_map/td,fd->tf/dot_general | solution.py:514
  148.4 10.2 %collective-permute-done.12.refs_16_.refs_15_ = bf16[4,512,640]{2,1,0:T(8,128)(2,1)} collective-permute-done((bf16[4,512,640]{2,1,0:T(8,128)(2,1)}, bf16[4,512,640]{2,1,0:T(8,128)(2,1)}, u32[]{:S(2)}, u32[]{:S(2)}) %collective-permute-start.12) | collective-permute-done | bytes 2621472 | tf_op jit(solution)/shard_map/ppermute | solution.py:40
  172.9 4.5 add_convert_fusion.refs_7_
  177.4 5.1 fusion.7.refs_2_
  182.6 22.6 %project_gradients.1.refs_8_ = f32[4,16,256,128]{3,2,1,0:T(8,128)} custom-call(s32[4,16]{1,0:T(4,128)} %pad_add_fusion.4.table_ref, bf16[256,768]{1,0:T(8,128)(2,1)} %bitcast.217, bf16[512,768]{1,0:T(8,128)(2,1)} %refs_1_.8, bf16[512,2048]{1,0:T(8,128)(2,1)} %fusion.7.refs_2_, bf16[256,768]{1,0:T(8,128)(2,1)} %bitcast.218, bf16[512,768]{1,0:T(8,128)(2,1)} %copy.43.refs_4_, ...), custom_call_target="tpu_custom_call" | custom-call | flops 12884901888 | bytes 16777216 | tf_op jit(solution)/shard_map/project_gradients/pallas_call | solution.py:165
  205.1 24.6 %collective-permute-done.11.refs_15_.refs_14_ = bf16[4,512,640]{2,1,0:T(8,128)(2,1)} collective-permute-done((bf16[4,512,640]{2,1,0:T(8,128)(2,1)}, bf16[4,512,640]{2,1,0:T(8,128)(2,1)}, u32[]{:S(2)}, u32[]{:S(2)}) %collective-permute-start.11) | collective-permute-done | bytes 2621472 | tf_op jit(solution)/shard_map/ppermute | solution.py:40
  230.0 55.1 %collective-permute-done.8.refs_11_.refs_10_ = bf16[4,512,768]{2,1,0:T(8,128)(2,1)} collective-permute-done((bf16[4,512,768]{2,1,0:T(8,128)(2,1)S(1)}, bf16[4,512,768]{2,1,0:T(8,128)(2,1)}, u32[]{:S(2)}, u32[]{:S(2)}) %collective-permute-start.8) | collective-permute-done | bytes 3145760 | tf_op jit(solution)/shard_map/ppermute | solution.py:40
  285.1 84.5 %reduce_head.3 = (bf16[256,2048]{1,0:T(8,128)(2,1)}, f32[2000,256]{1,0:T(8,128)}, f32[2000,256]{1,0:T(8,128)}, f32[4,4,256,128]{3,2,1,0:T(8,128)}) custom-call(bf16[768,512]{1,0:T(8,128)(2,1)} %copy-done.14, bf16[768,512]{1,0:T(8,128)(2,1)} %copy-done.17, bf16[768,512]{1,0:T(8,128)(2,1)} %copy-done.15, bf16[768,512]{1,0:T(8,128)(2,1)} %copy-done.18, ...), custom_call_target="tpu_custom_call" | custom-call | flops 60000002048 | bytes 100000000 | tf_op jit(solution)/shard_map/reduce_head/pallas_call | solution.py:400
  369.9 113.8 %reduce_head.4 = (bf16[256,2048]{1,0:T(8,128)(2,1)}, f32[2000,256]{1,0:T(8,128)}, f32[2000,256]{1,0:T(8,128)}, f32[4,1,256,128]{3,2,1,0:T(8,128)}) custom-call(bf16[768,512]{1,0:T(8,128)(2,1)} %copy-done.14, bf16[768,512]{1,0:T(8,128)(2,1)} %copy-done.17, bf16[768,512]{1,0:T(8,128)(2,1)} %copy-done.15, bf16[768,512]{1,0:T(8,128)(2,1)} %copy-done.18, ...), custom_call_target="tpu_custom_call" | custom-call | flops 60000002048 | bytes 100000000 | tf_op jit(solution)/shard_map/reduce_head/pallas_call | solution.py:400
  488.2 90.5 %reduce_head.5 = (bf16[256,2048]{1,0:T(8,128)(2,1)}, f32[2000,256]{1,0:T(8,128)}, f32[2000,256]{1,0:T(8,128)}) custom-call(bf16[768,512]{1,0:T(8,128)(2,1)} %copy-done.14, bf16[768,512]{1,0:T(8,128)(2,1)} %copy-done.17, bf16[768,512]{1,0:T(8,128)(2,1)} %copy-done.15, bf16[768,512]{1,0:T(8,128)(2,1)} %copy-done.18, ...), custom_call_target="tpu_custom_call" | custom-call | flops 60000002048 | bytes 100000000 | tf_op jit(solution)/shard_map/reduce_head/pallas_call | solution.py:400
  580.5 5.4 maximum_bitcast_fusion.1
  585.9 15.4 %place_parts.3.refs_1_ = bf16[768,32000]{1,0:T(8,128)(2,1)} custom-call(bf16[16,256,2048]{2,1,0:T(8,128)(2,1)} %bitcast.207), custom_call_target="tpu_custom_call" | custom-call | flops 131072000 | bytes 32768000 | tf_op jit(solution)/shard_map/place_parts/pallas_call | solution.py:452
  601.3 5.4 maximum_bitcast_fusion
  606.7 3.0 all-gather.7.cloned.1.call-done
  609.7 2.5 slice.56
  614.6 3.2 copy.48
  617.8 15.3 %place_parts.4.refs_1_ = bf16[768,32000]{1,0:T(8,128)(2,1)} custom-call(bf16[16,320,2048]{2,1,0:T(8,128)(2,1)} %bitcast.203, bf16[768,32000]{1,0:T(8,128)(2,1)} %place_parts.3.refs_1_), custom_call_target="tpu_custom_call", output_to_operand_aliasing={{}: (1, {})} | custom-call | flops 131072000 | bytes 32768000 | tf_op jit(solution)/shard_map/place_parts/pallas_call | solution.py:452
  633.1 13.6 %back_project.1 = (bf16[2,768,2048]{2,1,0:T(8,128)(2,1)}, bf16[2,2048,768]{2,1,0:T(8,128)(2,1)}) custom-call(bf16[16,4,256,128]{3,2,1,0:T(8,128)(2,1)} %bitcast.200, bf16[16,4,256,128]{3,2,1,0:T(8,128)(2,1)} %bitcast.201, bf16[2,768,2048]{2,1,0:T(8,128)(2,1)} %w_up_ref.1, bf16[2,2048,768]{2,1,0:T(8,128)(2,1)} %w_down_ref.1, bf16[2,768,256]{2,1,0:T(8,128)(2,1)} %p_ref.1, ...), custom_call_target="tpu_custom_call" | custom-call | flops 3221225472 | bytes 30000000 | tf_op jit(solution)/shard_map/back_project/pallas_call | solution.py:481
  646.7 41.0 %all-gather.9.cloned.1.call-done = bf16[4096,2048]{1,0:T(8,128)(2,1)} async-done(((bf16[256,2048]{1,0:T(8,128)(2,1)}), bf16[4096,2048]{1,0:T(8,128)(2,1)}) %all-gather.9.cloned.1.call-update) | async-done | bytes 16777232 | tf_op jit(solution)/shard_map/all_gather | solution.py:578
  687.8 15.0 %place_parts.5 = bf16[768,32000]{1,0:T(8,128)(2,1)} custom-call(bf16[16,256,2048]{2,1,0:T(8,128)(2,1)} %bitcast.204, bf16[768,32000]{1,0:T(8,128)(2,1)} %place_parts.4.refs_1_), custom_call_target="tpu_custom_call", output_to_operand_aliasing={{}: (1, {})} | custom-call | flops 131072000 | bytes 32768000 | tf_op jit(solution)/shard_map/place_parts/pallas_call | solution.py:452
  (157 shorter events, 38.8 us)
Async XLA Ops:
  7.2 578.7 %all-gather.11.cloned.1.call-start = ((), (), s32[]{:S(2)}) async-start(), calls=%async_computation.2 | async-start | bytes 17825792 | tf_op jit(solution)/shard_map/all_gather | solution.py:578
  20.0 10.7 %copy-start.13 = (s32[4]{0:T(128)S(1)}, s32[4]{0:T(128)}, u32[]{:S(2)}) copy-start(s32[4]{0:T(128)} %constant.264) | copy-start | bytes 52
  59.2 11.2 %slice-start.4 = ((s8[6291456]{0:T(1024)(128)(4,1)}), s8[4194304]{0:T(1024)(128)(4,1)S(1)}, s32[]{:S(2)}) async-start(s8[6291456]{0:T(1024)(128)(4,1)} %bitcast.212), calls=%async_computation.7 | async-start | bytes 8388608
  59.2 15.3 %slice-start = ((s8[6291456]{0:T(1024)(128)(4,1)}), s8[4194304]{0:T(1024)(128)(4,1)S(1)}, s32[]{:S(2)}) async-start(s8[6291456]{0:T(1024)(128)(4,1)} %bitcast.208), calls=%async_computation.3 | async-start | bytes 8388608
  76.9 60.6 %copy-start = (bf16[2,768,256]{2,1,0:T(8,128)(2,1)S(1)}, bf16[2,768,256]{2,1,0:T(8,128)(2,1)}, u32[]{:S(2)}) copy-start(bf16[2,768,256]{2,1,0:T(8,128)(2,1)} %p_ref.1) | copy-start | bytes 2359300
  76.9 20.8 %collective-permute-start.1 = (bf16[768,512]{1,0:T(8,128)(2,1)S(1)}, bf16[768,512]{1,0:T(8,128)(2,1)S(1)}, u32[]{:S(2)}, u32[]{:S(2)}) collective-permute-start(bf16[768,512]{1,0:T(8,128)(2,1)S(1)} %fusion.57.refs_0_), channel_id=1, source_target_pairs={{0,2},{1,3},{2,0},{3,1},{4,6},{5,7},{6,4},{7,5},{8,10},{9,11},{10,... | collective-permute-start | bytes 2359304 | tf_op jit(solution)/shard_map/ppermute | solution.py:40
  80.1 19.1 %collective-permute-start.3 = (bf16[768,512]{1,0:T(8,128)(2,1)S(1)}, bf16[768,512]{1,0:T(8,128)(2,1)}, u32[]{:S(2)}, u32[]{:S(2)}) collective-permute-start(bf16[768,512]{1,0:T(8,128)(2,1)S(1)} %fusion.57.refs_0_), channel_id=1, source_target_pairs={{0,4},{1,5},{2,6},{3,7},{4,0},{5,1},{6,2},{7,3},{8,12},{9,13},{10,... | collective-permute-start | bytes 2359304 | tf_op jit(solution)/shard_map/ppermute | solution.py:40
  81.6 18.7 %collective-permute-start.5 = (bf16[768,512]{1,0:T(8,128)(2,1)S(1)}, bf16[768,512]{1,0:T(8,128)(2,1)S(1)}, u32[]{:S(2)}, u32[]{:S(2)}) collective-permute-start(bf16[768,512]{1,0:T(8,128)(2,1)S(1)} %fusion.57.refs_0_), channel_id=1, source_target_pairs={{0,8},{1,9},{2,10},{3,11},{4,12},{5,13},{6,14},{7,15},{8,0},{9,1},... | collective-permute-start | bytes 2359304 | tf_op jit(solution)/shard_map/ppermute | solution.py:40
  83.2 17.6 %collective-permute-start = (bf16[768,512]{1,0:T(8,128)(2,1)S(1)}, bf16[768,512]{1,0:T(8,128)(2,1)S(1)}, u32[]{:S(2)}, u32[]{:S(2)}) collective-permute-start(bf16[768,512]{1,0:T(8,128)(2,1)S(1)} %fusion.57.refs_0_), channel_id=1, source_target_pairs={{0,1},{1,0},{2,3},{3,2},{4,5},{5,4},{6,7},{7,6},{8,9},{9,8},{10,11... | collective-permute-start | bytes 2359304 | tf_op jit(solution)/shard_map/ppermute | solution.py:40
  97.7 3.6 collective-permute-start.2
  97.7 49.3 %collective-permute-start.10 = (bf16[4,512,640]{2,1,0:T(8,128)(2,1)}, bf16[4,512,640]{2,1,0:T(8,128)(2,1)}, u32[]{:S(2)}, u32[]{:S(2)}) collective-permute-start(bf16[4,512,640]{2,1,0:T(8,128)(2,1)} %get-tuple-element.65), channel_id=1, source_target_pairs={{0,1},{1,0},{2,3},{3,2},{4,5},{5,4},{6,7},{7,6},{8,9},{9,8},{10,11... | collective-permute-start | bytes 7864328 | tf_op jit(solution)/shard_map/ppermute | solution.py:40
  99.2 59.4 %collective-permute-start.12 = (bf16[4,512,640]{2,1,0:T(8,128)(2,1)}, bf16[4,512,640]{2,1,0:T(8,128)(2,1)}, u32[]{:S(2)}, u32[]{:S(2)}) collective-permute-start(bf16[4,512,640]{2,1,0:T(8,128)(2,1)} %get-tuple-element.67), channel_id=1, source_target_pairs={{0,5},{1,4},{2,7},{3,6},{4,1},{5,0},{6,3},{7,2},{8,13},{9,12},{10,... | collective-permute-start | bytes 7864328 | tf_op jit(solution)/shard_map/ppermute | solution.py:40
  100.4 70.4 %collective-permute-start.13 = (bf16[4,512,640]{2,1,0:T(8,128)(2,1)}, bf16[4,512,640]{2,1,0:T(8,128)(2,1)}, u32[]{:S(2)}, u32[]{:S(2)}) collective-permute-start(bf16[4,512,640]{2,1,0:T(8,128)(2,1)} %get-tuple-element.69), channel_id=1, source_target_pairs={{0,1},{1,0},{2,3},{3,2},{4,5},{5,4},{6,7},{7,6},{8,9},{9,8},{10,11... | collective-permute-start | bytes 7864328 | tf_op jit(solution)/shard_map/ppermute | solution.py:40
  100.9 70.8 %collective-permute-start.15 = (bf16[4,512,640]{2,1,0:T(8,128)(2,1)}, bf16[4,512,640]{2,1,0:T(8,128)(2,1)}, u32[]{:S(2)}, u32[]{:S(2)}) collective-permute-start(bf16[4,512,640]{2,1,0:T(8,128)(2,1)} %get-tuple-element.71), channel_id=1, source_target_pairs={{0,3},{1,2},{2,1},{3,0},{4,7},{5,6},{6,5},{7,4},{8,11},{9,10},{10,... | collective-permute-start | bytes 7864328 | tf_op jit(solution)/shard_map/ppermute | solution.py:40
  102.7 35.6 %collective-permute-start.4 = (bf16[768,512]{1,0:T(8,128)(2,1)}, bf16[768,512]{1,0:T(8,128)(2,1)}, u32[]{:S(2)}, u32[]{:S(2)}) collective-permute-start(bf16[768,512]{1,0:T(8,128)(2,1)} %collective-permute-done.3.refs_4_), channel_id=1, source_target_pairs={{0,1},{1,0},{2,3},{3,2},{4,5},{5,4},{6,7},{7,6},{8,9},{9,8},{10,11... | collective-permute-start | bytes 2359304 | tf_op jit(solution)/shard_map/ppermute | solution.py:40
  138.3 20.3 %copy-start.2 = (bf16[4,512,768]{2,1,0:T(8,128)(2,1)S(1)}, bf16[4,512,768]{2,1,0:T(8,128)(2,1)}, u32[]{:S(2)}) copy-start(bf16[4,512,768]{2,1,0:T(8,128)(2,1)} %pack_columns.7) | copy-start | bytes 9437188
  138.3 21.9 %copy-start.1 = (bf16[2,768,256]{2,1,0:T(8,128)(2,1)S(1)}, bf16[2,768,256]{2,1,0:T(8,128)(2,1)}, u32[]{:S(2)}) copy-start(bf16[2,768,256]{2,1,0:T(8,128)(2,1)} %q_ref.1) | copy-start | bytes 2359300
  138.3 8.4 %collective-permute-start.6 = (bf16[768,512]{1,0:T(8,128)(2,1)}, bf16[768,512]{1,0:T(8,128)(2,1)S(1)}, u32[]{:S(2)}, u32[]{:S(2)}) collective-permute-start(bf16[768,512]{1,0:T(8,128)(2,1)} %copy-done.16), channel_id=1, source_target_pairs={{0,1},{1,0},{2,3},{3,2},{4,5},{5,4},{6,7},{7,6},{8,9},{9,8},{10,11... | collective-permute-start | bytes 2359304 | tf_op jit(solution)/shard_map/ppermute | solution.py:40
  146.7 13.5 %copy-start.19 = (bf16[768,512]{1,0:T(8,128)(2,1)}, bf16[768,512]{1,0:T(8,128)(2,1)S(1)}, u32[]{:S(2)}) copy-start(bf16[768,512]{1,0:T(8,128)(2,1)S(1)} %collective-permute-done.6.refs_7_) | copy-start | bytes 2359300
  146.7 83.2 %collective-permute-start.7 = (bf16[4,512,768]{2,1,0:T(8,128)(2,1)}, bf16[4,512,768]{2,1,0:T(8,128)(2,1)}, u32[]{:S(2)}, u32[]{:S(2)}) collective-permute-start(bf16[4,512,768]{2,1,0:T(8,128)(2,1)} %get-tuple-element.62), channel_id=1, source_target_pairs={{0,1},{1,0},{2,3},{3,2},{4,5},{5,4},{6,7},{7,6},{8,9},{9,8},{10,11... | collective-permute-start | bytes 9437192 | tf_op jit(solution)/shard_map/ppermute | solution.py:40
  146.9 83.0 %collective-permute-start.9 = (bf16[4,512,768]{2,1,0:T(8,128)(2,1)}, bf16[4,512,768]{2,1,0:T(8,128)(2,1)}, u32[]{:S(2)}, u32[]{:S(2)}) collective-permute-start(bf16[4,512,768]{2,1,0:T(8,128)(2,1)} %get-tuple-element.63), channel_id=1, source_target_pairs={{0,9},{1,8},{2,11},{3,10},{4,13},{5,12},{6,15},{7,14},{8,1},{9,0},... | collective-permute-start | bytes 9437192 | tf_op jit(solution)/shard_map/ppermute | solution.py:40
  158.6 126.4 %collective-permute-start.8 = (bf16[4,512,768]{2,1,0:T(8,128)(2,1)S(1)}, bf16[4,512,768]{2,1,0:T(8,128)(2,1)}, u32[]{:S(2)}, u32[]{:S(2)}) collective-permute-start(bf16[4,512,768]{2,1,0:T(8,128)(2,1)S(1)} %copy-done.2), channel_id=1, source_target_pairs={{0,8},{1,9},{2,10},{3,11},{4,12},{5,13},{6,14},{7,15},{8,0},{9,1},... | collective-permute-start | bytes 9437192 | tf_op jit(solution)/shard_map/ppermute | solution.py:40
  170.7 59.0 %collective-permute-start.11 = (bf16[4,512,640]{2,1,0:T(8,128)(2,1)}, bf16[4,512,640]{2,1,0:T(8,128)(2,1)}, u32[]{:S(2)}, u32[]{:S(2)}) collective-permute-start(bf16[4,512,640]{2,1,0:T(8,128)(2,1)} %get-tuple-element.66), channel_id=1, source_target_pairs={{0,4},{1,5},{2,6},{3,7},{4,0},{5,1},{6,2},{7,3},{8,12},{9,13},{10,... | collective-permute-start | bytes 7864328 | tf_op jit(solution)/shard_map/ppermute | solution.py:40
  171.7 58.2 %collective-permute-start.14 = (bf16[4,512,640]{2,1,0:T(8,128)(2,1)}, bf16[4,512,640]{2,1,0:T(8,128)(2,1)}, u32[]{:S(2)}, u32[]{:S(2)}) collective-permute-start(bf16[4,512,640]{2,1,0:T(8,128)(2,1)} %get-tuple-element.70), channel_id=1, source_target_pairs={{0,2},{1,3},{2,0},{3,1},{4,6},{5,7},{6,4},{7,5},{8,10},{9,11},{10,... | collective-permute-start | bytes 7864328 | tf_op jit(solution)/shard_map/ppermute | solution.py:40
  285.1 84.5 %copy-start.8 = (f32[2,128,256]{2,1,0:T(8,128)S(1)}, f32[2,128,256]{2,1,0:T(8,128)}, u32[]{:S(2)}) copy-start(f32[2,128,256]{2,1,0:T(8,128)} %param.34) | copy-start | bytes 786436
  285.1 84.7 %copy-start.9 = (f32[2,128,256]{2,1,0:T(8,128)S(1)}, f32[2,128,256]{2,1,0:T(8,128)}, u32[]{:S(2)}) copy-start(f32[2,128,256]{2,1,0:T(8,128)} %param.35) | copy-start | bytes 786436
  369.6 240.2 %all-gather.7.cloned.1.call-start = ((), (), s32[]{:S(2)}) async-start(), calls=%async_computation | async-start | bytes 22282240 | tf_op jit(solution)/shard_map/all_gather | solution.py:578
  369.9 115.1 %copy-start.10 = (f32[2,256,128]{2,1,0:T(8,128)S(1)}, f32[2,256,128]{2,1,0:T(8,128)}, u32[]{:S(2)}) copy-start(f32[2,256,128]{2,1,0:T(8,128)} %param.32) | copy-start | bytes 786436
  369.9 115.1 %copy-start.11 = (f32[2,256,128]{2,1,0:T(8,128)S(1)}, f32[2,256,128]{2,1,0:T(8,128)}, u32[]{:S(2)}) copy-start(f32[2,256,128]{2,1,0:T(8,128)} %param.33) | copy-start | bytes 786436
  488.2 92.3 %copy-start.4 = (f32[2000,256]{1,0:T(8,128)S(1)}, f32[2000,256]{1,0:T(8,128)}, u32[]{:S(2)}) copy-start(f32[2000,256]{1,0:T(8,128)} %get-tuple-element.110) | copy-start | bytes 6144004
  488.2 199.6 %all-gather.9.cloned.1.call-start = ((), (), s32[]{:S(2)}) async-start(), calls=%async_computation.1 | async-start | bytes 17825792 | tf_op jit(solution)/shard_map/all_gather | solution.py:578
  585.9 15.4 %copy-start.3 = (f32[2000,256]{1,0:T(8,128)S(1)}, f32[2000,256]{1,0:T(8,128)}, u32[]{:S(2)}) copy-start(f32[2000,256]{1,0:T(8,128)} %get-tuple-element.107) | copy-start | bytes 6144004
  (17 other events, 84.8 us)
Sparse Core Ops, SparseCore 0:
  369.7 117.9 all-gather.10
  490.5 119.1 all-gather.6
  612.0 75.7 all-gather.8

commit v3 on v2

--- a/solution.py
+++ b/solution.py
@@ -20,7 +20,9 @@
 GROUP_BITS = ((Z, Y, X), (Y, X, Z), (X, Z, Y))
 GROUP_TILES = (6, 5, 5)
 TERM_BITS = ((X, Y, Z), (Y, Z, X), (Z, X, Y), (Z, Y, X))
-LOW_STEPS = 2
+LOW_STEPS = (1, 3)
+PLACE_SPLIT = 1
+TAIL_ROWS = 64
 PACKS = (((0, 2),), ((1, 2), (2, 2)), ((0, 3), (1, 3), (2, 3)), ((0, 1), (1, 1), (2, 1)), ((0, 0), (1, 0), (2, 0)))
 ROW_CHUNKS = (256, 256, 256)
 
@@ -32,7 +34,7 @@
 def adam_update(gradient, moment_one, moment_two):
     moment_one = BETA1 * moment_one + (1.0 - BETA1) * gradient
     moment_two = BETA2 * moment_two + (1.0 - BETA2) * gradient * gradient
-    direction = (moment_one / (1.0 - BETA1 ** STEP)) / (jnp.sqrt(moment_two / (1.0 - BETA2 ** STEP)) + EPS)
+    direction = (moment_one * (1.0 / (1.0 - BETA1 ** STEP))) / (jnp.sqrt(moment_two * (1.0 / (1.0 - BETA2 ** STEP))) + EPS)
     return moment_one, moment_two, direction
 
 
@@ -139,23 +141,35 @@
     table = jnp.stack([sum(jnp.where(rel & bit, owners >> (k + 1), 0) for k, bit in enumerate((CORE, *bits))) for bits in TERM_BITS])
 
     def body(table_ref, *refs):
-        out_ref, turned = refs[-2], refs[-1]
+        out_ref, turned, left, right, middle = refs[-5:]
+        term = pl.program_id(0)
         for m in range(count):
             p_ref, h_ref, e_ref = refs[3 * m:3 * m + 3]
 
-            @pl.when(pl.program_id(0) == m)
+            @pl.when(term == m)
             def _():
                 @pl.when(pl.program_id(1) == 0)
                 def _():
-                    turned[...] = h_ref[...].T
-
-                gradient = jnp.dot(turned[...], e_ref[...], preferred_element_type=jnp.float32)
-                high = gradient.astype(jnp.bfloat16)
-                low = (gradient - high.astype(jnp.float32)).astype(jnp.bfloat16)
-                left = p_ref[...]
-                total = jnp.dot(left, high, preferred_element_type=jnp.float32) + jnp.dot(left, low, preferred_element_type=jnp.float32)
-                for k in range(step_owners):
-                    out_ref[0, table_ref[m, pl.program_id(1) * step_owners + k]] = total[:, k * cols:(k + 1) * cols]
+                    left[...] = p_ref[...]
+                    right[...] = h_ref[...]
+
+                def move(i, carry):
+                    sl = pl.ds(pl.multiple_of(i * 64, 64), 64)
+                    middle[sl] = e_ref[sl]
+                    return carry
+
+                lax.fori_loop(0, tokens // 64, move, 0)
+
+        @pl.when(pl.program_id(1) == 0)
+        def _():
+            turned[...] = right[...].T
+
+        gradient = jnp.dot(turned[...], middle[...], preferred_element_type=jnp.float32)
+        high = gradient.astype(jnp.bfloat16)
+        low = (gradient - high.astype(jnp.float32)).astype(jnp.bfloat16)
+        total = jnp.dot(left[...], high, preferred_element_type=jnp.float32) + jnp.dot(left[...], low, preferred_element_type=jnp.float32)
+        for k in range(step_owners):
+            out_ref[0, table_ref[term, pl.program_id(1) * step_owners + k]] = total[:, k * cols:(k + 1) * cols]
 
     in_specs, operands = [], []
     for m, (p, h, e) in enumerate(terms):
@@ -169,7 +183,7 @@
             grid=(count, hidden // block),
             in_specs=in_specs,
             out_specs=pl.BlockSpec((1, owners, rank, cols), lambda t, c, _: (t, 0, 0, 0)),
-            scratch_shapes=[pltpu.VMEM((model, tokens), jnp.bfloat16)],
+            scratch_shapes=[pltpu.VMEM(dims, jnp.bfloat16) for dims in ((model, tokens), (rank, model), (tokens, model), (tokens, block))],
         ),
         out_shape=jax.ShapeDtypeStruct((count, owners, rank, cols), jnp.float32),
         cost_estimate=pl.CostEstimate(flops=count * 2 * model * hidden * (tokens + 2 * rank), bytes_accessed=count * hidden * (tokens * 2 + rank * 4), transcendentals=0),
@@ -182,6 +196,8 @@
     offsets = group_offsets()
     row_chunk = ROW_CHUNKS[chunk]
     places = 0 if low is None else low.shape[1]
+    low_steps = 0 if low is None else LOW_STEPS[chunk]
+    low_done = sum(LOW_STEPS[:chunk])
     last_tile = (w_out.shape[1] - offsets[-1] - LANES) // LANES
     shard_cols = mom_out.shape[0]
     owners, tokens, _ = packed[0][0].shape
@@ -199,8 +215,8 @@
         w_ref, mom_ref, var_ref, w_out_ref, mom_out_ref, var_out_ref = refs[:6]
         refs = refs[6:]
         if low is not None:
-            low_out_ref, low_buf, *low_got, low_load, low_send, low_recv = refs[:5 + LOW_STEPS]
-            refs = refs[5 + LOW_STEPS:]
+            low_out_ref, low_buf, *low_got, low_load, low_send, low_recv = refs[:5 + low_steps]
+            refs = refs[5 + low_steps:]
         near_buf, near_sem, w_window, *refs = refs
         blocks, refs = refs[:groups], refs[groups:]
         part, refs = refs[:groups], refs[groups:]
@@ -239,7 +255,7 @@
             source = low_ref if at == 0 else low_buf
             return pltpu.make_async_remote_copy(
                 src_ref=source.at[term, pl.ds(half, half)], dst_ref=low_got[at].at[term], send_sem=low_send.at[at, term], recv_sem=low_recv.at[at, term],
-                device_id=(me ^ (CORE, *TERM_BITS[term])[chunk * LOW_STEPS + at],), device_id_type=pl.DeviceIdType.MESH)
+                device_id=(me ^ (CORE, *TERM_BITS[term])[low_done + at],), device_id_type=pl.DeviceIdType.MESH)
 
         def low_step(at):
             half = places >> (at + 1)
@@ -251,7 +267,7 @@
                     return carry
 
                 lax.fori_loop(0, half, add, 0)
-                if at + 1 < LOW_STEPS:
+                if at + 1 < low_steps:
                     low_copy(at + 1, term).start()
 
         if low is not None:
@@ -275,12 +291,6 @@
 
         def step(i, carry):
             entry = 3 - i
-            if low is not None:
-                @pl.when(i == 1)
-                def _():
-                    for copy in low_loads:
-                        copy.wait()
-                    low_step(0)
             for g in range(groups):
                 for copy in load(g, entry):
                     copy.wait()
@@ -322,6 +332,10 @@
 
         lax.fori_loop(0, 4, step, 0)
 
+        if low is not None:
+            for copy in low_loads:
+                copy.wait()
+            low_step(0)
         for copy in state:
             copy.wait()
         lane = lax.broadcasted_iota(jnp.int32, (64, LANES), 1)
@@ -333,13 +347,20 @@
             return carry
 
         lax.fori_loop(0, row_chunk // 64, align, 0)
-        for at in range(0, offsets[-1], LANES):
-            cols = slice(at, at + LANES)
-            mom_buf[:, cols] = mom_turned[cols].T
-            var_buf[:, cols] = var_turned[cols].T
+
+        def turn_in(i, carry):
+            for k in range(2):
+                cols = pl.ds(pl.multiple_of((2 * i + k) * LANES, LANES), LANES)
+                mom_buf[:, cols] = mom_turned[cols].T
+                var_buf[:, cols] = var_turned[cols].T
+            return carry
+
+        lax.fori_loop(0, offsets[-1] // (2 * LANES), turn_in, 0)
         block = 32
         for g in range(groups):
             first_copy(g, 2).wait_recv()
+        if low_steps > 1:
+            low_step(1)
         for g in range(groups):
             second_copy(g).wait_recv()
             cols = slice(offsets[g], offsets[g + 1])
@@ -358,18 +379,24 @@
                    pltpu.make_async_copy(mom_turned.at[valid], mom_out_ref, state_sem.at[1]),
                    pltpu.make_async_copy(var_turned.at[valid], var_out_ref, state_sem.at[2])]
         results[0].start()
-        for at in range(0, offsets[-1], LANES):
-            cols = slice(at, at + LANES)
-            mom_turned[cols] = mom_buf[:, cols].T
-            var_turned[cols] = var_buf[:, cols].T
+
+        def turn_out(i, carry):
+            for k in range(4):
+                cols = pl.ds(pl.multiple_of((4 * i + k) * LANES, LANES), LANES)
+                mom_turned[cols] = mom_buf[:, cols].T
+                var_turned[cols] = var_buf[:, cols].T
+            return carry
+
+        lax.fori_loop(0, offsets[-1] // (4 * LANES), turn_out, 0)
         results[1].start()
         results[2].start()
         if low is not None:
-            low_step(1)
-            results += [pltpu.make_async_copy(low_buf.at[term, pl.ds(0, places >> LOW_STEPS)], low_out_ref.at[term], low_load.at[term]) for term in range(len(TERM_BITS))]
+            if low_steps > 2:
+                low_step(2)
+            results += [pltpu.make_async_copy(low_buf.at[term, pl.ds(0, places >> low_steps)], low_out_ref.at[term], low_load.at[term]) for term in range(len(TERM_BITS))]
             for copy in results[3:]:
                 copy.start()
-            for at in range(LOW_STEPS):
+            for at in range(low_steps):
                 for term in range(len(TERM_BITS)):
                     low_copy(at, term).wait_send()
         for g in range(groups):
@@ -384,10 +411,10 @@
     scratch = []
     if low is not None:
         terms, _, rank, cols = low.shape
-        out_shapes.append(jax.ShapeDtypeStruct((terms, places >> LOW_STEPS, rank, cols), jnp.float32))
+        out_shapes.append(jax.ShapeDtypeStruct((terms, places >> low_steps, rank, cols), jnp.float32))
         scratch.append(pltpu.VMEM((terms, places // 2, rank, cols), jnp.float32))
-        scratch += [pltpu.VMEM((terms, places >> (at + 1), rank, cols), jnp.float32) for at in range(LOW_STEPS)]
-        scratch += [pltpu.SemaphoreType.DMA((terms,)), pltpu.SemaphoreType.DMA((LOW_STEPS, terms)), pltpu.SemaphoreType.DMA((LOW_STEPS, terms))]
+        scratch += [pltpu.VMEM((terms, places >> (at + 1), rank, cols), jnp.float32) for at in range(low_steps)]
+        scratch += [pltpu.SemaphoreType.DMA((terms,)), pltpu.SemaphoreType.DMA((low_steps, terms)), pltpu.SemaphoreType.DMA((low_steps, terms))]
     scratch += [pltpu.VMEM((groups, 4, row_chunk, tokens), jnp.bfloat16), pltpu.SemaphoreType.DMA((groups, 4)), pltpu.VMEM((row_chunk, offsets[-1] + LANES), jnp.bfloat16)]
     scratch += [pltpu.VMEM((4, tokens, w), jnp.bfloat16) for w in widths]
     scratch += [pltpu.VMEM((owners, row_chunk, w), jnp.float32) for w in widths]
@@ -409,20 +436,90 @@
     )(*[near[k] for k in near_keys], *([] if low is None else [low]), *[packed[g][m] for g in range(groups) for m in masks[g]], w_out, mom_out, var_out)
 
 
-def place_parts(parts, vocab, total_rows, chunk, previous):
+def gather_rows(values, first_row):
+    total, width = values.shape
+    count = total - first_row
+    groups = len(GROUP_BITS)
+    offsets = group_offsets()
+    hops = []
+    for bit, first, second in GROUP_BITS:
+        known = [0]
+        moves = []
+        for axis in (bit, first, second, CORE):
+            moves += [(rel, axis) for rel in known]
+            known += [rel | axis for rel in known]
+        hops.append(moves)
+
+    def body(values_ref, out_ref, own_sem, send_sem, recv_sem):
+        me = lax.axis_index(DATA_AXIS)
+        barrier = pltpu.get_barrier_semaphore()
+        for bit in (X, Y, Z, CORE):
+            pl.semaphore_signal(barrier, inc=1, device_id=(me ^ bit,), device_id_type=pl.DeviceIdType.MESH)
+        own = pltpu.make_async_copy(values_ref.at[pl.ds(first_row, count)], out_ref.at[me], own_sem)
+        own.start()
+        pl.semaphore_wait(barrier, 4)
+        own.wait()
+
+        def hop(g, rel, axis):
+            at = hops[g].index((rel, axis))
+            block = out_ref.at[me ^ rel, :, pl.ds(offsets[g], offsets[g + 1] - offsets[g])]
+            return pltpu.make_async_remote_copy(
+                src_ref=block, dst_ref=block, send_sem=send_sem.at[g, at], recv_sem=recv_sem.at[g, at],
+                device_id=(me ^ axis,), device_id_type=pl.DeviceIdType.MESH)
+
+        def arrival(g, rel, axis):
+            at = hops[g].index((rel, axis))
+            block = out_ref.at[me ^ rel ^ axis, :, pl.ds(offsets[g], offsets[g + 1] - offsets[g])]
+            return pltpu.make_async_remote_copy(
+                src_ref=block, dst_ref=block, send_sem=send_sem.at[g, at], recv_sem=recv_sem.at[g, at],
+                device_id=(me ^ axis,), device_id_type=pl.DeviceIdType.MESH)
+
+        for g in range(groups):
+            for axis in (*GROUP_BITS[g], CORE):
+                hop(g, 0, axis).start()
+        for step in range(7):
+            for g in range(groups):
+                bit, first, second = GROUP_BITS[g]
+                rel, axis = ((0, bit), (0, first), (bit, first), (0, second), (bit, second), (first, second), (bit | first, second))[step]
+                arrival(g, rel, axis).wait_recv()
+                later = {bit: (first, second, CORE), first: (second, CORE), second: (CORE,)}[axis]
+                for onward in later:
+                    hop(g, rel | axis, onward).start()
+        for g in range(groups):
+            for rel, axis in hops[g]:
+                if axis == CORE:
+                    arrival(g, rel, axis).wait_recv()
+        for g in range(groups):
+            for rel, axis in hops[g]:
+                hop(g, rel, axis).wait_send()
+
+    return pl.pallas_call(
+        body,
+        in_specs=[pl.BlockSpec(memory_space=pl.ANY)],
+        out_specs=pl.BlockSpec(memory_space=pltpu.VMEM),
+        out_shape=jax.ShapeDtypeStruct((DEVICES, count, width), values.dtype),
+        scratch_shapes=[pltpu.SemaphoreType.DMA, pltpu.SemaphoreType.DMA((groups, 15)), pltpu.SemaphoreType.DMA((groups, 15))],
+        cost_estimate=pl.CostEstimate(flops=10_000_000_000, bytes_accessed=10_000_000, transcendentals=0),
+        compiler_params=pltpu.CompilerParams(collective_id=len(ROW_CHUNKS), has_side_effects=True),
+        name='gather_rows',
+    )(values)
+
+
+def place_parts(parts, vocab, total_rows, start_row, count_rows, previous):
     shard_cols = vocab // DEVICES
     rows = 32
     count = -(-shard_cols // LANES)
+    share = DEVICES // PLACE_SPLIT
 
     def body(*refs):
-        part_ref, out_ref = refs[0], refs[-1]
+        part_refs, out_ref = refs[:PLACE_SPLIT], refs[-1]
         lane = lax.broadcasted_iota(jnp.int32, (rows, LANES), 1)
         pending = None
         for owner in range(DEVICES):
             base, shift = divmod(owner * shard_cols, LANES)
             rolled = []
             for index in range(count):
-                piece = part_ref[owner, :, index * LANES:(index + 1) * LANES]
+                piece = part_refs[owner // share][owner % share, :, index * LANES:(index + 1) * LANES]
                 rolled.append(pltpu.roll(piece, shift, 1) if shift else piece)
             end = owner * shard_cols + shard_cols
             for tile in range(base, -(-end // LANES)):
@@ -440,15 +537,15 @@
                 else:
                     pending = value
 
-    steps = ROW_CHUNKS[chunk] // rows
-    start = sum(ROW_CHUNKS[:chunk]) // rows
-    in_specs = [pl.BlockSpec((DEVICES, rows, count * LANES), lambda s: (0, s, 0))]
-    operands = [parts]
+    steps = count_rows // rows
+    start = start_row // rows
+    in_specs = [pl.BlockSpec((share, rows, count * LANES), lambda s, k=k: (k, s, 0)) for k in range(PLACE_SPLIT)]
+    operands = [parts] * PLACE_SPLIT
     aliases = {}
     if previous is not None:
         in_specs.append(pl.BlockSpec(memory_space=pl.ANY))
         operands.append(previous)
-        aliases = {1: 0}
+        aliases = {PLACE_SPLIT: 0}
     return pl.pallas_call(
         body,
         grid=(steps,),
@@ -456,7 +553,7 @@
         out_specs=pl.BlockSpec((rows, vocab), lambda s: (start + s, 0)),
         out_shape=jax.ShapeDtypeStruct((total_rows, vocab), jnp.bfloat16),
         input_output_aliases=aliases,
-        cost_estimate=pl.CostEstimate(flops=ROW_CHUNKS[chunk] * vocab * 16, bytes_accessed=ROW_CHUNKS[chunk] * vocab * 4, transcendentals=0),
+        cost_estimate=pl.CostEstimate(flops=count_rows * vocab * 16, bytes_accessed=count_rows * vocab * 4, transcendentals=0),
         name='place_parts',
     )(*operands)
 
@@ -567,6 +664,8 @@
         results.append(list(reduce_head(near, packed, w_out, mom_out.T, var_out.T, chunk, low)))
         low = results[-1][3] if chunk == 0 else None
         payload = results[-1][0]
+        if chunk == chunks - 1:
+            payload = payload[:-TAIL_ROWS]
         if chunk == 1:
             low_scattered = results[1][3][:, 0]
             m_up, v_up, dir_up = adam_update(low_scattered[:layers], mom_up, var_up)
@@ -577,9 +676,12 @@
             payload = jnp.concatenate([payload, dirs], axis=0)
         gathered.append(lax.all_gather(payload, DATA_AXIS, axis=0))
     w_out_new = None
-    gathered[0], results[-1][1] = lax.optimization_barrier((gathered[0], results[-1][1]))
-    for chunk in range(chunks):
-        w_out_new = place_parts(gathered[chunk], vocab, total_rows, chunk, w_out_new)
+    gathered.append(gather_rows(results[-1][0], ROW_CHUNKS[-1] - TAIL_ROWS))
+    gathered[0], gathered[-1] = lax.optimization_barrier((gathered[0], gathered[-1]))
+    pieces = list(zip(gathered[:-2], ROW_CHUNKS)) + [(gathered[-1], TAIL_ROWS), (gathered[-2], ROW_CHUNKS[-1] - TAIL_ROWS)]
+    starts = [sum(ROW_CHUNKS[:k]) for k in range(chunks - 1)] + [total_rows - TAIL_ROWS, total_rows - ROW_CHUNKS[-1]]
+    for (piece, count), start in zip(pieces, starts):
+        w_out_new = place_parts(piece, vocab, total_rows, start, count, w_out_new)
     dirs = gathered[1][:, ROW_CHUNKS[1]:].reshape(DEVICES, -1, side, cols).transpose(0, 2, 1, 3).reshape(DEVICES, 2 * layers, rank, cols)
     w_up_new, w_down_new = back_project(dirs, w_up, w_down, proj_up, proj_down)
     m_out = jnp.concatenate([r[1] for r in results], axis=1).T

time: 718 us -> 722 us (level)
  waiting for transfers between devices: 151 us -> 110 us
  Pallas kernels: 418 us -> 451 us
  matrix products: 69.9 us -> 81.5 us
    all_gather x3, waiting for transfers between devices: 44.1 us -> 3.93 us  [local_step(): gathered.append(lax.all_gather(payload, DATA_AXIS, axis=0))]
    pallas_call x0 -> x1, Pallas kernels: none -> 29.2 us  [gather_rows(): pl.pallas_call(body, in_specs=[pl.BlockSpec(memory_space=pl.ANY)], out_sp...]
    dot_general x2, matrix products: 10.2 us -> 22.2 us  [forward(): jnp.dot(hidden, w_up[layer_idx], preferred_element_type=jnp.float32)]
    pallas_call x3 -> x4, Pallas kernels: 45.8 us -> 46.5 us  [place_parts(): pl.pallas_call(body, grid=(steps,), in_specs=in_specs, out_specs=pl.Block...]
  transfers between devices with their start and end apart: 19 -> 19, of which waited for: 9 -> 8; matrix products, arithmetic and copies ran while one was open for 13% -> 12% of each run, Pallas kernels for 38% -> 46%
where the time goes in v3:
time: 722 us; the launch traced here: 713 us
  Pallas kernels  451 us (62%)
  waiting for transfers between devices  110 us (15%)
  matrix products  81.5 us (11%)
  local copies, waits for them, and re-layouts  24.9 us (3%)
  other arithmetic  17.8 us (2%)
  between operations  14.7 us (2%)
  starting transfers between devices  14.1 us (2%)
    pallas_call x3, Pallas kernels, reduce_head(): pl.pallas_call(body, in_specs=[anywhere] * (len(near_keys) + 4 * groups +...  291 us
    ppermute x16, waiting for transfers between devices, swap(): lax.ppermute(values, DATA_AXIS, [(i, i ^ mask) for i in range(DEVICES)])  106 us
    pallas_call x5, Pallas kernels, pack_columns(): pl.pallas_call(body, grid_spec=pltpu.PrefetchScalarGridSpec(num_scalar_pr...  47.4 us
    pallas_call x4, Pallas kernels, place_parts(): pl.pallas_call(body, grid=(steps,), in_specs=in_specs, out_specs=pl.Block...  46.5 us
    dot_general x1, matrix products, backward(): jnp.einsum('tv,dv->td', d_logits, w_out, preferred_element_type=jnp.float32)  34.2 us
    pallas_call x1, Pallas kernels, gather_rows(): pl.pallas_call(body, in_specs=[pl.BlockSpec(memory_space=pl.ANY)], out_sp...  29.2 us
    pallas_call x1, Pallas kernels, project_gradients(): pl.pallas_call(body, grid_spec=pltpu.PrefetchScalarGridSpec(num_scalar_pr...  23.4 us
    dot_general x2, matrix products, forward(): jnp.dot(hidden, w_up[layer_idx], preferred_element_type=jnp.float32)  22.2 us
  transfers between devices with their start and end apart: 19, of which 8 were waited for; matrix products, arithmetic and copies ran while one was open for 12% of the time, Pallas kernels for 46%

profile of v3, /device:TPU:0, one launch (start us, length us, event | category | flops | bytes accessed | tf_op | source)
XLA Modules:
  0.0 713.5 jit_solution(9920400194592035675)
XLA Ops:
  8.9 10.5 %pack_columns.5 = (bf16[4,512,768]{2,1,0:T(8,128)(2,1)}, bf16[4,512,640]{2,1,0:T(8,128)(2,1)}, bf16[4,512,640]{2,1,0:T(8,128)(2,1)}) custom-call(s32[3,3,4]{2,1,0:T(4,128)} %pad_add_fusion.table_ref, bf16[512,32000]{1,0:T(8,128)(2,1)} %refs_1_.7, bf16[512,32000]{1,0:T(8,128)(2,1)} %refs_1_.7, bf16[512,32000]{1,0:T(8,128)(2,1)} %refs_1_.7), custom_call_target="tpu_custom_call" | custom-call | flops 3221225472 | bytes 16777216 | tf_op jit(solution)/shard_map/pack_columns/pallas_call | solution.py:123
  20.0 10.7 %pack_columns.6 = (bf16[4,512,768]{2,1,0:T(8,128)(2,1)}, bf16[4,512,640]{2,1,0:T(8,128)(2,1)}, bf16[4,512,640]{2,1,0:T(8,128)(2,1)}) custom-call(s32[3,3,4]{2,1,0:T(4,128)} %pad_add_fusion.1.table_ref, bf16[512,32000]{1,0:T(8,128)(2,1)} %refs_1_.7, bf16[512,32000]{1,0:T(8,128)(2,1)} %refs_1_.7, bf16[512,32000]{1,0:T(8,128)(2,1)} %refs_1_.7), custom_call_target="tpu_custom_call" | custom-call | flops 3221225472 | bytes 16777216 | tf_op jit(solution)/shard_map/pack_columns/pallas_call | solution.py:123
  31.4 10.5 %pack_columns.8 = (bf16[4,512,768]{2,1,0:T(8,128)(2,1)}, bf16[4,512,640]{2,1,0:T(8,128)(2,1)}, bf16[4,512,640]{2,1,0:T(8,128)(2,1)}) custom-call(s32[3,3,4]{2,1,0:T(4,128)} %pad_add_fusion.2.table_ref, bf16[512,32000]{1,0:T(8,128)(2,1)} %refs_1_.7, bf16[512,32000]{1,0:T(8,128)(2,1)} %refs_1_.7, bf16[512,32000]{1,0:T(8,128)(2,1)} %refs_1_.7), custom_call_target="tpu_custom_call" | custom-call | flops 3221225472 | bytes 16777216 | tf_op jit(solution)/shard_map/pack_columns/pallas_call | solution.py:123
  42.6 8.7 %pack_columns.9 = (bf16[4,512,640]{2,1,0:T(8,128)(2,1)}, bf16[4,512,640]{2,1,0:T(8,128)(2,1)}) custom-call(s32[2,3,4]{2,1,0:T(4,128)} %pad_add_fusion.3.table_ref, bf16[512,32000]{1,0:T(8,128)(2,1)} %refs_1_.7, bf16[512,32000]{1,0:T(8,128)(2,1)} %refs_1_.7), custom_call_target="tpu_custom_call" | custom-call | flops 2013265920 | bytes 10485760 | tf_op jit(solution)/shard_map/pack_columns/pallas_call | solution.py:123
  51.8 7.0 pack_columns.7
  59.2 6.1 fusion.11
  65.3 5.0 add_convert_fusion.2
  70.4 16.1 %fusion.17 = (bf16[512,2048]{1,0:T(8,128)(2,1)}, bf16[512,2048]{1,0:T(8,128)(2,1)S(1)}) fusion(bf16[512,768]{0,1:T(8,128)(2,1)S(1)} %add_convert_fusion.2, bf16[2,768,2048]{2,1,0:T(8,128)(2,1)S(1)} %bitcast.213), kind=kOutput, calls=%fused_computation.29 | convolution fusion | flops 1622147072 | bytes 8126464 | tf_op jit(solution)/shard_map/dot_general | solution.py:596
  88.9 3.2 collective-permute-start.1
  95.2 14.4 %collective-permute-done.1.refs_2_ = bf16[768,512]{1,0:T(8,128)(2,1)S(1)} collective-permute-done((bf16[768,512]{1,0:T(8,128)(2,1)S(1)}, bf16[768,512]{1,0:T(8,128)(2,1)S(1)}, u32[]{:S(2)}, u32[]{:S(2)}) %collective-permute-start.1) | collective-permute-done | bytes 786464 | tf_op jit(solution)/shard_map/ppermute | solution.py:42
  114.9 34.2 %convolution_convert_fusion.refs_10_ = bf16[512,768]{1,0:T(8,128)(2,1)} fusion(bf16[512,32000]{1,0:T(8,128)(2,1)} %refs_1_.7, bf16[768,32000]{1,0:T(8,128)(2,1)} %refs_20_.1), kind=kOutput, calls=%fused_computation.59 | convolution fusion | flops 25166217216 | bytes 82706432 | tf_op jit(solution)/shard_map/tv,dv->td/dot_general | solution.py:605
  150.2 8.1 %fusion.4.refs_5_ = bf16[512,2048]{1,0:T(8,128)(2,1)} fusion(bf16[512,2048]{1,0:T(8,128)(2,1)} %copy-done.25, bf16[512,768]{1,0:T(8,128)(2,1)} %convolution_convert_fusion.refs_10_, bf16[2,2048,768]{2,1,0:T(8,128)(2,1)} %w_down_ref.1), kind=kOutput, calls=%fused_computation.16 | convolution fusion | flops 1632632832 | bytes 8126464 | tf_op jit(solution)/shard_map/td,fd->tf/dot_general | solution.py:611
  160.0 10.6 %collective-permute-done.12.refs_16_.refs_15_ = bf16[4,512,640]{2,1,0:T(8,128)(2,1)} collective-permute-done((bf16[4,512,640]{2,1,0:T(8,128)(2,1)}, bf16[4,512,640]{2,1,0:T(8,128)(2,1)}, u32[]{:S(2)}, u32[]{:S(2)}) %collective-permute-start.12) | collective-permute-done | bytes 2621472 | tf_op jit(solution)/shard_map/ppermute | solution.py:42
  184.9 4.5 add_convert_fusion.refs_7_
  189.5 5.1 fusion.7.refs_2_
  194.6 23.4 %project_gradients.1.refs_8_ = f32[4,16,256,128]{3,2,1,0:T(8,128)} custom-call(s32[4,16]{1,0:T(4,128)} %pad_add_fusion.4.table_ref, bf16[256,768]{1,0:T(8,128)(2,1)} %bitcast.217, bf16[512,768]{1,0:T(8,128)(2,1)} %refs_1_.8, bf16[512,2048]{1,0:T(8,128)(2,1)} %fusion.7.refs_2_, bf16[256,768]{1,0:T(8,128)(2,1)} %bitcast.218, bf16[512,768]{1,0:T(8,128)(2,1)} %copy.44.refs_4_, ...), custom_call_target="tpu_custom_call" | custom-call | flops 12884901888 | bytes 16777216 | tf_op jit(solution)/shard_map/project_gradients/pallas_call | solution.py:179
  218.0 23.7 %collective-permute-done.11.refs_15_.refs_14_ = bf16[4,512,640]{2,1,0:T(8,128)(2,1)} collective-permute-done((bf16[4,512,640]{2,1,0:T(8,128)(2,1)}, bf16[4,512,640]{2,1,0:T(8,128)(2,1)}, u32[]{:S(2)}, u32[]{:S(2)}) %collective-permute-start.11) | collective-permute-done | bytes 2621472 | tf_op jit(solution)/shard_map/ppermute | solution.py:42
  242.0 54.7 %collective-permute-done.8.refs_11_.refs_10_ = bf16[4,512,768]{2,1,0:T(8,128)(2,1)} collective-permute-done((bf16[4,512,768]{2,1,0:T(8,128)(2,1)S(1)}, bf16[4,512,768]{2,1,0:T(8,128)(2,1)}, u32[]{:S(2)}, u32[]{:S(2)}) %collective-permute-start.8) | collective-permute-done | bytes 3145760 | tf_op jit(solution)/shard_map/ppermute | solution.py:42
  296.7 64.2 %reduce_head.3 = (bf16[256,2048]{1,0:T(8,128)(2,1)}, f32[2000,256]{1,0:T(8,128)}, f32[2000,256]{1,0:T(8,128)}, f32[4,8,256,128]{3,2,1,0:T(8,128)}) custom-call(bf16[768,512]{1,0:T(8,128)(2,1)} %copy-done.16, bf16[768,512]{1,0:T(8,128)(2,1)} %copy-done.19, bf16[768,512]{1,0:T(8,128)(2,1)} %copy-done.17, bf16[768,512]{1,0:T(8,128)(2,1)} %copy-done.20, ...), custom_call_target="tpu_custom_call" | custom-call | flops 60000002048 | bytes 100000000 | tf_op jit(solution)/shard_map/reduce_head/pallas_call | solution.py:427
  361.2 133.7 %reduce_head.4 = (bf16[256,2048]{1,0:T(8,128)(2,1)}, f32[2000,256]{1,0:T(8,128)}, f32[2000,256]{1,0:T(8,128)}, f32[4,1,256,128]{3,2,1,0:T(8,128)}) custom-call(bf16[768,512]{1,0:T(8,128)(2,1)} %copy-done.16, bf16[768,512]{1,0:T(8,128)(2,1)} %copy-done.19, bf16[768,512]{1,0:T(8,128)(2,1)} %copy-done.17, bf16[768,512]{1,0:T(8,128)(2,1)} %copy-done.20, ...), custom_call_target="tpu_custom_call" | custom-call | flops 60000002048 | bytes 100000000 | tf_op jit(solution)/shard_map/reduce_head/pallas_call | solution.py:427
  499.4 92.7 %reduce_head.5 = (bf16[256,2048]{1,0:T(8,128)(2,1)}, f32[2000,256]{1,0:T(8,128)}, f32[2000,256]{1,0:T(8,128)}) custom-call(bf16[768,512]{1,0:T(8,128)(2,1)} %copy-done.16, bf16[768,512]{1,0:T(8,128)(2,1)} %copy-done.19, bf16[768,512]{1,0:T(8,128)(2,1)} %copy-done.17, bf16[768,512]{1,0:T(8,128)(2,1)} %copy-done.20, ...), custom_call_target="tpu_custom_call" | custom-call | flops 60000002048 | bytes 100000000 | tf_op jit(solution)/shard_map/reduce_head/pallas_call | solution.py:427
  596.0 5.8 maximum_bitcast_fusion.1
  601.8 3.1 maximum_bitcast_fusion
  604.9 29.2 %gather_rows.1.refs_0_ = bf16[16,64,2048]{2,1,0:T(8,128)(2,1)} custom-call(bf16[256,2048]{1,0:T(8,128)(2,1)} %get-tuple-element.104.values_ref), custom_call_target="tpu_custom_call" | custom-call | flops 10000000000 | bytes 10000000 | tf_op jit(solution)/shard_map/gather_rows/pallas_call | solution.py:496
  634.1 15.2 %place_parts.4.refs_1_ = bf16[768,32000]{1,0:T(8,128)(2,1)} custom-call(bf16[16,256,2048]{2,1,0:T(8,128)(2,1)} %bitcast.206), custom_call_target="tpu_custom_call" | custom-call | flops 131072000 | bytes 32768000 | tf_op jit(solution)/shard_map/place_parts/pallas_call | solution.py:549
  649.3 2.6 slice.60
  654.3 3.2 copy.49
  657.5 15.8 %place_parts.5.refs_1_ = bf16[768,32000]{1,0:T(8,128)(2,1)} custom-call(bf16[16,320,2048]{2,1,0:T(8,128)(2,1)} %bitcast.203, bf16[768,32000]{1,0:T(8,128)(2,1)} %place_parts.4.refs_1_), custom_call_target="tpu_custom_call", output_to_operand_aliasing={{}: (1, {})} | custom-call | flops 131072000 | bytes 32768000 | tf_op jit(solution)/shard_map/place_parts/pallas_call | solution.py:549
  673.3 4.1 place_parts.6.refs_1_
  677.4 13.9 %back_project.1 = (bf16[2,768,2048]{2,1,0:T(8,128)(2,1)}, bf16[2,2048,768]{2,1,0:T(8,128)(2,1)}) custom-call(bf16[16,4,256,128]{3,2,1,0:T(8,128)(2,1)} %bitcast.200, bf16[16,4,256,128]{3,2,1,0:T(8,128)(2,1)} %bitcast.201, bf16[2,768,2048]{2,1,0:T(8,128)(2,1)} %w_up_ref.1, bf16[2,2048,768]{2,1,0:T(8,128)(2,1)} %w_down_ref.1, bf16[2,768,256]{2,1,0:T(8,128)(2,1)} %p_ref.1, ...), custom_call_target="tpu_custom_call" | custom-call | flops 3221225472 | bytes 30000000 | tf_op jit(solution)/shard_map/back_project/pallas_call | solution.py:578
  691.3 3.9 all-gather.9.cloned.1.call-done
  695.2 11.4 %place_parts.7 = bf16[768,32000]{1,0:T(8,128)(2,1)} custom-call(bf16[16,192,2048]{2,1,0:T(8,128)(2,1)} %bitcast.207, bf16[768,32000]{1,0:T(8,128)(2,1)} %place_parts.6.refs_1_), custom_call_target="tpu_custom_call", output_to_operand_aliasing={{}: (1, {})} | custom-call | flops 98304000 | bytes 24576000 | tf_op jit(solution)/shard_map/place_parts/pallas_call | solution.py:549
  (164 shorter events, 43.3 us)
Async XLA Ops:
  7.2 627.0 %all-gather.11.cloned.1.call-start = ((), (), s32[]{:S(2)}) async-start(), calls=%async_computation.2 | async-start | bytes 17825792 | tf_op jit(solution)/shard_map/all_gather | solution.py:677
  20.0 10.7 %copy-start.15 = (s32[4]{0:T(128)S(1)}, s32[4]{0:T(128)}, u32[]{:S(2)}) copy-start(s32[4]{0:T(128)} %constant.260) | copy-start | bytes 52
  59.2 11.2 %slice-start.4 = ((s8[6291456]{0:T(1024)(128)(4,1)}), s8[4194304]{0:T(1024)(128)(4,1)S(1)}, s32[]{:S(2)}) async-start(s8[6291456]{0:T(1024)(128)(4,1)} %bitcast.212), calls=%async_computation.7 | async-start | bytes 8388608
  59.2 27.4 %slice-start = ((s8[6291456]{0:T(1024)(128)(4,1)}), s8[4194304]{0:T(1024)(128)(4,1)S(1)}, s32[]{:S(2)}) async-start(s8[6291456]{0:T(1024)(128)(4,1)} %bitcast.208), calls=%async_computation.3 | async-start | bytes 8388608
  65.3 21.2 %slice-start.1 = ((s8[6291456]{0:T(1024)(128)(4,1)}), s8[2097152]{0:T(1024)(128)(4,1)S(1)}, s32[]{:S(2)}) async-start(s8[6291456]{0:T(1024)(128)(4,1)} %bitcast.208), calls=%async_computation.4 | async-start | bytes 4194304
  70.4 16.2 %copy-start.9 = (bf16[512,768]{0,1:T(8,128)(2,1)}, bf16[512,768]{0,1:T(8,128)(2,1)S(1)}, u32[]{:S(2)}) copy-start(bf16[512,768]{0,1:T(8,128)(2,1)S(1)} %add_convert_fusion.2) | copy-start | bytes 2359300
  88.9 60.2 %copy-start = (bf16[2,768,256]{2,1,0:T(8,128)(2,1)S(1)}, bf16[2,768,256]{2,1,0:T(8,128)(2,1)}, u32[]{:S(2)}) copy-start(bf16[2,768,256]{2,1,0:T(8,128)(2,1)} %p_ref.1) | copy-start | bytes 2359300
  88.9 20.8 %collective-permute-start.1 = (bf16[768,512]{1,0:T(8,128)(2,1)S(1)}, bf16[768,512]{1,0:T(8,128)(2,1)S(1)}, u32[]{:S(2)}, u32[]{:S(2)}) collective-permute-start(bf16[768,512]{1,0:T(8,128)(2,1)S(1)} %fusion.57.refs_0_), channel_id=1, source_target_pairs={{0,2},{1,3},{2,0},{3,1},{4,6},{5,7},{6,4},{7,5},{8,10},{9,11},{10,... | collective-permute-start | bytes 2359304 | tf_op jit(solution)/shard_map/ppermute | solution.py:42
  92.1 19.1 %collective-permute-start.3 = (bf16[768,512]{1,0:T(8,128)(2,1)S(1)}, bf16[768,512]{1,0:T(8,128)(2,1)}, u32[]{:S(2)}, u32[]{:S(2)}) collective-permute-start(bf16[768,512]{1,0:T(8,128)(2,1)S(1)} %fusion.57.refs_0_), channel_id=1, source_target_pairs={{0,4},{1,5},{2,6},{3,7},{4,0},{5,1},{6,2},{7,3},{8,12},{9,13},{10,... | collective-permute-start | bytes 2359304 | tf_op jit(solution)/shard_map/ppermute | solution.py:42
  93.7 18.7 %collective-permute-start.5 = (bf16[768,512]{1,0:T(8,128)(2,1)S(1)}, bf16[768,512]{1,0:T(8,128)(2,1)S(1)}, u32[]{:S(2)}, u32[]{:S(2)}) collective-permute-start(bf16[768,512]{1,0:T(8,128)(2,1)S(1)} %fusion.57.refs_0_), channel_id=1, source_target_pairs={{0,8},{1,9},{2,10},{3,11},{4,12},{5,13},{6,14},{7,15},{8,0},{9,1},... | collective-permute-start | bytes 2359304 | tf_op jit(solution)/shard_map/ppermute | solution.py:42
  95.2 17.6 %collective-permute-start = (bf16[768,512]{1,0:T(8,128)(2,1)S(1)}, bf16[768,512]{1,0:T(8,128)(2,1)S(1)}, u32[]{:S(2)}, u32[]{:S(2)}) collective-permute-start(bf16[768,512]{1,0:T(8,128)(2,1)S(1)} %fusion.57.refs_0_), channel_id=1, source_target_pairs={{0,1},{1,0},{2,3},{3,2},{4,5},{5,4},{6,7},{7,6},{8,9},{9,8},{10,11... | collective-permute-start | bytes 2359304 | tf_op jit(solution)/shard_map/ppermute | solution.py:42
  109.7 3.6 collective-permute-start.2
  109.7 48.9 %collective-permute-start.10 = (bf16[4,512,640]{2,1,0:T(8,128)(2,1)}, bf16[4,512,640]{2,1,0:T(8,128)(2,1)}, u32[]{:S(2)}, u32[]{:S(2)}) collective-permute-start(bf16[4,512,640]{2,1,0:T(8,128)(2,1)} %get-tuple-element.65), channel_id=1, source_target_pairs={{0,1},{1,0},{2,3},{3,2},{4,5},{5,4},{6,7},{7,6},{8,9},{9,8},{10,11... | collective-permute-start | bytes 7864328 | tf_op jit(solution)/shard_map/ppermute | solution.py:42
  111.2 59.4 %collective-permute-start.12 = (bf16[4,512,640]{2,1,0:T(8,128)(2,1)}, bf16[4,512,640]{2,1,0:T(8,128)(2,1)}, u32[]{:S(2)}, u32[]{:S(2)}) collective-permute-start(bf16[4,512,640]{2,1,0:T(8,128)(2,1)} %get-tuple-element.67), channel_id=1, source_target_pairs={{0,5},{1,4},{2,7},{3,6},{4,1},{5,0},{6,3},{7,2},{8,13},{9,12},{10,... | collective-permute-start | bytes 7864328 | tf_op jit(solution)/shard_map/ppermute | solution.py:42
  112.4 70.4 %collective-permute-start.13 = (bf16[4,512,640]{2,1,0:T(8,128)(2,1)}, bf16[4,512,640]{2,1,0:T(8,128)(2,1)}, u32[]{:S(2)}, u32[]{:S(2)}) collective-permute-start(bf16[4,512,640]{2,1,0:T(8,128)(2,1)} %get-tuple-element.69), channel_id=1, source_target_pairs={{0,1},{1,0},{2,3},{3,2},{4,5},{5,4},{6,7},{7,6},{8,9},{9,8},{10,11... | collective-permute-start | bytes 7864328 | tf_op jit(solution)/shard_map/ppermute | solution.py:42
  112.9 70.9 %collective-permute-start.15 = (bf16[4,512,640]{2,1,0:T(8,128)(2,1)}, bf16[4,512,640]{2,1,0:T(8,128)(2,1)}, u32[]{:S(2)}, u32[]{:S(2)}) collective-permute-start(bf16[4,512,640]{2,1,0:T(8,128)(2,1)} %get-tuple-element.71), channel_id=1, source_target_pairs={{0,3},{1,2},{2,1},{3,0},{4,7},{5,6},{6,5},{7,4},{8,11},{9,10},{10,... | collective-permute-start | bytes 7864328 | tf_op jit(solution)/shard_map/ppermute | solution.py:42
  114.7 35.2 %collective-permute-start.4 = (bf16[768,512]{1,0:T(8,128)(2,1)}, bf16[768,512]{1,0:T(8,128)(2,1)}, u32[]{:S(2)}, u32[]{:S(2)}) collective-permute-start(bf16[768,512]{1,0:T(8,128)(2,1)} %collective-permute-done.3.refs_4_), channel_id=1, source_target_pairs={{0,1},{1,0},{2,3},{3,2},{4,5},{5,4},{6,7},{7,6},{8,9},{9,8},{10,11... | collective-permute-start | bytes 2359304 | tf_op jit(solution)/shard_map/ppermute | solution.py:42
  149.9 20.7 %copy-start.2 = (bf16[4,512,768]{2,1,0:T(8,128)(2,1)S(1)}, bf16[4,512,768]{2,1,0:T(8,128)(2,1)}, u32[]{:S(2)}) copy-start(bf16[4,512,768]{2,1,0:T(8,128)(2,1)} %pack_columns.7) | copy-start | bytes 9437188
  149.9 22.3 %copy-start.1 = (bf16[2,768,256]{2,1,0:T(8,128)(2,1)S(1)}, bf16[2,768,256]{2,1,0:T(8,128)(2,1)}, u32[]{:S(2)}) copy-start(bf16[2,768,256]{2,1,0:T(8,128)(2,1)} %q_ref.1) | copy-start | bytes 2359300
  149.9 8.4 %collective-permute-start.6 = (bf16[768,512]{1,0:T(8,128)(2,1)}, bf16[768,512]{1,0:T(8,128)(2,1)S(1)}, u32[]{:S(2)}, u32[]{:S(2)}) collective-permute-start(bf16[768,512]{1,0:T(8,128)(2,1)} %copy-done.18), channel_id=1, source_target_pairs={{0,1},{1,0},{2,3},{3,2},{4,5},{5,4},{6,7},{7,6},{8,9},{9,8},{10,11... | collective-permute-start | bytes 2359304 | tf_op jit(solution)/shard_map/ppermute | solution.py:42
  158.3 13.9 %copy-start.21 = (bf16[768,512]{1,0:T(8,128)(2,1)}, bf16[768,512]{1,0:T(8,128)(2,1)S(1)}, u32[]{:S(2)}) copy-start(bf16[768,512]{1,0:T(8,128)(2,1)S(1)} %collective-permute-done.6.refs_7_) | copy-start | bytes 2359300
  158.3 83.7 %collective-permute-start.7 = (bf16[4,512,768]{2,1,0:T(8,128)(2,1)}, bf16[4,512,768]{2,1,0:T(8,128)(2,1)}, u32[]{:S(2)}, u32[]{:S(2)}) collective-permute-start(bf16[4,512,768]{2,1,0:T(8,128)(2,1)} %get-tuple-element.62), channel_id=1, source_target_pairs={{0,1},{1,0},{2,3},{3,2},{4,5},{5,4},{6,7},{7,6},{8,9},{9,8},{10,11... | collective-permute-start | bytes 9437192 | tf_op jit(solution)/shard_map/ppermute | solution.py:42
  158.5 83.4 %collective-permute-start.9 = (bf16[4,512,768]{2,1,0:T(8,128)(2,1)}, bf16[4,512,768]{2,1,0:T(8,128)(2,1)}, u32[]{:S(2)}, u32[]{:S(2)}) collective-permute-start(bf16[4,512,768]{2,1,0:T(8,128)(2,1)} %get-tuple-element.63), channel_id=1, source_target_pairs={{0,9},{1,8},{2,11},{3,10},{4,13},{5,12},{6,15},{7,14},{8,1},{9,0},... | collective-permute-start | bytes 9437192 | tf_op jit(solution)/shard_map/ppermute | solution.py:42
  170.6 126.0 %collective-permute-start.8 = (bf16[4,512,768]{2,1,0:T(8,128)(2,1)S(1)}, bf16[4,512,768]{2,1,0:T(8,128)(2,1)}, u32[]{:S(2)}, u32[]{:S(2)}) collective-permute-start(bf16[4,512,768]{2,1,0:T(8,128)(2,1)S(1)} %copy-done.2), channel_id=1, source_target_pairs={{0,8},{1,9},{2,10},{3,11},{4,12},{5,13},{6,14},{7,15},{8,0},{9,1},... | collective-permute-start | bytes 9437192 | tf_op jit(solution)/shard_map/ppermute | solution.py:42
  182.7 59.0 %collective-permute-start.11 = (bf16[4,512,640]{2,1,0:T(8,128)(2,1)}, bf16[4,512,640]{2,1,0:T(8,128)(2,1)}, u32[]{:S(2)}, u32[]{:S(2)}) collective-permute-start(bf16[4,512,640]{2,1,0:T(8,128)(2,1)} %get-tuple-element.66), channel_id=1, source_target_pairs={{0,4},{1,5},{2,6},{3,7},{4,0},{5,1},{6,2},{7,3},{8,12},{9,13},{10,... | collective-permute-start | bytes 7864328 | tf_op jit(solution)/shard_map/ppermute | solution.py:42
  183.7 58.2 %collective-permute-start.14 = (bf16[4,512,640]{2,1,0:T(8,128)(2,1)}, bf16[4,512,640]{2,1,0:T(8,128)(2,1)}, u32[]{:S(2)}, u32[]{:S(2)}) collective-permute-start(bf16[4,512,640]{2,1,0:T(8,128)(2,1)} %get-tuple-element.70), channel_id=1, source_target_pairs={{0,2},{1,3},{2,0},{3,1},{4,6},{5,7},{6,4},{7,5},{8,10},{9,11},{10,... | collective-permute-start | bytes 7864328 | tf_op jit(solution)/shard_map/ppermute | solution.py:42
  296.7 64.3 %copy-start.10 = (f32[2,128,256]{2,1,0:T(8,128)S(1)}, f32[2,128,256]{2,1,0:T(8,128)}, u32[]{:S(2)}) copy-start(f32[2,128,256]{2,1,0:T(8,128)} %param.34) | copy-start | bytes 786436
  296.7 64.4 %copy-start.11 = (f32[2,128,256]{2,1,0:T(8,128)S(1)}, f32[2,128,256]{2,1,0:T(8,128)}, u32[]{:S(2)}) copy-start(f32[2,128,256]{2,1,0:T(8,128)} %param.35) | copy-start | bytes 786436
  360.9 288.4 %all-gather.7.cloned.1.call-start = ((), (), s32[]{:S(2)}) async-start(), calls=%async_computation | async-start | bytes 22282240 | tf_op jit(solution)/shard_map/all_gather | solution.py:677
  361.2 134.9 %copy-start.12 = (f32[2,256,128]{2,1,0:T(8,128)S(1)}, f32[2,256,128]{2,1,0:T(8,128)}, u32[]{:S(2)}) copy-start(f32[2,256,128]{2,1,0:T(8,128)} %param.32) | copy-start | bytes 786436
  361.2 134.9 %copy-start.13 = (f32[2,256,128]{2,1,0:T(8,128)S(1)}, f32[2,256,128]{2,1,0:T(8,128)}, u32[]{:S(2)}) copy-start(f32[2,256,128]{2,1,0:T(8,128)} %param.33) | copy-start | bytes 786436
  499.3 195.9 %all-gather.9.cloned.1.call-start = ((), (), s32[]{:S(2)}) async-start(), calls=%async_computation.1 | async-start | bytes 13369344 | tf_op jit(solution)/shard_map/all_gather | solution.py:677
  (19 other events, 92.8 us)
Sparse Core Ops, SparseCore 0:
  361.0 128.7 all-gather.10
  499.4 131.1 all-gather.6
  632.9 62.2 all-gather.8

commit v4 on v3

--- a/solution.py
+++ b/solution.py
@@ -22,7 +22,7 @@
 TERM_BITS = ((X, Y, Z), (Y, Z, X), (Z, X, Y), (Z, Y, X))
 LOW_STEPS = (1, 3)
 PLACE_SPLIT = 1
-TAIL_ROWS = 64
+TAIL_ROWS = 96
 PACKS = (((0, 2),), ((1, 2), (2, 2)), ((0, 3), (1, 3), (2, 3)), ((0, 1), (1, 1), (2, 1)), ((0, 0), (1, 0), (2, 0)))
 ROW_CHUNKS = (256, 256, 256)
 
@@ -558,15 +558,25 @@
     )(*operands)
 
 
-def back_project(gathered, w_up, w_down, proj_up, proj_down):
+def back_project(gathered, first_row, w_up, w_down, proj_up, proj_down):
     layers, model, hidden = w_up.shape
-    _, _, rank, cols = gathered.shape
+    owners, _, width = gathered.shape
+    rank, cols = proj_up.shape[2], hidden // owners
+    depth = 2 * layers * rank * cols // width
     step_owners = 4
     block = step_owners * cols
 
-    def body(up_dir_ref, down_dir_ref, w_up_ref, w_down_ref, p_ref, q_ref, up_ref, down_ref):
-        up_dir = jnp.concatenate([up_dir_ref[k, 0] for k in range(step_owners)], axis=1)
-        down_dir = jnp.concatenate([down_dir_ref[k, 0] for k in range(step_owners)], axis=1)
+    def direction(ref, term):
+        parts = []
+        for k in range(step_owners):
+            lanes = [pl.ds(pl.multiple_of((term * (rank // depth) + q) * cols, cols), cols) for q in range(rank // depth)]
+            parts.append(jnp.concatenate([ref[k, :, at] for at in lanes], axis=0))
+        return jnp.concatenate(parts, axis=1)
+
+    def body(dir_ref, w_up_ref, w_down_ref, p_ref, q_ref, up_ref, down_ref):
+        layer = pl.program_id(0)
+        up_dir = direction(dir_ref, layer)
+        down_dir = direction(dir_ref, layers + layer)
         step_up = jnp.dot(p_ref[0], up_dir, preferred_element_type=jnp.float32)
         up_ref[0] = (w_up_ref[0].astype(jnp.float32) - LR * ALPHA * step_up).astype(jnp.bfloat16)
         step_down = lax.dot_general(down_dir, q_ref[0], (((0,), (1,)), ((), ())), preferred_element_type=jnp.float32)
@@ -578,26 +588,83 @@
     return pl.pallas_call(
         body,
         grid=(layers, hidden // block),
-        in_specs=[pl.BlockSpec((step_owners, 1, rank, cols), lambda l, c: (c, l, 0, 0)),
-                  pl.BlockSpec((step_owners, 1, rank, cols), lambda l, c: (c, layers + l, 0, 0)),
+        in_specs=[pl.BlockSpec((step_owners, depth, width), lambda l, c: (c, first_row // depth, 0)),
                   up_spec, down_spec, proj_spec, proj_spec],
         out_specs=[up_spec, down_spec],
         out_shape=[jax.ShapeDtypeStruct(w_up.shape, jnp.bfloat16), jax.ShapeDtypeStruct(w_down.shape, jnp.bfloat16)],
         cost_estimate=pl.CostEstimate(flops=8 * model * hidden * rank, bytes_accessed=30_000_000, transcendentals=0),
         name='back_project',
-    )(gathered, gathered, w_up, w_down, proj_up, proj_down)
+    )(gathered, w_up, w_down, proj_up, proj_down)
 
 
 def forward(tokens, w_up, w_down):
-    num_layers = w_up.shape[0]
-    hidden = tokens
-    saved_acts = []
-    for layer_idx in range(num_layers):
-        pre_act = jnp.dot(hidden, w_up[layer_idx], preferred_element_type=jnp.float32).astype(jnp.bfloat16)
-        post_act = gelu_tanh(pre_act.astype(jnp.float32)).astype(jnp.bfloat16)
-        saved_acts.append((hidden, pre_act, post_act))
-        hidden = (hidden.astype(jnp.float32) + jnp.dot(post_act, w_down[layer_idx], preferred_element_type=jnp.float32)).astype(jnp.bfloat16)
-    return hidden, saved_acts
+    layers, model, hidden = w_up.shape
+    rows = tokens.shape[0]
+    block = 512
+    row_block = 256
+    blocks = hidden // block
+
+    def body(tokens_ref, w_up_ref, w_down_ref, *refs):
+        pre_refs, post_refs = refs[:layers], refs[layers:2 * layers]
+        state_refs, turned_ref, state, total = refs[2 * layers:-3], refs[-3], refs[-2], refs[-1]
+        layer, step = pl.program_id(0), pl.program_id(1)
+
+        @pl.when(jnp.logical_and(layer == 0, step == 0))
+        def _():
+            state[...] = tokens_ref[...]
+
+        @pl.when(step == 0)
+        def _():
+            total[...] = jnp.zeros_like(total)
+
+        def part(i, carry):
+            sl = pl.ds(pl.multiple_of(i * row_block, row_block), row_block)
+            pre = jnp.dot(state[sl], w_up_ref[0], preferred_element_type=jnp.float32).astype(jnp.bfloat16)
+            post = gelu_tanh(pre.astype(jnp.float32)).astype(jnp.bfloat16)
+            for m in range(layers):
+                @pl.when(layer == m)
+                def _():
+                    pre_refs[m][sl] = pre
+                    post_refs[m][sl] = post
+            total[sl] += jnp.dot(post, w_down_ref[0], preferred_element_type=jnp.float32)
+            return carry
+
+        lax.fori_loop(0, rows // row_block, part, 0)
+
+        @pl.when(step == blocks - 1)
+        def _():
+            def finish(i, carry):
+                sl = pl.ds(pl.multiple_of(i * 128, 128), 128)
+                new = (state[sl].astype(jnp.float32) + total[sl]).astype(jnp.bfloat16)
+                state[sl] = new
+                for m in range(layers - 1):
+                    @pl.when(layer == m)
+                    def _():
+                        state_refs[m][sl] = new
+                turned_ref[:, sl] = new.T
+                return carry
+
+            lax.fori_loop(0, rows // 128, finish, 0)
+
+    act_specs = [pl.BlockSpec((rows, block), lambda l, c, m=m: (0, jnp.where(l == m, c, jnp.where(l < m, 0, blocks - 1)))) for m in range(layers)]
+    act_shapes = [jax.ShapeDtypeStruct((rows, hidden), jnp.bfloat16)] * layers
+    state_specs = [pl.BlockSpec((rows, model), lambda l, c: (0, 0))] * (layers - 1)
+    state_shapes = [jax.ShapeDtypeStruct((rows, model), jnp.bfloat16)] * (layers - 1)
+    outs = pl.pallas_call(
+        body,
+        grid=(layers, blocks),
+        in_specs=[pl.BlockSpec((rows, model), lambda l, c: (0, 0)),
+                  pl.BlockSpec((1, model, block), lambda l, c: (l, 0, c)),
+                  pl.BlockSpec((1, block, model), lambda l, c: (l, c, 0))],
+        out_specs=[*act_specs, *act_specs, *state_specs, pl.BlockSpec((model, rows), lambda l, c: (0, 0))],
+        out_shape=[*act_shapes, *act_shapes, *state_shapes, jax.ShapeDtypeStruct((model, rows), jnp.bfloat16)],
+        scratch_shapes=[pltpu.VMEM((rows, model), jnp.bfloat16), pltpu.VMEM((rows, model), jnp.float32)],
+        cost_estimate=pl.CostEstimate(flops=4 * layers * rows * model * hidden, bytes_accessed=20_000_000, transcendentals=0),
+        name='forward_blocks',
+    )(tokens, w_up, w_down)
+    states = [tokens, *outs[2 * layers:-1]]
+    saved = [(states[m], outs[m], outs[layers + m]) for m in range(layers)]
+    return outs[-1], saved
 
 
 def backward(saved_acts, d_logits, w_up, w_down, w_out):
@@ -617,8 +684,8 @@
     return up_terms, down_terms
 
 
-def exchange_hidden(hidden):
-    near = {0: hidden.T}
+def exchange_hidden(hidden_t):
+    near = {0: hidden_t}
     near[CORE] = swap(near[0], CORE)
     for bit in (Z, Y, X):
         near[bit] = swap(near[0], bit)
@@ -648,12 +715,12 @@
     for (g, mask), value in mine.items():
         packed[g][mask] = swap(value, mask) if mask else value
     tokens, mine = lax.optimization_barrier((tokens, mine))
-    hidden, saved_acts = forward(tokens, w_up, w_down)
-    near = exchange_hidden(hidden)
+    hidden_t, saved_acts = forward(tokens, w_up, w_down)
+    near = exchange_hidden(hidden_t)
     up_terms, down_terms = backward(saved_acts, d_logits, w_up, w_down, w_out)
     terms = [(proj_up[l], *up_terms[l]) for l in range(layers)] + [(proj_down[l], *down_terms[l]) for l in range(layers)]
     low = project_gradients(terms, DEVICES, me)
-    _, _, rank, cols = low.shape
+    _, _, _, cols = low.shape
     near, low = lax.optimization_barrier((near, low))
     chunks = len(ROW_CHUNKS)
     results = []
@@ -682,8 +749,7 @@
     starts = [sum(ROW_CHUNKS[:k]) for k in range(chunks - 1)] + [total_rows - TAIL_ROWS, total_rows - ROW_CHUNKS[-1]]
     for (piece, count), start in zip(pieces, starts):
         w_out_new = place_parts(piece, vocab, total_rows, start, count, w_out_new)
-    dirs = gathered[1][:, ROW_CHUNKS[1]:].reshape(DEVICES, -1, side, cols).transpose(0, 2, 1, 3).reshape(DEVICES, 2 * layers, rank, cols)
-    w_up_new, w_down_new = back_project(dirs, w_up, w_down, proj_up, proj_down)
+    w_up_new, w_down_new = back_project(gathered[1], ROW_CHUNKS[1], w_up, w_down, proj_up, proj_down)
     m_out = jnp.concatenate([r[1] for r in results], axis=1).T
     v_out = jnp.concatenate([r[2] for r in results], axis=1).T
     return w_up_new, w_down_new, w_out_new, m_up, v_up, m_down, v_down, m_out, v_out

time: 722 us -> 704 us (0.975); the launches traced: 713 us -> 703 us
  Pallas kernels: 451 us -> 482 us
  matrix products: 81.5 us -> 51.9 us
  local copies, waits for them, and re-layouts: 24.9 us -> 15.2 us
    dot_general x4 -> x0, matrix products: 29.5 us -> none  [the longest x2 22.2 us: forward(): jnp.dot(hidden, w_up[layer_idx], preferred_element_type=jnp.float32)]
    pallas_call x0 -> x1, Pallas kernels: none -> 21.1 us  [forward(): pl.pallas_call(body, grid=(layers, blocks), in_specs=[pl.BlockSpec((rows,...]
    pallas_call x1, Pallas kernels: 29.2 us -> 36.9 us  [gather_rows(): pl.pallas_call(body, in_specs=[pl.BlockSpec(memory_space=pl.ANY)], out_sp...]
  transfers between devices with their start and end apart: 19 -> 19, of which waited for: 8 -> 6; matrix products, arithmetic and copies ran while one was open for 12% -> 11% of each run, Pallas kernels for 46% -> 48%
where the time goes in v4:
time: 704 us; the launch traced here: 703 us
  Pallas kernels  482 us (68%)
  waiting for transfers between devices  105 us (15%)
  matrix products  51.9 us (7%)
  other arithmetic  17.5 us (2%)
  starting transfers between devices  17 us (2%)
  local copies, waits for them, and re-layouts  15.2 us (2%)
  between operations  14.2 us (2%)
    pallas_call x3, Pallas kernels, reduce_head(): pl.pallas_call(body, in_specs=[anywhere] * (len(near_keys) + 4 * groups +...  290 us
    ppermute x16, waiting for transfers between devices, swap(): lax.ppermute(values, DATA_AXIS, [(i, i ^ mask) for i in range(DEVICES)])  105 us
    pallas_call x4, Pallas kernels, place_parts(): pl.pallas_call(body, grid=(steps,), in_specs=in_specs, out_specs=pl.Block...  48.1 us
    pallas_call x5, Pallas kernels, pack_columns(): pl.pallas_call(body, grid_spec=pltpu.PrefetchScalarGridSpec(num_scalar_pr...  47.3 us
    pallas_call x1, Pallas kernels, gather_rows(): pl.pallas_call(body, in_specs=[pl.BlockSpec(memory_space=pl.ANY)], out_sp...  36.9 us
    dot_general x1, matrix products, backward(): jnp.einsum('tv,dv->td', d_logits, w_out, preferred_element_type=jnp.float32)  34.2 us
    pallas_call x1, Pallas kernels, project_gradients(): pl.pallas_call(body, grid_spec=pltpu.PrefetchScalarGridSpec(num_scalar_pr...  23.4 us
    pallas_call x1, Pallas kernels, forward(): pl.pallas_call(body, grid=(layers, blocks), in_specs=[pl.BlockSpec((rows,...  21.1 us
  transfers between devices with their start and end apart: 19, of which 6 were waited for; matrix products, arithmetic and copies ran while one was open for 11% of the time, Pallas kernels for 48%

profile of v4, /device:TPU:0, one launch (start us, length us, event | category | flops | bytes accessed | tf_op | source)
XLA Modules:
  0.0 702.9 jit_solution(12825858180824940131)
XLA Ops:
  8.9 10.5 %pack_columns.5 = (bf16[4,512,768]{2,1,0:T(8,128)(2,1)}, bf16[4,512,640]{2,1,0:T(8,128)(2,1)}, bf16[4,512,640]{2,1,0:T(8,128)(2,1)}) custom-call(s32[3,3,4]{2,1,0:T(4,128)} %pad_add_fusion.table_ref, bf16[512,32000]{1,0:T(8,128)(2,1)} %refs_1_.7, bf16[512,32000]{1,0:T(8,128)(2,1)} %refs_1_.7, bf16[512,32000]{1,0:T(8,128)(2,1)} %refs_1_.7), custom_call_target="tpu_custom_call" | custom-call | flops 3221225472 | bytes 16777216 | tf_op jit(solution)/shard_map/pack_columns/pallas_call | solution.py:123
  20.0 10.7 %pack_columns.6 = (bf16[4,512,768]{2,1,0:T(8,128)(2,1)}, bf16[4,512,640]{2,1,0:T(8,128)(2,1)}, bf16[4,512,640]{2,1,0:T(8,128)(2,1)}) custom-call(s32[3,3,4]{2,1,0:T(4,128)} %pad_add_fusion.1.table_ref, bf16[512,32000]{1,0:T(8,128)(2,1)} %refs_1_.7, bf16[512,32000]{1,0:T(8,128)(2,1)} %refs_1_.7, bf16[512,32000]{1,0:T(8,128)(2,1)} %refs_1_.7), custom_call_target="tpu_custom_call" | custom-call | flops 3221225472 | bytes 16777216 | tf_op jit(solution)/shard_map/pack_columns/pallas_call | solution.py:123
  31.4 10.5 %pack_columns.8 = (bf16[4,512,768]{2,1,0:T(8,128)(2,1)}, bf16[4,512,640]{2,1,0:T(8,128)(2,1)}, bf16[4,512,640]{2,1,0:T(8,128)(2,1)}) custom-call(s32[3,3,4]{2,1,0:T(4,128)} %pad_add_fusion.2.table_ref, bf16[512,32000]{1,0:T(8,128)(2,1)} %refs_1_.7, bf16[512,32000]{1,0:T(8,128)(2,1)} %refs_1_.7, bf16[512,32000]{1,0:T(8,128)(2,1)} %refs_1_.7), custom_call_target="tpu_custom_call" | custom-call | flops 3221225472 | bytes 16777216 | tf_op jit(solution)/shard_map/pack_columns/pallas_call | solution.py:123
  42.5 8.7 %pack_columns.9 = (bf16[4,512,640]{2,1,0:T(8,128)(2,1)}, bf16[4,512,640]{2,1,0:T(8,128)(2,1)}) custom-call(s32[2,3,4]{2,1,0:T(4,128)} %pad_add_fusion.3.table_ref, bf16[512,32000]{1,0:T(8,128)(2,1)} %refs_1_.7, bf16[512,32000]{1,0:T(8,128)(2,1)} %refs_1_.7), custom_call_target="tpu_custom_call" | custom-call | flops 2013265920 | bytes 10485760 | tf_op jit(solution)/shard_map/pack_columns/pallas_call | solution.py:123
  51.8 6.9 pack_columns.7
  58.7 21.1 %forward_blocks.1 = (bf16[512,2048]{1,0:T(8,128)(2,1)}, bf16[512,2048]{1,0:T(8,128)(2,1)}, bf16[512,2048]{1,0:T(8,128)(2,1)}, bf16[512,2048]{1,0:T(8,128)(2,1)},...) custom-call(bf16[512,768]{1,0:T(8,128)(2,1)} %refs_1_.8, bf16[2,768,2048]{2,1,0:T(8,128)(2,1)} %w_up_ref.3, ...), custom_call_target="tpu_custom_call" | custom-call | flops 6442450944 | bytes 20000000 | tf_op jit(solution)/shard_map/forward_blocks/pallas_call | solution.py:653
  79.8 3.2 collective-permute-start.1
  86.2 14.6 %collective-permute-done.1.refs_2_ = bf16[768,512]{1,0:T(8,128)(2,1)S(1)} collective-permute-done((bf16[768,512]{1,0:T(8,128)(2,1)}, bf16[768,512]{1,0:T(8,128)(2,1)S(1)}, u32[]{:S(2)}, u32[]{:S(2)}) %collective-permute-start.1) | collective-permute-done | bytes 786464 | tf_op jit(solution)/shard_map/ppermute | solution.py:42
  106.6 34.2 %convolution_convert_fusion.refs_10_ = bf16[512,768]{1,0:T(8,128)(2,1)} fusion(bf16[512,32000]{1,0:T(8,128)(2,1)} %refs_1_.7, bf16[768,32000]{1,0:T(8,128)(2,1)} %refs_20_.1), kind=kOutput, calls=%fused_computation.38 | convolution fusion | flops 25166217216 | bytes 82706432 | tf_op jit(solution)/shard_map/tv,dv->td/dot_general | solution.py:672
  142.5 8.1 %fusion.7.refs_5_ = bf16[512,2048]{1,0:T(8,128)(2,1)} fusion(bf16[512,2048]{1,0:T(8,128)(2,1)} %get-tuple-element.80, bf16[512,768]{1,0:T(8,128)(2,1)} %convolution_convert_fusion.refs_10_, bf16[2,2048,768]{2,1,0:T(8,128)(2,1)} %w_down_ref.3), kind=kOutput, calls=%fused_computation.17 | convolution fusion | flops 1632632832 | bytes 8126464 | tf_op jit(solution)/shard_map/td,fd->tf/dot_general | solution.py:678
  152.3 9.1 %collective-permute-done.12.refs_16_.refs_15_ = bf16[4,512,640]{2,1,0:T(8,128)(2,1)} collective-permute-done((bf16[4,512,640]{2,1,0:T(8,128)(2,1)}, bf16[4,512,640]{2,1,0:T(8,128)(2,1)}, u32[]{:S(2)}, u32[]{:S(2)}) %collective-permute-start.12) | collective-permute-done | bytes 2621472 | tf_op jit(solution)/shard_map/ppermute | solution.py:42
  164.2 1.9 copy.47
  167.1 1.9 copy.49
  169.0 1.9 copy.50
  174.6 4.5 add_convert_fusion.refs_7_
  179.2 5.1 fusion.4.refs_2_
  184.3 23.4 %project_gradients.1.refs_8_ = f32[4,16,256,128]{3,2,1,0:T(8,128)} custom-call(s32[4,16]{1,0:T(4,128)} %pad_add_fusion.4.table_ref, bf16[256,768]{1,0:T(8,128)(2,1)} %bitcast.173, bf16[512,768]{1,0:T(8,128)(2,1)} %refs_1_.8, bf16[512,2048]{1,0:T(8,128)(2,1)} %fusion.4.refs_2_, bf16[256,768]{1,0:T(8,128)(2,1)} %bitcast.174, ...), custom_call_target="tpu_custom_call" | custom-call | flops 12884901888 | bytes 16777216 | tf_op jit(solution)/shard_map/project_gradients/pallas_call | solution.py:179
  207.7 23.0 %collective-permute-done.11.refs_15_.refs_14_ = bf16[4,512,640]{2,1,0:T(8,128)(2,1)} collective-permute-done((bf16[4,512,640]{2,1,0:T(8,128)(2,1)}, bf16[4,512,640]{2,1,0:T(8,128)(2,1)}, u32[]{:S(2)}, u32[]{:S(2)}) %collective-permute-start.11) | collective-permute-done | bytes 2621472 | tf_op jit(solution)/shard_map/ppermute | solution.py:42
  231.9 56.9 %collective-permute-done.8.refs_11_.refs_10_ = bf16[4,512,768]{2,1,0:T(8,128)(2,1)} collective-permute-done((bf16[4,512,768]{2,1,0:T(8,128)(2,1)S(1)}, bf16[4,512,768]{2,1,0:T(8,128)(2,1)}, u32[]{:S(2)}, u32[]{:S(2)}) %collective-permute-start.8) | collective-permute-done | bytes 3145760 | tf_op jit(solution)/shard_map/ppermute | solution.py:42
  288.8 64.1 %reduce_head.3 = (bf16[256,2048]{1,0:T(8,128)(2,1)}, f32[2000,256]{1,0:T(8,128)}, f32[2000,256]{1,0:T(8,128)}, f32[4,8,256,128]{3,2,1,0:T(8,128)}) custom-call(bf16[768,512]{1,0:T(8,128)(2,1)} %get-tuple-element.108.refs_0_, bf16[768,512]{1,0:T(8,128)(2,1)} %copy-done.16, bf16[768,512]{1,0:T(8,128)(2,1)} %copy-done.14, bf16[768,512]{1,0:T(8,128)(2,1)} %copy-done.17, ...), custom_call_target="tpu_custom_call" | custom-call | flops 60000002048 | bytes 100000000 | tf_op jit(solution)/shard_map/reduce_head/pallas_call | solution.py:427
  353.3 133.6 %reduce_head.4 = (bf16[256,2048]{1,0:T(8,128)(2,1)}, f32[2000,256]{1,0:T(8,128)}, f32[2000,256]{1,0:T(8,128)}, f32[4,1,256,128]{3,2,1,0:T(8,128)}) custom-call(bf16[768,512]{1,0:T(8,128)(2,1)} %get-tuple-element.108.refs_0_, bf16[768,512]{1,0:T(8,128)(2,1)} %copy-done.16, bf16[768,512]{1,0:T(8,128)(2,1)} %copy-done.14, bf16[768,512]{1,0:T(8,128)(2,1)} %copy-done.17, ...), custom_call_target="tpu_custom_call" | custom-call | flops 60000002048 | bytes 100000000 | tf_op jit(solution)/shard_map/reduce_head/pallas_call | solution.py:427
  488.3 1.9 divide_convert_fusion.1
  491.5 92.6 %reduce_head.5 = (bf16[256,2048]{1,0:T(8,128)(2,1)}, f32[2000,256]{1,0:T(8,128)}, f32[2000,256]{1,0:T(8,128)}) custom-call(bf16[768,512]{1,0:T(8,128)(2,1)} %get-tuple-element.108.refs_0_, bf16[768,512]{1,0:T(8,128)(2,1)} %copy-done.16, bf16[768,512]{1,0:T(8,128)(2,1)} %copy-done.14, bf16[768,512]{1,0:T(8,128)(2,1)} %copy-done.17, ...), custom_call_target="tpu_custom_call" | custom-call | flops 60000002048 | bytes 100000000 | tf_op jit(solution)/shard_map/reduce_head/pallas_call | solution.py:427
  584.1 2.1 slice.47
  587.9 5.6 maximum_bitcast_fusion.1
  593.5 3.1 maximum_bitcast_fusion
  596.5 36.9 %gather_rows.1.refs_0_ = bf16[16,96,2048]{2,1,0:T(8,128)(2,1)} custom-call(bf16[256,2048]{1,0:T(8,128)(2,1)} %get-tuple-element.116.values_ref), custom_call_target="tpu_custom_call" | custom-call | flops 10000000000 | bytes 10000000 | tf_op jit(solution)/shard_map/gather_rows/pallas_call | solution.py:496
  633.4 15.1 %place_parts.4.refs_1_ = bf16[768,32000]{1,0:T(8,128)(2,1)} custom-call(bf16[16,256,2048]{2,1,0:T(8,128)(2,1)} %bitcast.166), custom_call_target="tpu_custom_call" | custom-call | flops 131072000 | bytes 32768000 | tf_op jit(solution)/shard_map/place_parts/pallas_call | solution.py:549
  648.5 15.2 %place_parts.5.refs_1_ = bf16[768,32000]{1,0:T(8,128)(2,1)} custom-call(bf16[16,320,2048]{2,1,0:T(8,128)(2,1)} %bitcast.164, bf16[768,32000]{1,0:T(8,128)(2,1)} %place_parts.4.refs_1_), custom_call_target="tpu_custom_call", output_to_operand_aliasing={{}: (1, {})} | custom-call | flops 131072000 | bytes 32768000 | tf_op jit(solution)/shard_map/place_parts/pallas_call | solution.py:549
  663.7 7.1 %place_parts.6.refs_1_ = bf16[768,32000]{1,0:T(8,128)(2,1)} custom-call(bf16[16,96,2048]{2,1,0:T(8,128)(2,1)} %gather_rows.1.refs_0_, bf16[768,32000]{1,0:T(8,128)(2,1)} %place_parts.5.refs_1_), custom_call_target="tpu_custom_call", output_to_operand_aliasing={{}: (1, {})} | custom-call | flops 49152000 | bytes 12288000 | tf_op jit(solution)/shard_map/place_parts/pallas_call | solution.py:549
  670.8 14.8 %back_project.1 = (bf16[2,768,2048]{2,1,0:T(8,128)(2,1)}, bf16[2,2048,768]{2,1,0:T(8,128)(2,1)}) custom-call(bf16[16,320,2048]{2,1,0:T(8,128)(2,1)} %bitcast.165, bf16[2,768,2048]{2,1,0:T(8,128)(2,1)} %w_up_ref.3, bf16[2,2048,768]{2,1,0:T(8,128)(2,1)} %w_down_ref.3, bf16[2,768,256]{2,1,0:T(8,128)(2,1)} %p_ref.1, bf16[2,768,256]{2,1,0:T(8,128)(2,1)} %q_ref.1), custom_call_target="tpu_custom_call" | custom-call | flops 3221225472 | bytes 30000000 | tf_op jit(solution)/shard_map/back_project/pallas_call | solution.py:588
  685.6 10.7 %place_parts.7 = bf16[768,32000]{1,0:T(8,128)(2,1)} custom-call(bf16[16,160,2048]{2,1,0:T(8,128)(2,1)} %bitcast.167, bf16[768,32000]{1,0:T(8,128)(2,1)} %place_parts.6.refs_1_), custom_call_target="tpu_custom_call", output_to_operand_aliasing={{}: (1, {})} | custom-call | flops 81920000 | bytes 20480000 | tf_op jit(solution)/shard_map/place_parts/pallas_call | solution.py:549
  (137 shorter events, 29.5 us)
Async XLA Ops:
  7.2 626.3 %all-gather.11.cloned.1.call-start = ((), (), s32[]{:S(2)}) async-start(), calls=%async_computation.2 | async-start | bytes 17825792 | tf_op jit(solution)/shard_map/all_gather | solution.py:744
  20.0 10.7 %copy-start.12 = (s32[4]{0:T(128)S(1)}, s32[4]{0:T(128)}, u32[]{:S(2)}) copy-start(s32[4]{0:T(128)} %constant.259) | copy-start | bytes 52
  20.0 10.7 %copy-start.13 = (s32[4]{0:T(128)S(1)}, s32[4]{0:T(128)}, u32[]{:S(2)}) copy-start(s32[4]{0:T(128)} %constant.260) | copy-start | bytes 52
  79.8 61.0 %copy-start.1 = (bf16[2,768,256]{2,1,0:T(8,128)(2,1)S(1)}, bf16[2,768,256]{2,1,0:T(8,128)(2,1)}, u32[]{:S(2)}) copy-start(bf16[2,768,256]{2,1,0:T(8,128)(2,1)} %p_ref.1) | copy-start | bytes 2359300
  79.8 21.0 %collective-permute-start.1 = (bf16[768,512]{1,0:T(8,128)(2,1)}, bf16[768,512]{1,0:T(8,128)(2,1)S(1)}, u32[]{:S(2)}, u32[]{:S(2)}) collective-permute-start(bf16[768,512]{1,0:T(8,128)(2,1)} %get-tuple-element.108.refs_0_), channel_id=1, source_target_pairs={{0,2},{1,3},{2,0},{3,1},{4,6},{5,7},{6,4},{7,5},{8,10},{9,11},{10,... | collective-permute-start | bytes 2359304 | tf_op jit(solution)/shard_map/ppermute | solution.py:42
  83.1 19.2 %collective-permute-start.3 = (bf16[768,512]{1,0:T(8,128)(2,1)}, bf16[768,512]{1,0:T(8,128)(2,1)S(1)}, u32[]{:S(2)}, u32[]{:S(2)}) collective-permute-start(bf16[768,512]{1,0:T(8,128)(2,1)} %get-tuple-element.108.refs_0_), channel_id=1, source_target_pairs={{0,4},{1,5},{2,6},{3,7},{4,0},{5,1},{6,2},{7,3},{8,12},{9,13},{10,... | collective-permute-start | bytes 2359304 | tf_op jit(solution)/shard_map/ppermute | solution.py:42
  84.6 19.1 %collective-permute-start.5 = (bf16[768,512]{1,0:T(8,128)(2,1)}, bf16[768,512]{1,0:T(8,128)(2,1)}, u32[]{:S(2)}, u32[]{:S(2)}) collective-permute-start(bf16[768,512]{1,0:T(8,128)(2,1)} %get-tuple-element.108.refs_0_), channel_id=1, source_target_pairs={{0,8},{1,9},{2,10},{3,11},{4,12},{5,13},{6,14},{7,15},{8,0},{9,1},... | collective-permute-start | bytes 2359304 | tf_op jit(solution)/shard_map/ppermute | solution.py:42
  86.2 18.0 %collective-permute-start = (bf16[768,512]{1,0:T(8,128)(2,1)}, bf16[768,512]{1,0:T(8,128)(2,1)S(1)}, u32[]{:S(2)}, u32[]{:S(2)}) collective-permute-start(bf16[768,512]{1,0:T(8,128)(2,1)} %get-tuple-element.108.refs_0_), channel_id=1, source_target_pairs={{0,1},{1,0},{2,3},{3,2},{4,5},{5,4},{6,7},{7,6},{8,9},{9,8},{10,11... | collective-permute-start | bytes 2359304 | tf_op jit(solution)/shard_map/ppermute | solution.py:42
  101.7 3.6 collective-permute-start.2
  101.7 49.0 %collective-permute-start.10 = (bf16[4,512,640]{2,1,0:T(8,128)(2,1)}, bf16[4,512,640]{2,1,0:T(8,128)(2,1)}, u32[]{:S(2)}, u32[]{:S(2)}) collective-permute-start(bf16[4,512,640]{2,1,0:T(8,128)(2,1)} %get-tuple-element.71), channel_id=1, source_target_pairs={{0,1},{1,0},{2,3},{3,2},{4,5},{5,4},{6,7},{7,6},{8,9},{9,8},{10,11... | collective-permute-start | bytes 7864328 | tf_op jit(solution)/shard_map/ppermute | solution.py:42
  102.3 38.5 %copy-start.15 = (bf16[768,512]{1,0:T(8,128)(2,1)}, bf16[768,512]{1,0:T(8,128)(2,1)S(1)}, u32[]{:S(2)}) copy-start(bf16[768,512]{1,0:T(8,128)(2,1)S(1)} %collective-permute-done.3.refs_4_) | copy-start | bytes 2359300
  102.3 59.2 %collective-permute-start.12 = (bf16[4,512,640]{2,1,0:T(8,128)(2,1)}, bf16[4,512,640]{2,1,0:T(8,128)(2,1)}, u32[]{:S(2)}, u32[]{:S(2)}) collective-permute-start(bf16[4,512,640]{2,1,0:T(8,128)(2,1)} %get-tuple-element.73), channel_id=1, source_target_pairs={{0,5},{1,4},{2,7},{3,6},{4,1},{5,0},{6,3},{7,2},{8,13},{9,12},{10,... | collective-permute-start | bytes 7864328 | tf_op jit(solution)/shard_map/ppermute | solution.py:42
  103.6 67.9 %collective-permute-start.13 = (bf16[4,512,640]{2,1,0:T(8,128)(2,1)}, bf16[4,512,640]{2,1,0:T(8,128)(2,1)}, u32[]{:S(2)}, u32[]{:S(2)}) collective-permute-start(bf16[4,512,640]{2,1,0:T(8,128)(2,1)} %get-tuple-element.75), channel_id=1, source_target_pairs={{0,1},{1,0},{2,3},{3,2},{4,5},{5,4},{6,7},{7,6},{8,9},{9,8},{10,11... | collective-permute-start | bytes 7864328 | tf_op jit(solution)/shard_map/ppermute | solution.py:42
  104.1 69.0 %collective-permute-start.15 = (bf16[4,512,640]{2,1,0:T(8,128)(2,1)}, bf16[4,512,640]{2,1,0:T(8,128)(2,1)}, u32[]{:S(2)}, u32[]{:S(2)}) collective-permute-start(bf16[4,512,640]{2,1,0:T(8,128)(2,1)} %get-tuple-element.77), channel_id=1, source_target_pairs={{0,3},{1,2},{2,1},{3,0},{4,7},{5,6},{6,5},{7,4},{8,11},{9,10},{10,... | collective-permute-start | bytes 7864328 | tf_op jit(solution)/shard_map/ppermute | solution.py:42
  106.1 35.5 %collective-permute-start.4 = (bf16[768,512]{1,0:T(8,128)(2,1)S(1)}, bf16[768,512]{1,0:T(8,128)(2,1)S(1)}, u32[]{:S(2)}, u32[]{:S(2)}) collective-permute-start(bf16[768,512]{1,0:T(8,128)(2,1)S(1)} %collective-permute-done.3.refs_4_), channel_id=1, source_target_pairs={{0,1},{1,0},{2,3},{3,2},{4,5},{5,4},{6,7},{7,6},{8,9},{9,8},{10,11... | collective-permute-start | bytes 2359304 | tf_op jit(solution)/shard_map/ppermute | solution.py:42
  141.6 9.0 %collective-permute-start.6 = (bf16[768,512]{1,0:T(8,128)(2,1)}, bf16[768,512]{1,0:T(8,128)(2,1)S(1)}, u32[]{:S(2)}, u32[]{:S(2)}) collective-permute-start(bf16[768,512]{1,0:T(8,128)(2,1)} %collective-permute-done.5.refs_6_), channel_id=1, source_target_pairs={{0,1},{1,0},{2,3},{3,2},{4,5},{5,4},{6,7},{7,6},{8,9},{9,8},{10,11... | collective-permute-start | bytes 2359304 | tf_op jit(solution)/shard_map/ppermute | solution.py:42
  142.5 19.0 %copy-start = (bf16[4,512,768]{2,1,0:T(8,128)(2,1)S(1)}, bf16[4,512,768]{2,1,0:T(8,128)(2,1)}, u32[]{:S(2)}) copy-start(bf16[4,512,768]{2,1,0:T(8,128)(2,1)} %pack_columns.7) | copy-start | bytes 9437188
  142.5 20.8 %copy-start.2 = (bf16[2,768,256]{2,1,0:T(8,128)(2,1)S(1)}, bf16[2,768,256]{2,1,0:T(8,128)(2,1)}, u32[]{:S(2)}) copy-start(bf16[2,768,256]{2,1,0:T(8,128)(2,1)} %q_ref.1) | copy-start | bytes 2359300
  150.6 13.6 %copy-start.19 = (bf16[768,512]{1,0:T(8,128)(2,1)}, bf16[768,512]{1,0:T(8,128)(2,1)S(1)}, u32[]{:S(2)}) copy-start(bf16[768,512]{1,0:T(8,128)(2,1)S(1)} %collective-permute-done.6.refs_7_) | copy-start | bytes 2359300
  150.6 81.3 %collective-permute-start.7 = (bf16[4,512,768]{2,1,0:T(8,128)(2,1)}, bf16[4,512,768]{2,1,0:T(8,128)(2,1)}, u32[]{:S(2)}, u32[]{:S(2)}) collective-permute-start(bf16[4,512,768]{2,1,0:T(8,128)(2,1)} %get-tuple-element.68), channel_id=1, source_target_pairs={{0,1},{1,0},{2,3},{3,2},{4,5},{5,4},{6,7},{7,6},{8,9},{9,8},{10,11... | collective-permute-start | bytes 9437192 | tf_op jit(solution)/shard_map/ppermute | solution.py:42
  150.7 81.3 %collective-permute-start.9 = (bf16[4,512,768]{2,1,0:T(8,128)(2,1)}, bf16[4,512,768]{2,1,0:T(8,128)(2,1)}, u32[]{:S(2)}, u32[]{:S(2)}) collective-permute-start(bf16[4,512,768]{2,1,0:T(8,128)(2,1)} %get-tuple-element.69), channel_id=1, source_target_pairs={{0,9},{1,8},{2,11},{3,10},{4,13},{5,12},{6,15},{7,14},{8,1},{9,0},... | collective-permute-start | bytes 9437192 | tf_op jit(solution)/shard_map/ppermute | solution.py:42
  161.5 127.3 %collective-permute-start.8 = (bf16[4,512,768]{2,1,0:T(8,128)(2,1)S(1)}, bf16[4,512,768]{2,1,0:T(8,128)(2,1)}, u32[]{:S(2)}, u32[]{:S(2)}) collective-permute-start(bf16[4,512,768]{2,1,0:T(8,128)(2,1)S(1)} %copy-done), channel_id=1, source_target_pairs={{0,8},{1,9},{2,10},{3,11},{4,12},{5,13},{6,14},{7,15},{8,0},{9,1},... | collective-permute-start | bytes 9437192 | tf_op jit(solution)/shard_map/ppermute | solution.py:42
  170.9 8.2 %slice-start = ((s8[6291456]{0:T(1024)(128)(4,1)}), s8[4194304]{0:T(1024)(128)(4,1)S(1)}, s32[]{:S(2)}) async-start(s8[6291456]{0:T(1024)(128)(4,1)} %bitcast.168), calls=%async_computation.3 | async-start | bytes 8388608
  171.5 7.6 %copy-start.21 = (bf16[512,2048]{1,0:T(8,128)(2,1)S(1)}, bf16[512,2048]{1,0:T(8,128)(2,1)}, u32[]{:S(2)}) copy-start(bf16[512,2048]{1,0:T(8,128)(2,1)} %get-tuple-element.81) | copy-start | bytes 6291460
  171.5 59.1 %collective-permute-start.11 = (bf16[4,512,640]{2,1,0:T(8,128)(2,1)}, bf16[4,512,640]{2,1,0:T(8,128)(2,1)}, u32[]{:S(2)}, u32[]{:S(2)}) collective-permute-start(bf16[4,512,640]{2,1,0:T(8,128)(2,1)} %get-tuple-element.72), channel_id=1, source_target_pairs={{0,4},{1,5},{2,6},{3,7},{4,0},{5,1},{6,2},{7,3},{8,12},{9,13},{10,... | collective-permute-start | bytes 7864328 | tf_op jit(solution)/shard_map/ppermute | solution.py:42
  173.1 58.9 %collective-permute-start.14 = (bf16[4,512,640]{2,1,0:T(8,128)(2,1)}, bf16[4,512,640]{2,1,0:T(8,128)(2,1)}, u32[]{:S(2)}, u32[]{:S(2)}) collective-permute-start(bf16[4,512,640]{2,1,0:T(8,128)(2,1)} %get-tuple-element.76), channel_id=1, source_target_pairs={{0,2},{1,3},{2,0},{3,1},{4,6},{5,7},{6,4},{7,5},{8,10},{9,11},{10,... | collective-permute-start | bytes 7864328 | tf_op jit(solution)/shard_map/ppermute | solution.py:42
  288.8 64.2 %copy-start.8 = (f32[2,128,256]{2,1,0:T(8,128)S(1)}, f32[2,128,256]{2,1,0:T(8,128)}, u32[]{:S(2)}) copy-start(f32[2,128,256]{2,1,0:T(8,128)} %param.34) | copy-start | bytes 786436
  288.8 64.4 %copy-start.9 = (f32[2,128,256]{2,1,0:T(8,128)S(1)}, f32[2,128,256]{2,1,0:T(8,128)}, u32[]{:S(2)}) copy-start(f32[2,128,256]{2,1,0:T(8,128)} %param.35) | copy-start | bytes 786436
  353.0 295.5 %all-gather.7.cloned.1.call-start = ((), (), s32[]{:S(2)}) async-start(), calls=%async_computation | async-start | bytes 22282240 | tf_op jit(solution)/shard_map/all_gather | solution.py:744
  353.3 134.9 %copy-start.10 = (f32[2,256,128]{2,1,0:T(8,128)S(1)}, f32[2,256,128]{2,1,0:T(8,128)}, u32[]{:S(2)}) copy-start(f32[2,256,128]{2,1,0:T(8,128)} %param.32) | copy-start | bytes 786436
  353.3 134.9 %copy-start.11 = (f32[2,256,128]{2,1,0:T(8,128)S(1)}, f32[2,256,128]{2,1,0:T(8,128)}, u32[]{:S(2)}) copy-start(f32[2,256,128]{2,1,0:T(8,128)} %param.33) | copy-start | bytes 786436
  491.4 194.2 %all-gather.9.cloned.1.call-start = ((), (), s32[]{:S(2)}) async-start(), calls=%async_computation.1 | async-start | bytes 11141120 | tf_op jit(solution)/shard_map/all_gather | solution.py:744
  (11 other events, 40.4 us)
Sparse Core Ops, SparseCore 0:
  353.1 128.8 all-gather.10
  491.5 130.9 all-gather.6
  624.8 56.0 all-gather.8
